TPU v7x, 32 devices: a whole 2x2x4 slice. The times are simulated.
32 devices in a mesh: seq: 4 (over x, core), dp: 8 (over z, y).
Axes of the slice: x: 2, y: 2, z: 4, core: 2. Of those that a mesh axis runs over, the one named last changes fastest.
Arguments:
- inputs: bfloat16 [32, 1024, 768], P('dp', 'seq'), may hold values from -6 to 6
- cotangent: bfloat16 [32, 1024, 768], P('dp', 'seq'), may hold values from -6 to 6
- segments: int32 [32, 1024], P('dp'), may hold values from 0 to 5, as said below
- padding: int32 [32, 1024], P('dp'), may hold values from 0 to 1, as said below
- random_blocks: int32 [12, 16, 3], replicated, may hold values from 0 to 15
- w_query: bfloat16 [768, 768], P('dp', 'seq'), may hold values from -0.21875 to 0.21875
- b_query: bfloat16 [768], P('dp'), may hold values from -1.5 to 1.5
- w_key: bfloat16 [768, 768], P('dp', 'seq'), may hold values from -0.21875 to 0.21875
- w_value: bfloat16 [768, 768], P('dp', 'seq'), may hold values from -0.21875 to 0.21875
- b_value: bfloat16 [768], P('dp'), may hold values from -1.5 to 1.5
- w_out: bfloat16 [768, 768], P('dp', 'seq'), may hold values from -0.875 to 0.875
- b_out: bfloat16 [768], P('dp'), may hold values from -1.5 to 1.5
- gain_one: bfloat16 [768], P('dp'), may hold values from 0.5 to 1.5
- shift_one: bfloat16 [768], P('dp'), may hold values from -1.5 to 1.5
- w_up: bfloat16 [768, 3072], P('dp', 'seq'), may hold values from -0.21875 to 0.21875
- b_up: bfloat16 [3072], P('dp'), may hold values from -1.5 to 1.5
- w_down: bfloat16 [3072, 768], P('dp', 'seq'), may hold values from -0.109375 to 0.109375
- b_down: bfloat16 [768], P('dp'), may hold values from -1.5 to 1.5
- gain_two: bfloat16 [768], P('dp'), may hold values from 0.5 to 1.5
- shift_two: bfloat16 [768], P('dp'), may hold values from -1.5 to 1.5
Outputs:
- output: bfloat16 [32, 1024, 768], P('dp', 'seq')
- grad_inputs: float32 [32, 1024, 768], P('dp', 'seq')
- grad_w_query: float32 [768, 768], P('dp', 'seq')
- grad_b_query: float32 [768], P('dp')
- grad_w_key: float32 [768, 768], P('dp', 'seq')
- grad_w_value: float32 [768, 768], P('dp', 'seq')
- grad_b_value: float32 [768], P('dp')
- grad_w_out: float32 [768, 768], P('dp', 'seq')
- grad_b_out: float32 [768], P('dp')
- grad_gain_one: float32 [768], P('dp')
- grad_shift_one: float32 [768], P('dp')
- grad_w_up: float32 [768, 3072], P('dp', 'seq')
- grad_b_up: float32 [3072], P('dp')
- grad_w_down: float32 [3072, 768], P('dp', 'seq')
- grad_b_down: float32 [768], P('dp')
- grad_gain_two: float32 [768], P('dp')
- grad_shift_two: float32 [768], P('dp')
Inputs may be any that keep to these rules, and one draw needn't show every extreme that they name: `segments`: in each sequence the numbers start at 0 and never fall; every number but the last names one whole document of 1024 // 5 to 1024 * 125 // 128 positions, and the positions after the last document carry the next number; the first sequence holds five documents of the shortest length. `padding`: 1 exactly on the positions of whole documents, which fill a leading run of each sequence.
All inputs are finite; a program needn't handle non-finite values.
Results may differ from a plain program's by a relative error of at most 0.014.
Values may be sent and summed in bfloat16 or wider, within the bound.
A program may use at most 192 MiB of HBM per device.

v0:
```python
from functools import partial

import jax
import jax.numpy as jnp
from jax import lax
from jax.sharding import PartitionSpec as P

H = 12
HD = 64
BLK = 64
NGLOB = 2
LEN = 1024
QB = 512


def layer_norm(hidden, gain, shift):
    mean_value = jnp.mean(hidden, axis=-1, keepdims=True)
    centered = hidden - mean_value
    spread = jnp.mean(centered * centered, axis=-1, keepdims=True)
    return centered * lax.rsqrt(spread + 1e-06) * gain + shift


def segment_inside(segment_row):
    places = jnp.arange(segment_row.shape[0], dtype=jnp.int32)
    begins = jnp.concatenate([jnp.ones((1,), dtype=jnp.bool_), segment_row[1:] != segment_row[:-1]])
    firsts = lax.cummax(jnp.where(begins, places, 0), axis=0)
    return places - firsts


def allowed_mask(segment_row, pad_row, inside_row, random_heads, row_start, row_count):
    key_places = jnp.arange(LEN, dtype=jnp.int32)
    query_places = row_start + jnp.arange(row_count, dtype=jnp.int32)
    query_segment = lax.dynamic_slice_in_dim(segment_row, row_start, row_count)
    query_inside = lax.dynamic_slice_in_dim(inside_row, row_start, row_count)
    query_block = query_places // BLK
    key_block = key_places // BLK
    same = (query_segment[:, None] == segment_row[None, :]) & (pad_row[None, :] == 1)
    plain = (
        (jnp.abs(query_block[:, None] - key_block[None, :]) <= 1)
        | (query_inside[:, None] < NGLOB * BLK)
        | (inside_row[None, :] < NGLOB * BLK)
    )
    chosen = lax.dynamic_slice_in_dim(random_heads, row_start // BLK, row_count // BLK, 1)
    picked = jnp.any(
        chosen[:, :, :, None] == jnp.arange(LEN // BLK, dtype=jnp.int32)[None, None, None, :],
        axis=2,
    )
    picked = jnp.repeat(jnp.repeat(picked, BLK, axis=1), BLK, axis=2)
    diagonal = query_places[:, None] == key_places[None, :]
    return (same & plain)[None] | same[None] & picked | diagonal[None]


def inner_rows(left, right):
    return lax.dot_general(
        left, right, (((0,), (0,)), ((), ())), preferred_element_type=jnp.float32
    )


def times_back(left, matrix):
    return lax.dot_general(
        left, matrix, (((1,), (1,)), ((), ())), preferred_element_type=jnp.float32
    )


def shards(
    inputs,
    cotangent,
    segments,
    padding,
    random_blocks,
    w_query,
    b_query,
    w_key,
    w_value,
    b_value,
    w_out,
    b_out,
    gain_one,
    shift_one,
    w_up,
    b_up,
    w_down,
    b_down,
    gain_two,
    shift_two,
):
    n_seq = lax.axis_size("seq")
    seqs_here, shard_len, width = inputs.shape
    rows = seqs_here * shard_len
    heads_here = H // n_seq
    piece = width // n_seq
    seq_len = shard_len * n_seq
    n_blocks = seq_len // QB
    scale = HD ** (-0.5)
    columns = (
        lax.all_gather(w_query, "seq", axis=1, tiled=True),
        lax.all_gather(w_key, "seq", axis=1, tiled=True),
        lax.all_gather(w_value, "seq", axis=1, tiled=True),
        lax.all_gather(w_out, "seq", axis=1, tiled=True),
        lax.all_gather(w_up, "seq", axis=1, tiled=True),
        lax.all_gather(w_down, "seq", axis=1, tiled=True),
    )
    whole = (
        lax.all_gather(columns[0], "dp", axis=0, tiled=True),
        lax.all_gather(columns[1], "dp", axis=0, tiled=True),
        lax.all_gather(columns[2], "dp", axis=0, tiled=True),
        lax.all_gather(columns[3], "dp", axis=0, tiled=True),
        lax.all_gather(columns[4], "dp", axis=0, tiled=True),
        lax.all_gather(columns[5], "dp", axis=0, tiled=True),
        lax.all_gather(b_query, "dp", axis=0, tiled=True),
        lax.all_gather(b_value, "dp", axis=0, tiled=True),
        lax.all_gather(b_out, "dp", axis=0, tiled=True),
        lax.all_gather(gain_one, "dp", axis=0, tiled=True),
        lax.all_gather(shift_one, "dp", axis=0, tiled=True),
        lax.all_gather(b_up, "dp", axis=0, tiled=True),
        lax.all_gather(b_down, "dp", axis=0, tiled=True),
        lax.all_gather(gain_two, "dp", axis=0, tiled=True),
        lax.all_gather(shift_two, "dp", axis=0, tiled=True),
    )
    full_query, full_key, full_value, full_out, full_up, full_down = whole[:6]
    (
        vec_query,
        vec_value,
        vec_out,
        vec_gain_one,
        vec_shift_one,
        vec_up,
        vec_down,
        vec_gain_two,
        vec_shift_two,
    ) = [item.astype(jnp.float32) for item in whole[6:]]
    flat = inputs.reshape(rows, width)
    queries = (jnp.dot(flat, full_query, preferred_element_type=jnp.float32) + vec_query).astype(
        jnp.bfloat16
    )
    keys = jnp.dot(flat, full_key, preferred_element_type=jnp.float32).astype(jnp.bfloat16)
    values = (jnp.dot(flat, full_value, preferred_element_type=jnp.float32) + vec_value).astype(
        jnp.bfloat16
    )

    def token_split(array):
        return array.reshape(seqs_here, shard_len, n_seq, piece)

    def head_form(array):
        return array.reshape(seqs_here, seq_len, heads_here, HD)

    head_q, head_k, head_v = (
        lax.all_to_all(token_split(queries), "seq", split_axis=2, concat_axis=1, tiled=True),
        lax.all_to_all(token_split(keys), "seq", split_axis=2, concat_axis=1, tiled=True),
        lax.all_to_all(token_split(values), "seq", split_axis=2, concat_axis=1, tiled=True),
    )
    head_q, head_k, head_v = (head_form(head_q), head_form(head_k), head_form(head_v))
    insides = jax.vmap(segment_inside)(segments)
    own_random = lax.dynamic_slice_in_dim(
        random_blocks, lax.axis_index("seq") * heads_here, heads_here, 0
    )

    def attend_sequence(items):
        queries_s, keys_s, values_s, segment_row, pad_row, inside_row = items

        def one_block(block_index):
            row_start = block_index * QB
            mask = allowed_mask(segment_row, pad_row, inside_row, own_random, row_start, QB)
            query_rows = lax.dynamic_slice_in_dim(queries_s, row_start, QB, 0)
            scores = (
                jnp.einsum("qhd,khd->hqk", query_rows, keys_s, preferred_element_type=jnp.float32)
                * scale
            )
            scores = jnp.where(mask, scores, -1e30)
            top = jnp.max(scores, axis=2, keepdims=True)
            weights = jnp.exp(scores - top)
            total = jnp.sum(weights, axis=2, keepdims=True)
            probs = (weights / total).astype(jnp.bfloat16)
            context = jnp.einsum(
                "hqk,khd->qhd", probs, values_s, preferred_element_type=jnp.float32
            ).astype(jnp.bfloat16)
            return (context, (top + jnp.log(total))[:, :, 0])

        contexts, sums = lax.map(one_block, jnp.arange(n_blocks, dtype=jnp.int32))
        return (contexts.reshape(seq_len, heads_here, HD), sums)

    contexts, lse_all = lax.map(
        attend_sequence, (head_q, head_k, head_v, segments, padding, insides)
    )
    context_tok = lax.all_to_all(
        contexts.reshape(seqs_here, seq_len, 1, heads_here * HD),
        "seq",
        split_axis=1,
        concat_axis=2,
        tiled=True,
    )
    context_tok = context_tok.reshape(rows, width)
    hidden = (
        flat.astype(jnp.float32)
        + jnp.dot(context_tok, full_out, preferred_element_type=jnp.float32)
        + vec_out
    )
    normed = layer_norm(hidden, vec_gain_one, vec_shift_one)
    normed_low = normed.astype(jnp.bfloat16)
    upper = jnp.dot(normed_low, full_up, preferred_element_type=jnp.float32) + vec_up
    gelu_value, gelu_back = jax.vjp(partial(jax.nn.gelu, approximate=False), upper)
    active = gelu_value.astype(jnp.bfloat16)
    mixed = normed + jnp.dot(active, full_down, preferred_element_type=jnp.float32) + vec_down
    output = layer_norm(mixed, vec_gain_two, vec_shift_two).astype(jnp.bfloat16)
    columns_back = (
        lax.all_gather(w_query, "seq", axis=1, tiled=True),
        lax.all_gather(w_key, "seq", axis=1, tiled=True),
        lax.all_gather(w_value, "seq", axis=1, tiled=True),
        lax.all_gather(w_out, "seq", axis=1, tiled=True),
        lax.all_gather(w_up, "seq", axis=1, tiled=True),
        lax.all_gather(w_down, "seq", axis=1, tiled=True),
    )
    back_query, back_key, back_value, back_out, back_up, back_down = (
        lax.all_gather(columns_back[0], "dp", axis=0, tiled=True),
        lax.all_gather(columns_back[1], "dp", axis=0, tiled=True),
        lax.all_gather(columns_back[2], "dp", axis=0, tiled=True),
        lax.all_gather(columns_back[3], "dp", axis=0, tiled=True),
        lax.all_gather(columns_back[4], "dp", axis=0, tiled=True),
        lax.all_gather(columns_back[5], "dp", axis=0, tiled=True),
    )
    grad_out = cotangent.reshape(rows, width).astype(jnp.float32)
    norm_two_back = jax.vjp(layer_norm, mixed, vec_gain_two, vec_shift_two)[1]
    grad_mixed, grad_gain_two, grad_shift_two = norm_two_back(grad_out)
    grad_lower = grad_mixed.astype(jnp.bfloat16)
    grad_b_down = jnp.sum(grad_lower.astype(jnp.float32), axis=0)
    grad_w_down = inner_rows(active, grad_lower)
    grad_upper = gelu_back(times_back(grad_lower, back_down))[0].astype(jnp.bfloat16)
    grad_b_up = jnp.sum(grad_upper.astype(jnp.float32), axis=0)
    grad_w_up = inner_rows(normed_low, grad_upper)
    grad_normed = grad_mixed + times_back(grad_upper, back_up)
    norm_one_back = jax.vjp(layer_norm, hidden, vec_gain_one, vec_shift_one)[1]
    grad_hidden, grad_gain_one, grad_shift_one = norm_one_back(grad_normed)
    grad_branch = grad_hidden.astype(jnp.bfloat16)
    grad_b_out = jnp.sum(grad_branch.astype(jnp.float32), axis=0)
    grad_w_out = inner_rows(context_tok, grad_branch)
    grad_context = times_back(grad_branch, back_out).astype(jnp.bfloat16)
    grad_heads = lax.all_to_all(
        token_split(grad_context), "seq", split_axis=2, concat_axis=1, tiled=True
    )
    grad_heads = head_form(grad_heads)

    def attend_back(items):
        queries_s, keys_s, values_s, grads_s, sums_s, segment_row, pad_row, inside_row = items

        def one_block(carry, block_index):
            grad_keys, grad_values = carry
            row_start = block_index * QB
            mask = allowed_mask(segment_row, pad_row, inside_row, own_random, row_start, QB)
            query_rows = lax.dynamic_slice_in_dim(queries_s, row_start, QB, 0)
            grad_rows = lax.dynamic_slice_in_dim(grads_s, row_start, QB, 0)
            lse = lax.dynamic_index_in_dim(sums_s, block_index, 0, keepdims=False)
            scores = (
                jnp.einsum("qhd,khd->hqk", query_rows, keys_s, preferred_element_type=jnp.float32)
                * scale
            )
            probs = jnp.where(mask, jnp.exp(scores - lse[:, :, None]), 0.0)
            probs_low = probs.astype(jnp.bfloat16)
            grad_values = grad_values + jnp.einsum(
                "hqk,qhd->khd", probs_low, grad_rows, preferred_element_type=jnp.float32
            )
            grad_probs = jnp.einsum(
                "qhd,khd->hqk", grad_rows, values_s, preferred_element_type=jnp.float32
            )
            inner = jnp.sum(probs * grad_probs, axis=2, keepdims=True)
            grad_scores = (probs * (grad_probs - inner)).astype(jnp.bfloat16)
            grad_query = (
                jnp.einsum("hqk,khd->qhd", grad_scores, keys_s, preferred_element_type=jnp.float32)
                * scale
            )
            grad_keys = (
                grad_keys
                + jnp.einsum(
                    "hqk,qhd->khd", grad_scores, query_rows, preferred_element_type=jnp.float32
                )
                * scale
            )
            return ((grad_keys, grad_values), grad_query)

        zeros = jnp.zeros(keys_s.shape, jnp.float32)
        (grad_keys, grad_values), grad_queries = lax.scan(
            one_block, (zeros, zeros), jnp.arange(n_blocks, dtype=jnp.int32)
        )
        grad_queries = grad_queries.reshape(keys_s.shape)
        return (
            grad_queries.astype(jnp.bfloat16),
            grad_keys.astype(jnp.bfloat16),
            grad_values.astype(jnp.bfloat16),
        )

    grad_q, grad_k, grad_v = lax.map(
        attend_back, (head_q, head_k, head_v, grad_heads, lse_all, segments, padding, insides)
    )

    def head_split(array):
        return array.reshape(seqs_here, seq_len, 1, heads_here * HD)

    grad_q, grad_k, grad_v = (
        lax.all_to_all(head_split(grad_q), "seq", split_axis=1, concat_axis=2, tiled=True),
        lax.all_to_all(head_split(grad_k), "seq", split_axis=1, concat_axis=2, tiled=True),
        lax.all_to_all(head_split(grad_v), "seq", split_axis=1, concat_axis=2, tiled=True),
    )
    grad_q, grad_k, grad_v = (
        grad_q.reshape(rows, width),
        grad_k.reshape(rows, width),
        grad_v.reshape(rows, width),
    )
    grad_w_query = inner_rows(flat, grad_q)
    grad_b_query = jnp.sum(grad_q.astype(jnp.float32), axis=0)
    grad_w_key = inner_rows(flat, grad_k)
    grad_w_value = inner_rows(flat, grad_v)
    grad_b_value = jnp.sum(grad_v.astype(jnp.float32), axis=0)
    grad_inputs = (
        grad_hidden
        + times_back(grad_q, back_query)
        + times_back(grad_k, back_key)
        + times_back(grad_v, back_value)
    )
    summed = (
        lax.psum_scatter(grad_w_query, "dp", scatter_dimension=0, tiled=True),
        lax.psum_scatter(grad_w_key, "dp", scatter_dimension=0, tiled=True),
        lax.psum_scatter(grad_w_value, "dp", scatter_dimension=0, tiled=True),
        lax.psum_scatter(grad_w_out, "dp", scatter_dimension=0, tiled=True),
        lax.psum_scatter(grad_w_up, "dp", scatter_dimension=0, tiled=True),
        lax.psum_scatter(grad_w_down, "dp", scatter_dimension=0, tiled=True),
        lax.psum_scatter(grad_b_query, "dp", scatter_dimension=0, tiled=True),
        lax.psum_scatter(grad_b_value, "dp", scatter_dimension=0, tiled=True),
        lax.psum_scatter(grad_b_out, "dp", scatter_dimension=0, tiled=True),
        lax.psum_scatter(grad_gain_one, "dp", scatter_dimension=0, tiled=True),
        lax.psum_scatter(grad_shift_one, "dp", scatter_dimension=0, tiled=True),
        lax.psum_scatter(grad_b_up, "dp", scatter_dimension=0, tiled=True),
        lax.psum_scatter(grad_b_down, "dp", scatter_dimension=0, tiled=True),
        lax.psum_scatter(grad_gain_two, "dp", scatter_dimension=0, tiled=True),
        lax.psum_scatter(grad_shift_two, "dp", scatter_dimension=0, tiled=True),
    )
    tiled = [jnp.broadcast_to(item[:, None], (item.shape[0], n_seq)) for item in summed[6:]]
    owned = (
        lax.psum_scatter(summed[0], "seq", scatter_dimension=1, tiled=True),
        lax.psum_scatter(summed[1], "seq", scatter_dimension=1, tiled=True),
        lax.psum_scatter(summed[2], "seq", scatter_dimension=1, tiled=True),
        lax.psum_scatter(summed[3], "seq", scatter_dimension=1, tiled=True),
        lax.psum_scatter(summed[4], "seq", scatter_dimension=1, tiled=True),
        lax.psum_scatter(summed[5], "seq", scatter_dimension=1, tiled=True),
        lax.psum_scatter(tiled[0], "seq", scatter_dimension=1, tiled=True),
        lax.psum_scatter(tiled[1], "seq", scatter_dimension=1, tiled=True),
        lax.psum_scatter(tiled[2], "seq", scatter_dimension=1, tiled=True),
        lax.psum_scatter(tiled[3], "seq", scatter_dimension=1, tiled=True),
        lax.psum_scatter(tiled[4], "seq", scatter_dimension=1, tiled=True),
        lax.psum_scatter(tiled[5], "seq", scatter_dimension=1, tiled=True),
        lax.psum_scatter(tiled[6], "seq", scatter_dimension=1, tiled=True),
        lax.psum_scatter(tiled[7], "seq", scatter_dimension=1, tiled=True),
        lax.psum_scatter(tiled[8], "seq", scatter_dimension=1, tiled=True),
    )
    vectors = [item[:, 0] for item in owned[6:]]
    return (
        output.reshape(seqs_here, shard_len, width),
        grad_inputs.reshape(seqs_here, shard_len, width),
        owned[0],
        vectors[0],
        owned[1],
        owned[2],
        vectors[1],
        owned[3],
        vectors[2],
        vectors[3],
        vectors[4],
        owned[4],
        vectors[5],
        owned[5],
        vectors[6],
        vectors[7],
        vectors[8],
    )


def solution(mesh):
    return jax.shard_map(
        shards,
        mesh=mesh,
        in_specs=(
            P("dp", "seq", None),
            P("dp", "seq", None),
            P("dp", None),
            P("dp", None),
            P(),
            P("dp", "seq"),
            P("dp"),
            P("dp", "seq"),
            P("dp", "seq"),
            P("dp"),
            P("dp", "seq"),
            P("dp"),
            P("dp"),
            P("dp"),
            P("dp", "seq"),
            P("dp"),
            P("dp", "seq"),
            P("dp"),
            P("dp"),
            P("dp"),
        ),
        out_specs=(
            P("dp", "seq", None),
            P("dp", "seq", None),
            P("dp", "seq"),
            P("dp"),
            P("dp", "seq"),
            P("dp", "seq"),
            P("dp"),
            P("dp", "seq"),
            P("dp"),
            P("dp"),
            P("dp"),
            P("dp", "seq"),
            P("dp"),
            P("dp", "seq"),
            P("dp"),
            P("dp"),
            P("dp"),
        ),
        check_vma=False,
    )
```

profile of v0, /device:TPU:0, one launch (start us, length us, event | category | flops | bytes accessed | tf_op | source)
XLA Modules:
  0.0 1549.7 jit_solution(3762413004708537252)
XLA Ops:
  39.3 38.5 %all-reduce.29 = (bf16[768]{0:T(1024)(128)(2,1)S(1)}, bf16[768]{0:T(1024)(128)(2,1)S(1)}, bf16[768]{0:T(1024)(128)(2,1)}, bf16[768]{0:T(1024)(128)(2,1)}, bf16[7...) all-reduce(bf16[768]{0:T(1024)(128)(2,1)S(1)} %dynamic-update-slice, ...), channel_id=1, replica_groups=mesh['seq'=4,'dp'=8] {'dp'}, use_global_device_ids=true, to_apply=%add.1 | all-reduce | flops 6144 | bytes 24576
  87.9 21.7 %all_gather.83 = bf16[96,768]{0,1:T(8,128)(2,1)S(1)} all-gather(bf16[96,192]{0,1:T(8,128)(2,1)S(1)} %copy.232), channel_id=1, replica_groups=mesh['seq'=4,'dp'=8] {'seq'}, dimensions={1}, use_global_device_ids=true | all-gather | bytes 184320 | tf_op jit(solution)/shard_map/all_gather | solution.py:99
  122.5 21.7 %all-gather.10.cloned.1.call-done = bf16[768,768]{1,0:T(8,128)(2,1)} async-done(((bf16[96,768]{1,0:T(8,128)(2,1)}), bf16[768,768]{1,0:T(8,128)(2,1)}) %all-gather.10.cloned.1.call-update) | async-done | bytes 1179664 | tf_op jit(solution)/shard_map/all_gather | solution.py:105
  159.4 24.4 %all_gather.88 = bf16[96,3072]{1,0:T(8,128)(2,1)} all-gather(bf16[96,768]{1,0:T(8,128)(2,1)S(1)} %copy-done.37), channel_id=1, replica_groups=mesh['seq'=4,'dp'=8] {'seq'}, dimensions={1}, use_global_device_ids=true | all-gather | bytes 737280 | tf_op jit(solution)/shard_map/all_gather | solution.py:100
  201.8 114.4 %while.94 = (s32[]{:T(128)}, bf16[4,1024,3,64]{1,3,2,0:T(8,128)(2,1)}, f32[4,2,3,512]{3,2,1,0:T(4,128)}, s32[4,1024]{1,0:T(4,128)S(1)}, s32[4,1024]{1,0:T(4,128)...) while((s32[]{:T(128)}, ...), condition=%wide.region_8.9_spmd, body=%wide.region_2.8_spmd.sunk | while | flops 424790912 | bytes 34466940 | solution.py:182
  205.0 22.9 %while.97 = (s32[]{:T(128)}, bf16[2,512,3,64]{1,3,2,0:T(8,128)(2,1)S(1)}, f32[2,3,512]{2,1,0:T(4,128)S(1)}, s32[2]{0:T(128)S(1)}, s32[1024]{0:T(1024)S(1)}, /*in...) while((s32[]{:T(128)}, ...), condition=%wide.region_7.7_spmd, body=%wide.region_3.6_spmd.sunk | while | flops 424790912 | bytes 29693712 | solution.py:179
  233.5 22.9 %while.97 = (s32[]{:T(128)}, bf16[2,512,3,64]{1,3,2,0:T(8,128)(2,1)S(1)}, f32[2,3,512]{2,1,0:T(4,128)S(1)}, s32[2]{0:T(128)S(1)}, s32[1024]{0:T(1024)S(1)}, /*in...) while((s32[]{:T(128)}, ...), condition=%wide.region_7.7_spmd, body=%wide.region_3.6_spmd.sunk | while | flops 424790912 | bytes 29693712 | solution.py:179
  262.1 22.9 %while.97 = (s32[]{:T(128)}, bf16[2,512,3,64]{1,3,2,0:T(8,128)(2,1)S(1)}, f32[2,3,512]{2,1,0:T(4,128)S(1)}, s32[2]{0:T(128)S(1)}, s32[1024]{0:T(1024)S(1)}, /*in...) while((s32[]{:T(128)}, ...), condition=%wide.region_7.7_spmd, body=%wide.region_3.6_spmd.sunk | while | flops 424790912 | bytes 29693712 | solution.py:179
  290.6 22.9 %while.97 = (s32[]{:T(128)}, bf16[2,512,3,64]{1,3,2,0:T(8,128)(2,1)S(1)}, f32[2,3,512]{2,1,0:T(4,128)S(1)}, s32[2]{0:T(128)S(1)}, s32[1024]{0:T(1024)S(1)}, /*in...) while((s32[]{:T(128)}, ...), condition=%wide.region_7.7_spmd, body=%wide.region_3.6_spmd.sunk | while | flops 424790912 | bytes 29693712 | solution.py:179
  324.9 30.0 %all_gather.91 = bf16[384,768]{0,1:T(8,128)(2,1)} all-gather(bf16[384,192]{0,1:T(8,128)(2,1)S(1)} %copy-done.38), channel_id=1, replica_groups=mesh['seq'=4,'dp'=8] {'seq'}, dimensions={1}, use_global_device_ids=true | all-gather | bytes 737280 | tf_op jit(solution)/shard_map/all_gather | solution.py:101
  355.1 26.6 %all-gather = bf16[8,1,384]{2,1,0:T(2,128)(2,1)S(1)} all-gather(bf16[1,1,384]{2,1,0:T(2,128)(2,1)S(1)} %reshape.730), channel_id=1, replica_groups=mesh['seq'=4,'dp'=8] {'dp'}, dimensions={0}, use_global_device_ids=true | all-gather | bytes 6912 | tf_op jit(solution)/shard_map/all_gather | solution.py:115
  393.6 36.4 %multiply_convert_fusion.1 = (bf16[1024,3072]{1,0:T(8,128)(2,1)}, f32[1024,3072]{1,0:T(8,128)}, f32[1024,3072]{1,0:T(8,128)}) fusion(f32[3072]{0:T(1024)S(1)} %bitcast.339, bf16[768,3072]{1,0:T(8,128)(2,1)} %all-gather.16.cloned.1.call-done, f32[1024,768]{1,0:T(8,128)S(1)} %get-tuple-element.1172, f32[768]{0:T(1024)S(1)} %convert_element_type.152, ...), kind=kOutput, calls=%fused_computation.113 | convolution fusion | flops 5043388416 | bytes 39348224 | tf_op jit(solution)/shard_map/dot_general | solution.py:200
  449.3 17.8 %convert_reduce_fusion = (f32[3072]{0:T(1024)}, bf16[1024,3072]{1,0:T(8,128)(2,1)}) fusion(f32[1024,3072]{1,0:T(8,128)} %get-tuple-element.1145, bf16[1024,768]{1,0:T(8,128)(2,1)S(1)} %get-tuple-element.1137, bf16[3072,768]{0,1:T(8,128)(2,1)} %all-gather.18.cloned.1.call-done, f32[1024,3072]{1,0:T(8,128)} %get-tuple-element.1173, f32[3072]{0:T(1024)S(1)} %bitcast.340), kind=kOutput, calls=%fused_computation.111 | convolution fusion | flops 4885312512 | bytes 37773312 | tf_op jit(solution)/shard_map/dot_general | solution.py:60
  495.2 15.6 %all-to-all-done.4 = bf16[4,256,4,192]{1,0,3,2:T(4,128)(2,1)S(1)} async-done(((bf16[4,256,4,192]{1,0,3,2:T(4,128)(2,1)}), bf16[4,256,4,192]{1,0,3,2:T(4,128)(2,1)S(1)}, u32[]{:S(2)}, u32[]{:S(2)}) %all-to-all-start.4) | async-done | bytes 1572896 | tf_op jit(solution)/shard_map/all_to_all | solution.py:237
  518.7 290.4 %while.96 = (s32[]{:T(128)}, bf16[4,1024,3,64]{1,3,2,0:T(8,128)(2,1)}, bf16[4,1024,3,64]{1,3,2,0:T(8,128)(2,1)}, bf16[4,1024,3,64]{1,3,2,0:T(8,128)(2,1)}, s32[4...) while((s32[]{:T(128)}, ...), condition=%wide.region_22.23_spmd, body=%wide.region_17.22_spmd.sunk | while | flops 1031719808 | bytes 148861008 | solution.py:290
  526.5 59.5 %while.98 = (s32[]{:T(128)}, f32[1024,3,64]{0,2,1:T(8,128)}, f32[1024,3,64]{0,2,1:T(8,128)}, bf16[2,512,3,64]{1,3,2,0:T(8,128)(2,1)}, s32[2]{0:T(128)S(1)}, /*in...) while((s32[]{:T(128)}, f32[1024,3,64]{0,2,1:T(8,128)}, ...), condition=%wide.region_21.21_spmd.clone, body=%wide.region_18.20_spmd.clone.sunk | while | flops 1031326592 | bytes 140946064 | solution.py:280
  599.1 59.5 %while.98 = (s32[]{:T(128)}, f32[1024,3,64]{0,2,1:T(8,128)}, f32[1024,3,64]{0,2,1:T(8,128)}, bf16[2,512,3,64]{1,3,2,0:T(8,128)(2,1)}, s32[2]{0:T(128)S(1)}, /*in...) while((s32[]{:T(128)}, f32[1024,3,64]{0,2,1:T(8,128)}, ...), condition=%wide.region_21.21_spmd.clone, body=%wide.region_18.20_spmd.clone.sunk | while | flops 1031326592 | bytes 140946064 | solution.py:280
  671.7 59.5 %while.98 = (s32[]{:T(128)}, f32[1024,3,64]{0,2,1:T(8,128)}, f32[1024,3,64]{0,2,1:T(8,128)}, bf16[2,512,3,64]{1,3,2,0:T(8,128)(2,1)}, s32[2]{0:T(128)S(1)}, /*in...) while((s32[]{:T(128)}, f32[1024,3,64]{0,2,1:T(8,128)}, ...), condition=%wide.region_21.21_spmd.clone, body=%wide.region_18.20_spmd.clone.sunk | while | flops 1031326592 | bytes 140946064 | solution.py:280
  744.2 59.5 %while.98 = (s32[]{:T(128)}, f32[1024,3,64]{0,2,1:T(8,128)}, f32[1024,3,64]{0,2,1:T(8,128)}, bf16[2,512,3,64]{1,3,2,0:T(8,128)(2,1)}, s32[2]{0:T(128)S(1)}, /*in...) while((s32[]{:T(128)}, f32[1024,3,64]{0,2,1:T(8,128)}, ...), condition=%wide.region_21.21_spmd.clone, body=%wide.region_18.20_spmd.clone.sunk | while | flops 1031326592 | bytes 140946064 | solution.py:280
  812.0 29.1 %all_to_all.120 = bf16[4,1024,1,192]{3,0,2,1:T(4,128)(2,1)} all-to-all(bf16[4,1024,1,192]{3,0,2,1:T(4,128)(2,1)S(1)} %copy.241), channel_id=1, replica_groups=mesh['seq'=4,'dp'=8] {'seq'}, dimensions={1} | all-to-all | bytes 3145728 | tf_op jit(solution)/shard_map/all_to_all | solution.py:299
  854.5 28.9 %all_to_all.121 = bf16[4,1024,1,192]{3,0,2,1:T(4,128)(2,1)} all-to-all(bf16[4,1024,1,192]{3,0,2,1:T(4,128)(2,1)S(1)} %copy.244), channel_id=1, replica_groups=mesh['seq'=4,'dp'=8] {'seq'}, dimensions={1} | all-to-all | bytes 3145728 | tf_op jit(solution)/shard_map/all_to_all | solution.py:300
  896.7 28.9 %all_to_all.122 = bf16[4,1024,1,192]{3,0,2,1:T(4,128)(2,1)} all-to-all(bf16[4,1024,1,192]{3,0,2,1:T(4,128)(2,1)S(1)} %copy.239), channel_id=1, replica_groups=mesh['seq'=4,'dp'=8] {'seq'}, dimensions={1} | all-to-all | bytes 3145728 | tf_op jit(solution)/shard_map/all_to_all | solution.py:298
  938.9 11.0 fusion.70
  965.5 25.6 %reduce-scatter.41.cloned.1.call-done = f32[96,768]{1,0:T(8,128)} async-done(((f32[768,768]{1,0:T(8,128)}), f32[96,768]{1,0:T(8,128)}) %reduce-scatter.41.cloned.1.call-update) | async-done | bytes 294928
  993.1 70.3 %reduce-scatter.37.cloned.1.call-done = f32[96,768]{1,0:T(8,128)} async-done(((f32[768,768]{1,0:T(8,128)}), f32[96,768]{1,0:T(8,128)}) %reduce-scatter.37.cloned.1.call-update) | async-done | bytes 294928
  1065.4 163.0 %reduce-scatter.31.cloned.1.call-done = f32[96,3072]{1,0:T(8,128)} async-done(((f32[768,3072]{1,0:T(8,128)}), f32[96,3072]{1,0:T(8,128)}) %reduce-scatter.31.cloned.1.call-update) | async-done | bytes 1179664 | tf_op jit(solution)/shard_map/reduce_scatter | solution.py:323
  1232.3 160.7 %reduce-scatter.35.cloned.1.call-done = f32[384,768]{1,0:T(8,128)} async-done(((f32[3072,768]{1,0:T(8,128)}), f32[384,768]{1,0:T(8,128)}) %reduce-scatter.35.cloned.1.call-update) | async-done | bytes 1179664 | tf_op jit(solution)/shard_map/reduce_scatter | solution.py:324
  1398.4 35.7 %all-reduce.27 = (f32[768]{0:T(1024)S(1)}, f32[768]{0:T(1024)S(1)}, f32[768]{0:T(1024)S(1)}, f32[768]{0:T(1024)S(1)}, f32[768]{0:T(1024)S(1)}, /*index=5*/f32[30...) all-reduce(f32[768]{0:T(1024)S(1)} %reduce_sum.199, ...), channel_id=4, replica_groups=mesh['seq'=4,'dp'=8] {'dp'}, use_global_device_ids=true, to_apply=%region_26.27.clone | all-reduce | flops 9216 | bytes 73728
  1434.9 10.5 all-reduce.28
  1466.1 19.0 %reduce-scatter.23.cloned.1.call-done = f32[96,192]{0,1:T(8,128)} async-done(((f32[96,768]{0,1:T(8,128)}), f32[96,192]{0,1:T(8,128)}) %reduce-scatter.23.cloned.1.call-update) | async-done | bytes 73744 | tf_op jit(solution)/shard_map/reduce_scatter | solution.py:337
  1486.7 27.0 %reduce-scatter.33.cloned.1.call-done = f32[96,768]{1,0:T(8,128)} async-done(((f32[96,3072]{1,0:T(8,128)}), f32[96,768]{1,0:T(8,128)}) %reduce-scatter.33.cloned.1.call-update) | async-done | bytes 294928 | tf_op jit(solution)/shard_map/reduce_scatter | solution.py:341
  1513.7 28.6 %reduce-scatter.45.cloned.1.call-done = f32[192,384]{1,0:T(8,128)} async-done(((f32[768,384]{1,0:T(8,128)}), f32[192,384]{1,0:T(8,128)}) %reduce-scatter.45.cloned.1.call-update) | async-done | bytes 294928
  (927 shorter events, 631.2 us)
Async XLA Ops:
  7.2 178.4 %copy-start = (s32[12,16,3]{1,2,0:T(4,128)S(1)}, s32[12,16,3]{1,2,0:T(4,128)}, u32[]{:S(2)}) copy-start(s32[12,16,3]{1,2,0:T(4,128)} %param.32) | copy-start | bytes 6916
  7.2 70.6 %all-gather.8.cloned.1.call-start = ((), (), s32[]{:S(2)}) async-start(), calls=%async_computation.20 | async-start | bytes 1327104 | tf_op jit(solution)/shard_map/all_gather | solution.py:104
  15.8 94.6 %all-gather.12.cloned.1.call-start = ((), (), s32[]{:S(2)}) async-start(), calls=%async_computation.22 | async-start | bytes 1327104 | tf_op jit(solution)/shard_map/all_gather | solution.py:106
  23.2 120.9 %all-gather.10.cloned.1.call-start = ((), (), s32[]{:S(2)}) async-start(), calls=%async_computation.21 | async-start | bytes 1327104 | tf_op jit(solution)/shard_map/all_gather | solution.py:105
  84.1 34.8 %all-to-all-start = ((bf16[4,256,4,192]{1,0,3,2:T(4,128)(2,1)}), bf16[4,256,4,192]{1,0,3,2:T(4,128)(2,1)S(1)}, u32[]{:S(2)}, u32[]{:S(2)}) async-start(bf16[4,256,4,192]{1,0,3,2:T(4,128)(2,1)} %reshape.687), calls=%async_computation | async-start | bytes 3145728 | tf_op jit(solution)/shard_map/all_to_all | solution.py:148
  87.7 301.2 %all-gather.14.cloned.1.call-start = ((), (), s32[]{:S(2)}) async-start(), calls=%async_computation.23 | async-start | bytes 1327104 | tf_op jit(solution)/shard_map/all_gather | solution.py:107
  118.9 36.0 %all-to-all-start.2 = ((bf16[4,256,4,192]{1,0,3,2:T(4,128)(2,1)}), bf16[4,256,4,192]{1,0,3,2:T(4,128)(2,1)S(1)}, u32[]{:S(2)}, u32[]{:S(2)}) async-start(bf16[4,256,4,192]{1,0,3,2:T(4,128)(2,1)} %reshape.691), calls=%async_computation.2 | async-start | bytes 3145728 | tf_op jit(solution)/shard_map/all_to_all | solution.py:150
  154.9 40.5 %all-to-all-start.1 = ((bf16[4,256,4,192]{1,0,3,2:T(4,128)(2,1)}), bf16[4,256,4,192]{1,0,3,2:T(4,128)(2,1)}, u32[]{:S(2)}, u32[]{:S(2)}) async-start(bf16[4,256,4,192]{1,0,3,2:T(4,128)(2,1)} %reshape.689), calls=%async_computation.1 | async-start | bytes 3145728 | tf_op jit(solution)/shard_map/all_to_all | solution.py:149
  159.3 234.3 %all-gather.16.cloned.1.call-start = ((), (), s32[]{:S(2)}) async-start(), calls=%async_computation.24 | async-start | bytes 5308416 | tf_op jit(solution)/shard_map/all_gather | solution.py:108
  320.4 61.4 %all-to-all-start.3 = ((bf16[4,1024,1,192]{3,0,2,1:T(4,128)(2,1)}), bf16[4,1024,1,192]{3,0,2,1:T(4,128)(2,1)}, u32[]{:S(2)}, u32[]{:S(2)}) async-start(bf16[4,1024,1,192]{3,0,2,1:T(4,128)(2,1)} %copy.230), calls=%async_computation.3 | async-start | bytes 4194304 | tf_op jit(solution)/shard_map/all_to_all | solution.py:185
  324.9 108.8 %all-gather.18.cloned.1.call-start = ((), (), s32[]{:S(2)}) async-start(), calls=%async_computation.25 | async-start | bytes 5308416 | tf_op jit(solution)/shard_map/all_gather | solution.py:109
  487.2 23.6 %all-to-all-start.4 = ((bf16[4,256,4,192]{1,0,3,2:T(4,128)(2,1)}), bf16[4,256,4,192]{1,0,3,2:T(4,128)(2,1)S(1)}, u32[]{:S(2)}, u32[]{:S(2)}) async-start(bf16[4,256,4,192]{1,0,3,2:T(4,128)(2,1)} %reshape.696), calls=%async_computation.4 | async-start | bytes 3145728 | tf_op jit(solution)/shard_map/all_to_all | solution.py:237
  490.8 470.8 %reduce-scatter.29.cloned.1.call-start = ((), (), s32[]{:S(2)}) async-start(), calls=%async_computation.29 | async-start | bytes 2654208 | tf_op jit(solution)/shard_map/reduce_scatter | solution.py:322
  495.1 468.4 %reduce-scatter.39.cloned.1.call-start = ((), (), s32[]{:S(2)}) async-start(), calls=%async_computation.34 | async-start | bytes 2654208
  851.5 139.7 %reduce-scatter.41.cloned.1.call-start = ((), (), s32[]{:S(2)}) async-start(), calls=%async_computation.35 | async-start | bytes 2654208
  893.7 169.8 %reduce-scatter.37.cloned.1.call-start = ((), (), s32[]{:S(2)}) async-start(), calls=%async_computation.33 | async-start | bytes 2654208
  938.8 289.6 %reduce-scatter.31.cloned.1.call-start = ((), (), s32[]{:S(2)}) async-start(), calls=%async_computation.30 | async-start | bytes 10616832 | tf_op jit(solution)/shard_map/reduce_scatter | solution.py:323
  949.9 443.1 %reduce-scatter.35.cloned.1.call-start = ((), (), s32[]{:S(2)}) async-start(), calls=%async_computation.32 | async-start | bytes 10616832 | tf_op jit(solution)/shard_map/reduce_scatter | solution.py:324
  961.5 268.3 %copy-start.64 = (u32[32]{0:T(128)S(1)}, u32[32]{0:T(128)}, u32[]{:S(2)}) copy-start(u32[32]{0:T(128)} %constant.472) | copy-start | bytes 388
  961.5 499.7 %reduce-scatter.43.cloned.1.call-start = ((), (), s32[]{:S(2)}) async-start(), calls=%async_computation.36 | async-start | bytes 491520
  963.5 499.3 %reduce-scatter.25.cloned.1.call-start = ((), (), s32[]{:S(2)}) async-start(), calls=%async_computation.27 | async-start | bytes 491520 | tf_op jit(solution)/shard_map/reduce_scatter | solution.py:338
  965.5 499.0 %reduce-scatter.27.cloned.1.call-start = ((), (), s32[]{:S(2)}) async-start(), calls=%async_computation.28 | async-start | bytes 491520 | tf_op jit(solution)/shard_map/reduce_scatter | solution.py:339
  993.1 492.0 %reduce-scatter.23.cloned.1.call-start = ((), (), s32[]{:S(2)}) async-start(), calls=%async_computation.26 | async-start | bytes 491520 | tf_op jit(solution)/shard_map/reduce_scatter | solution.py:337
  1065.3 448.4 %reduce-scatter.33.cloned.1.call-start = ((), (), s32[]{:S(2)}) async-start(), calls=%async_computation.31 | async-start | bytes 1474560 | tf_op jit(solution)/shard_map/reduce_scatter | solution.py:341
  1228.3 167.4 %copy-start.17 = (bf16[4,4,256,1,192]{2,1,4,0,3:T(4,128)(2,1)S(1)}, bf16[4,4,256,1,192]{2,1,4,0,3:T(4,128)(2,1)}, u32[]{:S(2)}) copy-start(bf16[4,4,256,1,192]{2,1,4,0,3:T(4,128)(2,1)} %copy-done.16) | copy-start | bytes 4718596
  1228.4 314.0 %reduce-scatter.45.cloned.1.call-start = ((), (), s32[]{:S(2)}) async-start(), calls=%async_computation.37 | async-start | bytes 1474560
  1232.2 166.2 %copy-start.46 = (f32[768]{0:T(1024)S(1)}, f32[768]{0:T(1024)}, u32[]{:S(2)}) copy-start(f32[768]{0:T(1024)} %get-tuple-element.1136) | copy-start | bytes 9220
  1232.2 166.2 %copy-start.47 = (f32[768]{0:T(1024)S(1)}, f32[768]{0:T(1024)}, u32[]{:S(2)}) copy-start(f32[768]{0:T(1024)} %get-tuple-element.1138) | copy-start | bytes 9220
  1232.2 166.2 %copy-start.48 = (f32[768]{0:T(1024)S(1)}, f32[768]{0:T(1024)}, u32[]{:S(2)}) copy-start(f32[768]{0:T(1024)} %get-tuple-element.1011) | copy-start | bytes 9220
  1232.2 166.2 %copy-start.49 = (f32[3072]{0:T(1024)S(1)}, f32[3072]{0:T(1024)}, u32[]{:S(2)}) copy-start(f32[3072]{0:T(1024)} %get-tuple-element.1177) | copy-start | bytes 36868
  1232.2 166.2 %copy-start.50 = (f32[768]{0:T(1024)S(1)}, f32[768]{0:T(1024)}, u32[]{:S(2)}) copy-start(f32[768]{0:T(1024)} %get-tuple-element.1009) | copy-start | bytes 9220
  1232.3 166.2 %copy-start.51 = (f32[768]{0:T(1024)S(1)}, f32[768]{0:T(1024)}, u32[]{:S(2)}) copy-start(f32[768]{0:T(1024)} %get-tuple-element.1013) | copy-start | bytes 9220
  (128 other events, 1712.2 us)
Sparse Core Ops, SparseCore 0:
  16.0 42.7 all-gather.7
  61.5 39.9 all-gather.11
  104.3 39.7 all-gather.9
  146.8 39.7 all-gather.13
  188.6 78.0 all-gather.15
  355.1 78.5 all-gather.17
  495.3 68.1 reduce-scatter.28
  851.6 66.9 reduce-scatter.38
  922.1 68.9 reduce-scatter.40
  994.5 68.8 reduce-scatter.36
  1067.0 161.2 reduce-scatter.30
  1231.8 161.1 reduce-scatter.34
  1395.5 19.9 reduce-scatter.42
  1417.8 20.8 reduce-scatter.24
  1441.0 20.8 reduce-scatter.26
  1464.3 20.8 reduce-scatter.22
  1488.1 25.5 reduce-scatter.32
  1516.7 25.6 reduce-scatter.44
where the time goes:
time: 1560 us; the launch traced here: 1550 us
  waiting for transfers between devices  536 us (34%)
  matrix products  304 us (19%)
  blocking collectives  293 us (19%)
  local copies, waits for them, and re-layouts  272 us (17%)
  other arithmetic  77.8 us (5%)
  loops' own time  29.3 us (2%)
  starting transfers between devices  20.2 us (1%)
  between operations  18 us (1%)
    reduce_scatter x1, waiting for transfers between devices, shards(): lax.psum_scatter(grad_w_up, 'dp', scatter_dimension=0, tiled=True)  163 us
    reduce_scatter x1, waiting for transfers between devices, shards(): lax.psum_scatter(grad_w_down, 'dp', scatter_dimension=0, tiled=True)  161 us
    unnamed x23, waiting for transfers between devices  125 us
    unnamed x3, blocking collectives  84.7 us
    dot_general x16, matrix products, one_block(): jnp.einsum('qhd,khd->hqk', query_rows, keys_s, preferred_element_type=jnp...  63.3 us
    unnamed x163, local copies, waits for them, and re-layouts  48.7 us
    dot_general x6, matrix products, times_back(): lax.dot_general(left, matrix, (((1,), (1,)), ((), ())), preferred_element...  38 us
    dot_general x1, matrix products, shards(): jnp.dot(normed_low, full_up, preferred_element_type=jnp.float32) + vec_up  36.4 us
  transfers between devices with their start and end apart: 23, of which 10 were waited for; matrix products, arithmetic and copies ran while one was open for 37% of the time, Pallas kernels for 0%

commit v1 on v0

--- a/solution.py
+++ b/solution.py
@@ -60,6 +60,111 @@
     return lax.dot_general(
         left, matrix, (((1,), (1,)), ((), ())), preferred_element_type=jnp.float32
     )
+
+
+def axis_bits(axis):
+    size = lax.axis_size(axis)
+    bits = size.bit_length() - 1
+    assert 1 << bits == size
+    return [(axis, b) for b in range(bits)]
+
+
+def bit_orders(n_parts):
+    seq_bits, dp_bits = axis_bits("seq"), axis_bits("dp")
+    first, last = seq_bits[:1], dp_bits[-1:]
+    middle = seq_bits[1:] + dp_bits[:-1]
+    orders = []
+    for part in range(n_parts):
+        shift = (part * len(middle)) // n_parts if middle else 0
+        orders.append(first + middle[shift:] + middle[:shift] + last)
+    return orders
+
+
+def layout_bits():
+    return [("dp", b) for b in reversed(range(len(axis_bits("dp"))))] + [
+        ("seq", b) for b in reversed(range(len(axis_bits("seq"))))
+    ]
+
+
+def my_bit(bit):
+    axis, b = bit
+    return (lax.axis_index(axis) >> b) & 1
+
+
+def partner(bit):
+    axis, b = bit
+    size = lax.axis_size(axis)
+    return [(i, i ^ (1 << b)) for i in range(size)]
+
+
+def split_parts(flat, n_parts):
+    width = flat.shape[-1]
+    step = -(-width // (n_parts * 128)) * 128
+    pad = step * n_parts - width
+    if pad:
+        flat = jnp.concatenate([flat, jnp.zeros(flat.shape[:-1] + (pad,), flat.dtype)], axis=-1)
+    return [flat[..., i * step:(i + 1) * step] for i in range(n_parts)], width
+
+
+def gather_blocks(flat, n_parts=3):
+    order_all = layout_bits()
+    parts, width = split_parts(flat, n_parts)
+    out = []
+    for part, order in zip(parts, bit_orders(n_parts)):
+        present = []
+        buf = part
+        for bit in reversed(order):
+            got = lax.ppermute(buf, bit[0], partner(bit))
+            mine = my_bit(bit) == 0
+            low = jnp.where(mine, buf, got)
+            high = jnp.where(mine, got, buf)
+            present.append(bit)
+            present.sort(key=order_all.index)
+            buf = jnp.stack([low, high], axis=present.index(bit))
+        out.append(buf.reshape(-1, buf.shape[-1]))
+    return jnp.concatenate(out, axis=-1)[:, :width]
+
+
+def reduce_blocks(blocked, n_parts=3):
+    order_all = layout_bits()
+    shape = [2] * len(order_all)
+    parts, width = split_parts(blocked, n_parts)
+    out = []
+    for part, order in zip(parts, bit_orders(n_parts)):
+        present = list(order_all)
+        buf = part.reshape(shape + [part.shape[-1]])
+        for bit in order:
+            axis = present.index(bit)
+            mine = my_bit(bit)
+            keep = lax.dynamic_index_in_dim(buf, mine, axis, keepdims=False)
+            send = lax.dynamic_index_in_dim(buf, 1 - mine, axis, keepdims=False)
+            buf = keep + lax.ppermute(send, bit[0], partner(bit))
+            present.remove(bit)
+        out.append(buf)
+    return jnp.concatenate(out, axis=-1)[:width]
+
+
+def to_blocks(matrix_block):
+    return matrix_block.reshape(-1)
+
+
+def from_blocks(gathered, n_dp, n_seq, rows, cols):
+    return (
+        gathered.reshape(n_dp, n_seq, rows, cols).transpose(0, 2, 1, 3).reshape(n_dp * rows, n_seq * cols)
+    )
+
+
+def blocked_grad(left, right, n_dp, n_seq):
+    tokens = left.shape[0]
+    a = left.reshape(tokens, n_dp, left.shape[1] // n_dp)
+    b = right.reshape(tokens, n_seq, right.shape[1] // n_seq)
+    g = jnp.einsum("tar,tbc->abrc", a, b, preferred_element_type=jnp.float32)
+    return g.reshape(n_dp * n_seq, -1)
+
+
+def blocked_vector(vector, n_dp, n_seq):
+    v = vector.reshape(n_dp, 1, -1)
+    return jnp.broadcast_to(v, (n_dp, n_seq, v.shape[-1])).reshape(n_dp * n_seq, -1)
 
 
 def shards(
@@ -92,32 +197,28 @@
     seq_len = shard_len * n_seq
     n_blocks = seq_len // QB
     scale = HD ** (-0.5)
-    columns = (
-        lax.all_gather(w_query, "seq", axis=1, tiled=True),
-        lax.all_gather(w_key, "seq", axis=1, tiled=True),
-        lax.all_gather(w_value, "seq", axis=1, tiled=True),
-        lax.all_gather(w_out, "seq", axis=1, tiled=True),
-        lax.all_gather(w_up, "seq", axis=1, tiled=True),
-        lax.all_gather(w_down, "seq", axis=1, tiled=True),
-    )
-    whole = (
-        lax.all_gather(columns[0], "dp", axis=0, tiled=True),
-        lax.all_gather(columns[1], "dp", axis=0, tiled=True),
-        lax.all_gather(columns[2], "dp", axis=0, tiled=True),
-        lax.all_gather(columns[3], "dp", axis=0, tiled=True),
-        lax.all_gather(columns[4], "dp", axis=0, tiled=True),
-        lax.all_gather(columns[5], "dp", axis=0, tiled=True),
-        lax.all_gather(b_query, "dp", axis=0, tiled=True),
-        lax.all_gather(b_value, "dp", axis=0, tiled=True),
-        lax.all_gather(b_out, "dp", axis=0, tiled=True),
-        lax.all_gather(gain_one, "dp", axis=0, tiled=True),
-        lax.all_gather(shift_one, "dp", axis=0, tiled=True),
-        lax.all_gather(b_up, "dp", axis=0, tiled=True),
-        lax.all_gather(b_down, "dp", axis=0, tiled=True),
-        lax.all_gather(gain_two, "dp", axis=0, tiled=True),
-        lax.all_gather(shift_two, "dp", axis=0, tiled=True),
-    )
-    full_query, full_key, full_value, full_out, full_up, full_down = whole[:6]
+    n_dp = lax.axis_size("dp")
+    first_group = [w_query, w_key, w_value, b_query, b_value]
+    second_group = [w_out, w_up, w_down, b_out, gain_one, shift_one, b_up, b_down, gain_two, shift_two]
+
+    def gather_group(items):
+        flat = jnp.concatenate([item.reshape(-1) for item in items])
+        got = gather_blocks(flat)
+        pieces, offset = [], 0
+        for item in items:
+            size = item.size
+            piece = got[:, offset:offset + size]
+            offset += size
+            if item.ndim == 2:
+                pieces.append(from_blocks(piece, n_dp, n_seq, item.shape[0], item.shape[1]))
+            else:
+                pieces.append(piece.reshape(n_dp, n_seq, size)[:, 0].reshape(-1))
+        return pieces
+
+    full_query, full_key, full_value, g_b_query, g_b_value = gather_group(first_group)
+    (
+        full_out, full_up, full_down, g_b_out, g_gain_one, g_shift_one, g_b_up, g_b_down, g_gain_two, g_shift_two,
+    ) = gather_group(second_group)
     (
         vec_query,
         vec_value,
@@ -128,7 +229,10 @@
         vec_down,
         vec_gain_two,
         vec_shift_two,
-    ) = [item.astype(jnp.float32) for item in whole[6:]]
+    ) = [
+        item.astype(jnp.float32)
+        for item in (g_b_query, g_b_value, g_b_out, g_gain_one, g_shift_one, g_b_up, g_b_down, g_gain_two, g_shift_two)
+    ]
     flat = inputs.reshape(rows, width)
     queries = (jnp.dot(flat, full_query, preferred_element_type=jnp.float32) + vec_query).astype(
         jnp.bfloat16
@@ -202,37 +306,29 @@
     active = gelu_value.astype(jnp.bfloat16)
     mixed = normed + jnp.dot(active, full_down, preferred_element_type=jnp.float32) + vec_down
     output = layer_norm(mixed, vec_gain_two, vec_shift_two).astype(jnp.bfloat16)
-    columns_back = (
-        lax.all_gather(w_query, "seq", axis=1, tiled=True),
-        lax.all_gather(w_key, "seq", axis=1, tiled=True),
-        lax.all_gather(w_value, "seq", axis=1, tiled=True),
-        lax.all_gather(w_out, "seq", axis=1, tiled=True),
-        lax.all_gather(w_up, "seq", axis=1, tiled=True),
-        lax.all_gather(w_down, "seq", axis=1, tiled=True),
-    )
     back_query, back_key, back_value, back_out, back_up, back_down = (
-        lax.all_gather(columns_back[0], "dp", axis=0, tiled=True),
-        lax.all_gather(columns_back[1], "dp", axis=0, tiled=True),
-        lax.all_gather(columns_back[2], "dp", axis=0, tiled=True),
-        lax.all_gather(columns_back[3], "dp", axis=0, tiled=True),
-        lax.all_gather(columns_back[4], "dp", axis=0, tiled=True),
-        lax.all_gather(columns_back[5], "dp", axis=0, tiled=True),
+        full_query, full_key, full_value, full_out, full_up, full_down
     )
     grad_out = cotangent.reshape(rows, width).astype(jnp.float32)
     norm_two_back = jax.vjp(layer_norm, mixed, vec_gain_two, vec_shift_two)[1]
     grad_mixed, grad_gain_two, grad_shift_two = norm_two_back(grad_out)
     grad_lower = grad_mixed.astype(jnp.bfloat16)
     grad_b_down = jnp.sum(grad_lower.astype(jnp.float32), axis=0)
-    grad_w_down = inner_rows(active, grad_lower)
+    grad_w_down = blocked_grad(active, grad_lower, n_dp, n_seq)
     grad_upper = gelu_back(times_back(grad_lower, back_down))[0].astype(jnp.bfloat16)
     grad_b_up = jnp.sum(grad_upper.astype(jnp.float32), axis=0)
-    grad_w_up = inner_rows(normed_low, grad_upper)
+    grad_w_up = blocked_grad(normed_low, grad_upper, n_dp, n_seq)
     grad_normed = grad_mixed + times_back(grad_upper, back_up)
     norm_one_back = jax.vjp(layer_norm, hidden, vec_gain_one, vec_shift_one)[1]
     grad_hidden, grad_gain_one, grad_shift_one = norm_one_back(grad_normed)
     grad_branch = grad_hidden.astype(jnp.bfloat16)
     grad_b_out = jnp.sum(grad_branch.astype(jnp.float32), axis=0)
-    grad_w_out = inner_rows(context_tok, grad_branch)
+    grad_w_out = blocked_grad(context_tok, grad_branch, n_dp, n_seq)
+    group_a = [grad_w_out, grad_w_up, grad_w_down] + [
+        blocked_vector(item, n_dp, n_seq)
+        for item in (grad_b_out, grad_gain_one, grad_shift_one, grad_b_up, grad_b_down, grad_gain_two, grad_shift_two)
+    ]
+    summed_a = reduce_blocks(jnp.concatenate(group_a, axis=1))
     grad_context = times_back(grad_branch, back_out).astype(jnp.bfloat16)
     grad_heads = lax.all_to_all(
         token_split(grad_context), "seq", split_axis=2, concat_axis=1, tiled=True
@@ -304,71 +400,57 @@
         grad_k.reshape(rows, width),
         grad_v.reshape(rows, width),
     )
-    grad_w_query = inner_rows(flat, grad_q)
+    grad_w_query = blocked_grad(flat, grad_q, n_dp, n_seq)
     grad_b_query = jnp.sum(grad_q.astype(jnp.float32), axis=0)
-    grad_w_key = inner_rows(flat, grad_k)
-    grad_w_value = inner_rows(flat, grad_v)
+    grad_w_key = blocked_grad(flat, grad_k, n_dp, n_seq)
+    grad_w_value = blocked_grad(flat, grad_v, n_dp, n_seq)
     grad_b_value = jnp.sum(grad_v.astype(jnp.float32), axis=0)
+    group_b = [grad_w_query, grad_w_key, grad_w_value] + [
+        blocked_vector(item, n_dp, n_seq) for item in (grad_b_query, grad_b_value)
+    ]
+    summed_b = reduce_blocks(jnp.concatenate(group_b, axis=1))
     grad_inputs = (
         grad_hidden
         + times_back(grad_q, back_query)
         + times_back(grad_k, back_key)
         + times_back(grad_v, back_value)
     )
-    summed = (
-        lax.psum_scatter(grad_w_query, "dp", scatter_dimension=0, tiled=True),
-        lax.psum_scatter(grad_w_key, "dp", scatter_dimension=0, tiled=True),
-        lax.psum_scatter(grad_w_value, "dp", scatter_dimension=0, tiled=True),
-        lax.psum_scatter(grad_w_out, "dp", scatter_dimension=0, tiled=True),
-        lax.psum_scatter(grad_w_up, "dp", scatter_dimension=0, tiled=True),
-        lax.psum_scatter(grad_w_down, "dp", scatter_dimension=0, tiled=True),
-        lax.psum_scatter(grad_b_query, "dp", scatter_dimension=0, tiled=True),
-        lax.psum_scatter(grad_b_value, "dp", scatter_dimension=0, tiled=True),
-        lax.psum_scatter(grad_b_out, "dp", scatter_dimension=0, tiled=True),
-        lax.psum_scatter(grad_gain_one, "dp", scatter_dimension=0, tiled=True),
-        lax.psum_scatter(grad_shift_one, "dp", scatter_dimension=0, tiled=True),
-        lax.psum_scatter(grad_b_up, "dp", scatter_dimension=0, tiled=True),
-        lax.psum_scatter(grad_b_down, "dp", scatter_dimension=0, tiled=True),
-        lax.psum_scatter(grad_gain_two, "dp", scatter_dimension=0, tiled=True),
-        lax.psum_scatter(grad_shift_two, "dp", scatter_dimension=0, tiled=True),
-    )
-    tiled = [jnp.broadcast_to(item[:, None], (item.shape[0], n_seq)) for item in summed[6:]]
-    owned = (
-        lax.psum_scatter(summed[0], "seq", scatter_dimension=1, tiled=True),
-        lax.psum_scatter(summed[1], "seq", scatter_dimension=1, tiled=True),
-        lax.psum_scatter(summed[2], "seq", scatter_dimension=1, tiled=True),
-        lax.psum_scatter(summed[3], "seq", scatter_dimension=1, tiled=True),
-        lax.psum_scatter(summed[4], "seq", scatter_dimension=1, tiled=True),
-        lax.psum_scatter(summed[5], "seq", scatter_dimension=1, tiled=True),
-        lax.psum_scatter(tiled[0], "seq", scatter_dimension=1, tiled=True),
-        lax.psum_scatter(tiled[1], "seq", scatter_dimension=1, tiled=True),
-        lax.psum_scatter(tiled[2], "seq", scatter_dimension=1, tiled=True),
-        lax.psum_scatter(tiled[3], "seq", scatter_dimension=1, tiled=True),
-        lax.psum_scatter(tiled[4], "seq", scatter_dimension=1, tiled=True),
-        lax.psum_scatter(tiled[5], "seq", scatter_dimension=1, tiled=True),
-        lax.psum_scatter(tiled[6], "seq", scatter_dimension=1, tiled=True),
-        lax.psum_scatter(tiled[7], "seq", scatter_dimension=1, tiled=True),
-        lax.psum_scatter(tiled[8], "seq", scatter_dimension=1, tiled=True),
-    )
-    vectors = [item[:, 0] for item in owned[6:]]
+    def unpack(summed, shapes):
+        pieces, offset = [], 0
+        for shape in shapes:
+            size = 1
+            for dim in shape:
+                size *= dim
+            pieces.append(summed[offset:offset + size].reshape(shape))
+            offset += size
+        return pieces
+
+    (
+        own_w_out, own_w_up, own_w_down, own_b_out, own_gain_one, own_shift_one, own_b_up, own_b_down,
+        own_gain_two, own_shift_two,
+    ) = unpack(summed_a, [w_out.shape, w_up.shape, w_down.shape, b_out.shape, gain_one.shape, shift_one.shape,
+                          b_up.shape, b_down.shape, gain_two.shape, shift_two.shape])
+    own_w_query, own_w_key, own_w_value, own_b_query, own_b_value = unpack(
+        summed_b, [w_query.shape, w_key.shape, w_value.shape, b_query.shape, b_value.shape]
+    )
     return (
         output.reshape(seqs_here, shard_len, width),
         grad_inputs.reshape(seqs_here, shard_len, width),
-        owned[0],
-        vectors[0],
-        owned[1],
-        owned[2],
-        vectors[1],
-        owned[3],
-        vectors[2],
-        vectors[3],
-        vectors[4],
-        owned[4],
-        vectors[5],
-        owned[5],
-        vectors[6],
-        vectors[7],
-        vectors[8],
+        own_w_query,
+        own_b_query,
+        own_w_key,
+        own_w_value,
+        own_b_value,
+        own_w_out,
+        own_b_out,
+        own_gain_one,
+        own_shift_one,
+        own_w_up,
+        own_b_up,
+        own_w_down,
+        own_b_down,
+        own_gain_two,
+        own_shift_two,
     )
 
 

time: 1560 us -> 1420 us (0.910)
  waiting for transfers between devices: 536 us -> 129 us
  local copies, waits for them, and re-layouts: 272 us -> 626 us
  blocking collectives: 293 us -> 0 us
  other arithmetic: 77.8 us -> 231 us
  starting transfers between devices: 20.2 us -> 90.5 us
    reduce_scatter x7 -> x0, waiting for transfers between devices: 370 us -> none  [the longest x1 163 us: shards(): lax.psum_scatter(grad_w_up, 'dp', scatter_dimension=0, tiled=True)]
    reshape x0 -> x41, local copies, waits for them, and re-layouts: none -> 149 us  [the longest x14 49.2 us: from_blocks(): gathered.reshape(n_dp, n_seq, rows, cols).transpose(0, 2, 1, 3)]
    unnamed x23 -> x0, waiting for transfers between devices: 125 us -> none
    all_gather x7 -> x0, blocking collectives: 121 us -> none  [the longest x1 30 us: shards(): lax.all_gather(w_down, 'seq', axis=1, tiled=True)]
    ppermute x0 -> x60, waiting for transfers between devices: none -> 102 us  [the longest x30 95.6 us: reduce_blocks(): buf = keep + lax.ppermute(send, bit[0], partner(bit))]
    another operation x14 -> x68, other arithmetic: 1.35 us -> 92.8 us  [the longest x54 91.5 us: gather_blocks(): buf = jnp.stack([low, high], axis=present.index(bit))]
    all_to_all x3 -> x0, blocking collectives: 86.9 us -> none  [the longest x1 29.1 us: shards(): lax.all_to_all(head_split(grad_k), 'seq', split_axis=1, concat_axis=2, ti...]
    unnamed x3 -> x0, blocking collectives: 84.7 us -> none
  transfers between devices with their start and end apart: 23 -> 68, of which waited for: 10 -> 16; matrix products, arithmetic and copies ran while one was open for 37% -> 48% of each run, Pallas kernels for 0% -> 0%
where the time goes in v1:
time: 1420 us; the launch traced here: 1410 us
  local copies, waits for them, and re-layouts  626 us (44%)
  matrix products  303 us (21%)
  other arithmetic  231 us (16%)
  waiting for transfers between devices  129 us (9%)
  starting transfers between devices  90.5 us (6%)
  loops' own time  29.5 us (2%)
    ppermute x30, waiting for transfers between devices, reduce_blocks(): buf = keep + lax.ppermute(send, bit[0], partner(bit))  95.6 us
    another operation x54, other arithmetic, gather_blocks(): buf = jnp.stack([low, high], axis=present.index(bit))  91.5 us
    unnamed x216, local copies, waits for them, and re-layouts  77.9 us
    dot_general x16, matrix products, one_block(): jnp.einsum('qhd,khd->hqk', query_rows, keys_s, preferred_element_type=jnp...  63.3 us
    dynamic_slice x18, local copies, waits for them, and re-layouts, reduce_blocks(): keep = lax.dynamic_index_in_dim(buf, mine, axis, keepdims=False)  59 us
    reshape x14, local copies, waits for them, and re-layouts, from_blocks(): gathered.reshape(n_dp, n_seq, rows, cols).transpose(0, 2, 1, 3)  49.2 us
    dot_general x6, matrix products, blocked_grad(): g = jnp.einsum('tar,tbc->abrc', a, b, preferred_element_type=jnp.float32)  39.8 us
    dot_general x1, matrix products, shards(): jnp.dot(normed_low, full_up, preferred_element_type=jnp.float32) + vec_up  36.6 us
  transfers between devices with their start and end apart: 68, of which 16 were waited for; matrix products, arithmetic and copies ran while one was open for 48% of the time, Pallas kernels for 0%

profile of v1, /device:TPU:0, one launch (start us, length us, event | category | flops | bytes accessed | tf_op | source)
XLA Modules:
  0.0 1412.3 jit_solution(14277702153258842725)
XLA Ops:
  203.7 16.9 %all-to-all-done = bf16[4,256,4,192]{1,0,3,2:T(4,128)(2,1)} async-done(((bf16[4,256,4,192]{1,0,3,2:T(4,128)(2,1)}), bf16[4,256,4,192]{1,0,3,2:T(4,128)(2,1)}, u32[]{:S(2)}, u32[]{:S(2)}) %all-to-all-start) | async-done | bytes 1572896 | tf_op jit(solution)/shard_map/all_to_all | solution.py:252
  251.4 117.2 %while.94 = (s32[]{:T(128)}, bf16[4,1024,3,64]{1,3,2,0:T(8,128)(2,1)}, f32[4,2,3,512]{3,2,1,0:T(4,128)}, s32[4,1024]{1,0:T(4,128)}, s32[4,1024]{1,0:T(4,128)S(1)...) while((s32[]{:T(128)}, ...), condition=%wide.region_8.9_spmd, body=%wide.region_2.8_spmd.sunk | while | flops 424790912 | bytes 34466940 | solution.py:286
  255.2 22.9 %while.97 = (s32[]{:T(128)}, bf16[2,512,3,64]{1,3,2,0:T(8,128)(2,1)S(1)}, f32[2,3,512]{2,1,0:T(4,128)S(1)}, s32[2]{0:T(128)S(1)}, s32[1024]{0:T(1024)S(1)}, /*in...) while((s32[]{:T(128)}, ...), condition=%wide.region_7.7_spmd, body=%wide.region_3.6_spmd.sunk | while | flops 424790912 | bytes 29693712 | solution.py:283
  284.5 22.9 %while.97 = (s32[]{:T(128)}, bf16[2,512,3,64]{1,3,2,0:T(8,128)(2,1)S(1)}, f32[2,3,512]{2,1,0:T(4,128)S(1)}, s32[2]{0:T(128)S(1)}, s32[1024]{0:T(1024)S(1)}, /*in...) while((s32[]{:T(128)}, ...), condition=%wide.region_7.7_spmd, body=%wide.region_3.6_spmd.sunk | while | flops 424790912 | bytes 29693712 | solution.py:283
  313.7 22.9 %while.97 = (s32[]{:T(128)}, bf16[2,512,3,64]{1,3,2,0:T(8,128)(2,1)S(1)}, f32[2,3,512]{2,1,0:T(4,128)S(1)}, s32[2]{0:T(128)S(1)}, s32[1024]{0:T(1024)S(1)}, /*in...) while((s32[]{:T(128)}, ...), condition=%wide.region_7.7_spmd, body=%wide.region_3.6_spmd.sunk | while | flops 424790912 | bytes 29693712 | solution.py:283
  342.9 22.9 %while.97 = (s32[]{:T(128)}, bf16[2,512,3,64]{1,3,2,0:T(8,128)(2,1)S(1)}, f32[2,3,512]{2,1,0:T(4,128)S(1)}, s32[2]{0:T(128)S(1)}, s32[1024]{0:T(1024)S(1)}, /*in...) while((s32[]{:T(128)}, ...), condition=%wide.region_7.7_spmd, body=%wide.region_3.6_spmd.sunk | while | flops 424790912 | bytes 29693712 | solution.py:283
  465.5 9.6 reshape.1006
  475.1 8.8 copy.423
  499.5 36.6 %multiply_convert_fusion.1 = (bf16[1024,3072]{1,0:T(8,128)(2,1)S(1)}, f32[1024,3072]{1,0:T(8,128)}, f32[1024,3072]{1,0:T(8,128)}) fusion(f32[3072]{0:T(1024)S(1)} %bitcast.685, bf16[1024,768]{0,1:T(8,128)(2,1)S(1)} %fusion.62, bf16[768,3072]{1,0:T(8,128)(2,1)S(1)} %bitcast.641), kind=kOutput, calls=%fused_computation.113 | convolution fusion | flops 5039456256 | bytes 37761024 | tf_op jit(solution)/shard_map/dot_general | solution.py:304
  550.4 17.2 %convert_reduce_fusion = (f32[3072]{0:T(1024)}, bf16[1024,3072]{1,0:T(8,128)(2,1)}) fusion(f32[1024,3072]{1,0:T(8,128)} %get-tuple-element.1101, bf16[1024,768]{0,1:T(8,128)(2,1)S(1)} %get-tuple-element.1093, bf16[3072,768]{0,1:T(8,128)(2,1)S(1)} %bitcast.645, f32[1024,3072]{1,0:T(8,128)} %get-tuple-element.1255, f32[3072]{0:T(1024)S(1)} %bitcast.686), kind=kOutput, calls=%fused_computation.111 | convolution fusion | flops 4885312512 | bytes 37773312 | tf_op jit(solution)/shard_map/dot_general | solution.py:60
  567.5 12.3 reshape.1031
  579.8 11.8 multiply_reduce_fusion.2
  595.5 10.3 fusion.58
  610.6 9.0 copy.537
  619.6 10.2 fusion.61
  629.7 11.5 copy.457
  641.3 10.9 reshape.1037
  686.1 8.4 pad_maximum_fusion
  715.4 290.1 %while.96 = (s32[]{:T(128)}, bf16[4,1024,3,64]{1,3,2,0:T(8,128)(2,1)}, bf16[4,1024,3,64]{1,3,2,0:T(8,128)(2,1)}, bf16[4,1024,3,64]{1,3,2,0:T(8,128)(2,1)}, s32[4...) while((s32[]{:T(128)}, ...), condition=%wide.region_22.23_spmd, body=%wide.region_17.22_spmd.sunk | while | flops 1031719808 | bytes 148861008 | solution.py:386
  723.4 59.3 %while.98 = (s32[]{:T(128)}, f32[1024,3,64]{0,2,1:T(8,128)}, f32[1024,3,64]{0,2,1:T(8,128)}, bf16[2,512,3,64]{1,3,2,0:T(8,128)(2,1)}, s32[2]{0:T(128)S(1)}, /*in...) while((s32[]{:T(128)}, f32[1024,3,64]{0,2,1:T(8,128)}, ...), condition=%wide.region_21.21_spmd.clone, body=%wide.region_18.20_spmd.clone.sunk | while | flops 1031326592 | bytes 140946064 | solution.py:376
  795.8 59.3 %while.98 = (s32[]{:T(128)}, f32[1024,3,64]{0,2,1:T(8,128)}, f32[1024,3,64]{0,2,1:T(8,128)}, bf16[2,512,3,64]{1,3,2,0:T(8,128)(2,1)}, s32[2]{0:T(128)S(1)}, /*in...) while((s32[]{:T(128)}, f32[1024,3,64]{0,2,1:T(8,128)}, ...), condition=%wide.region_21.21_spmd.clone, body=%wide.region_18.20_spmd.clone.sunk | while | flops 1031326592 | bytes 140946064 | solution.py:376
  868.3 59.3 %while.98 = (s32[]{:T(128)}, f32[1024,3,64]{0,2,1:T(8,128)}, f32[1024,3,64]{0,2,1:T(8,128)}, bf16[2,512,3,64]{1,3,2,0:T(8,128)(2,1)}, s32[2]{0:T(128)S(1)}, /*in...) while((s32[]{:T(128)}, f32[1024,3,64]{0,2,1:T(8,128)}, ...), condition=%wide.region_21.21_spmd.clone, body=%wide.region_18.20_spmd.clone.sunk | while | flops 1031326592 | bytes 140946064 | solution.py:376
  940.7 59.3 %while.98 = (s32[]{:T(128)}, f32[1024,3,64]{0,2,1:T(8,128)}, f32[1024,3,64]{0,2,1:T(8,128)}, bf16[2,512,3,64]{1,3,2,0:T(8,128)(2,1)}, s32[2]{0:T(128)S(1)}, /*in...) while((s32[]{:T(128)}, f32[1024,3,64]{0,2,1:T(8,128)}, ...), condition=%wide.region_21.21_spmd.clone, body=%wide.region_18.20_spmd.clone.sunk | while | flops 1031326592 | bytes 140946064 | solution.py:376
  1013.7 9.9 constant_dynamic-slice_fusion.11
  1046.6 8.4 reshape.1045
  1063.6 9.9 constant_dynamic-slice_fusion.17
  1077.6 8.5 reshape.1034
  1094.0 9.9 constant_dynamic-slice_fusion.25
  1263.6 30.6 %collective-permute-done.32 = f32[2,2,18560]{2,1,0:T(2,128)S(1)} collective-permute-done((f32[2,2,18560]{2,1,0:T(2,128)S(1)}, f32[2,2,18560]{2,1,0:T(2,128)S(1)}, u32[]{:S(2)}, u32[]{:S(2)}) %collective-permute-start.32) | collective-permute-done | bytes 296992 | tf_op jit(solution)/shard_map/ppermute | solution.py:141
  1329.6 28.4 %collective-permute-done.46 = f32[2,2,2,55680]{3,2,1,0:T(2,128)} collective-permute-done((f32[2,2,2,55680]{3,2,1,0:T(2,128)}, f32[2,2,2,55680]{3,2,1,0:T(2,128)}, u32[]{:S(2)}, u32[]{:S(2)}) %collective-permute-start.46) | collective-permute-done | bytes 1781792 | tf_op jit(solution)/shard_map/ppermute | solution.py:141
  1365.2 10.9 collective-permute-done.52
  1397.5 9.6 collective-permute-done.54
  (1272 shorter events, 1080.2 us)
Async XLA Ops:
  4.9 40.5 %collective-permute-start.25 = (bf16[55680]{0:T(1024)(128)(2,1)}, bf16[55680]{0:T(1024)(128)(2,1)}, u32[]{:S(2)}, u32[]{:S(2)}) collective-permute-start(bf16[55680]{0:T(1024)(128)(2,1)} %get-tuple-element.1238), channel_id=1, source_target_pairs={{0,4},{1,5},{2,6},{3,7},{4,0},{5,1},{6,2},{7,3},{8,12},{9,13},{10,... | collective-permute-start | bytes 334088 | tf_op jit(solution)/shard_map/ppermute | solution.py:117
  8.9 39.7 %collective-permute-start.15 = (bf16[55680]{0:T(1024)(128)(2,1)}, bf16[55680]{0:T(1024)(128)(2,1)}, u32[]{:S(2)}, u32[]{:S(2)}) collective-permute-start(bf16[55680]{0:T(1024)(128)(2,1)} %get-tuple-element.1239), channel_id=1, source_target_pairs={{0,4},{1,5},{2,6},{3,7},{4,0},{5,1},{6,2},{7,3},{8,12},{9,13},{10,... | collective-permute-start | bytes 334088 | tf_op jit(solution)/shard_map/ppermute | solution.py:117
  15.6 35.4 %collective-permute-start.20 = (bf16[55680]{0:T(1024)(128)(2,1)}, bf16[55680]{0:T(1024)(128)(2,1)}, u32[]{:S(2)}, u32[]{:S(2)}) collective-permute-start(bf16[55680]{0:T(1024)(128)(2,1)} %slice.340), channel_id=1, source_target_pairs={{0,4},{1,5},{2,6},{3,7},{4,0},{5,1},{6,2},{7,3},{8,12},{9,13},{10,... | collective-permute-start | bytes 334088 | tf_op jit(solution)/shard_map/ppermute | solution.py:117
  84.5 28.4 %collective-permute-start.9 = (bf16[2,2,2,2,18560]{4,0,1,2,3:T(2,128)(2,1)}, bf16[2,2,2,2,18560]{4,0,1,2,3:T(2,128)(2,1)}, u32[]{:S(2)}, u32[]{:S(2)}) collective-permute-start(bf16[2,2,2,2,18560]{4,0,1,2,3:T(2,128)(2,1)} %pad_maximum_fusion.21), channel_id=1, source_target_pairs={{0,8},{8,0},{16,24},{24,16},{1,9},{9,1},{17,25},{25,17},{2,10},{10... | collective-permute-start | bytes 1781768 | tf_op jit(solution)/shard_map/ppermute | solution.py:117
  87.8 92.5 %collective-permute-start.28 = (bf16[2,2,2,55680]{3,0,1,2:T(2,128)(2,1)}, bf16[2,2,2,55680]{3,0,1,2:T(2,128)(2,1)}, u32[]{:S(2)}, u32[]{:S(2)}) collective-permute-start(bf16[2,2,2,55680]{3,0,1,2:T(2,128)(2,1)} %pad_maximum_fusion.19), channel_id=1, source_target_pairs={{0,1},{1,0},{2,3},{3,2},{4,5},{5,4},{6,7},{7,6},{8,9},{9,8},{10,11... | collective-permute-start | bytes 2672648 | tf_op jit(solution)/shard_map/ppermute | solution.py:117
  91.6 96.3 %collective-permute-start.18 = (bf16[2,2,2,55680]{3,0,1,2:T(2,128)(2,1)}, bf16[2,2,2,55680]{3,0,1,2:T(2,128)(2,1)}, u32[]{:S(2)}, u32[]{:S(2)}) collective-permute-start(bf16[2,2,2,55680]{3,0,1,2:T(2,128)(2,1)} %pad_maximum_fusion.17), channel_id=1, source_target_pairs={{0,16},{8,24},{16,0},{24,8},{1,17},{9,25},{17,1},{25,9},{2,18},{10... | collective-permute-start | bytes 2672648 | tf_op jit(solution)/shard_map/ppermute | solution.py:117
  95.8 104.7 %collective-permute-start.23 = (bf16[2,2,2,55680]{3,0,1,2:T(2,128)(2,1)}, bf16[2,2,2,55680]{3,0,1,2:T(2,128)(2,1)}, u32[]{:S(2)}, u32[]{:S(2)}) collective-permute-start(bf16[2,2,2,55680]{3,0,1,2:T(2,128)(2,1)} %pad_maximum_fusion.18), channel_id=1, source_target_pairs={{0,2},{1,3},{2,0},{3,1},{4,6},{5,7},{6,4},{7,5},{8,10},{9,11},{10,... | collective-permute-start | bytes 2672648 | tf_op jit(solution)/shard_map/ppermute | solution.py:117
  139.9 56.2 %all-to-all-start.2 = ((bf16[4,256,4,192]{1,0,3,2:T(4,128)(2,1)}), bf16[4,256,4,192]{1,0,3,2:T(4,128)(2,1)S(1)}, u32[]{:S(2)}, u32[]{:S(2)}) async-start(bf16[4,256,4,192]{1,0,3,2:T(4,128)(2,1)} %reshape.988), calls=%async_computation.2 | async-start | bytes 3145728 | tf_op jit(solution)/shard_map/all_to_all | solution.py:254
  187.4 190.3 %collective-permute-start.29 = (bf16[2,2,2,2,55680]{4,0,1,2,3:T(2,128)(2,1)}, bf16[2,2,2,2,55680]{4,0,1,2,3:T(2,128)(2,1)}, u32[]{:S(2)}, u32[]{:S(2)}) collective-permute-start(bf16[2,2,2,2,55680]{4,0,1,2,3:T(2,128)(2,1)} %pad_maximum_fusion.11), channel_id=1, source_target_pairs={{0,8},{8,0},{16,24},{24,16},{1,9},{9,1},{17,25},{25,17},{2,10},{10... | collective-permute-start | bytes 5345288 | tf_op jit(solution)/shard_map/ppermute | solution.py:117
  196.0 192.1 %collective-permute-start.19 = (bf16[2,2,2,2,55680]{4,0,1,2,3:T(2,128)(2,1)}, bf16[2,2,2,2,55680]{4,0,1,2,3:T(2,128)(2,1)}, u32[]{:S(2)}, u32[]{:S(2)}) collective-permute-start(bf16[2,2,2,2,55680]{4,0,1,2,3:T(2,128)(2,1)} %pad_maximum_fusion.9), channel_id=1, source_target_pairs={{0,8},{8,0},{16,24},{24,16},{1,9},{9,1},{17,25},{25,17},{2,10},{10... | collective-permute-start | bytes 5345288 | tf_op jit(solution)/shard_map/ppermute | solution.py:117
  196.0 24.5 %all-to-all-start = ((bf16[4,256,4,192]{1,0,3,2:T(4,128)(2,1)}), bf16[4,256,4,192]{1,0,3,2:T(4,128)(2,1)}, u32[]{:S(2)}, u32[]{:S(2)}) async-start(bf16[4,256,4,192]{1,0,3,2:T(4,128)(2,1)} %reshape.978), calls=%async_computation | async-start | bytes 3145728 | tf_op jit(solution)/shard_map/all_to_all | solution.py:252
  228.7 193.3 %collective-permute-start.24 = (bf16[2,2,2,2,55680]{4,0,1,2,3:T(2,128)(2,1)}, bf16[2,2,2,2,55680]{4,0,1,2,3:T(2,128)(2,1)}, u32[]{:S(2)}, u32[]{:S(2)}) collective-permute-start(bf16[2,2,2,2,55680]{4,0,1,2,3:T(2,128)(2,1)} %pad_maximum_fusion.10), channel_id=1, source_target_pairs={{0,8},{8,0},{16,24},{24,16},{1,9},{9,1},{17,25},{25,17},{2,10},{10... | collective-permute-start | bytes 5345288 | tf_op jit(solution)/shard_map/ppermute | solution.py:117
  372.8 118.2 %all-to-all-start.3 = ((bf16[4,1024,1,192]{3,0,2,1:T(4,128)(2,1)}), bf16[4,1024,1,192]{3,0,2,1:T(4,128)(2,1)}, u32[]{:S(2)}, u32[]{:S(2)}) async-start(bf16[4,1024,1,192]{3,0,2,1:T(4,128)(2,1)} %copy.405), calls=%async_computation.3 | async-start | bytes 4194304 | tf_op jit(solution)/shard_map/all_to_all | solution.py:289
  1009.6 49.5 %all-to-all-start.5 = ((bf16[4,1024,1,192]{3,0,2,1:T(4,128)(2,1)}), bf16[4,1024,1,192]{3,0,2,1:T(4,128)(2,1)S(1)}, u32[]{:S(2)}, u32[]{:S(2)}) async-start(bf16[4,1024,1,192]{3,0,2,1:T(4,128)(2,1)} %copy.431), calls=%async_computation.5 | async-start | bytes 4194304 | tf_op jit(solution)/shard_map/all_to_all | solution.py:394
  1027.3 209.5 %collective-permute-start.55 = (f32[2,2,2,2,55680]{4,3,2,1,0:T(2,128)}, f32[2,2,2,2,55680]{4,3,2,1,0:T(2,128)}, u32[]{:S(2)}, u32[]{:S(2)}) collective-permute-start(f32[2,2,2,2,55680]{4,3,2,1,0:T(2,128)} %bitcast.508), channel_id=1, source_target_pairs={{0,8},{8,0},{16,24},{24,16},{1,9},{9,1},{17,25},{25,17},{2,10},{10... | collective-permute-start | bytes 10690568 | tf_op jit(solution)/shard_map/ppermute | solution.py:141
  1059.2 30.2 %all-to-all-start.6 = ((bf16[4,1024,1,192]{3,0,2,1:T(4,128)(2,1)}), bf16[4,1024,1,192]{3,0,2,1:T(4,128)(2,1)}, u32[]{:S(2)}, u32[]{:S(2)}) async-start(bf16[4,1024,1,192]{3,0,2,1:T(4,128)(2,1)} %copy.435), calls=%async_computation.6 | async-start | bytes 4194304 | tf_op jit(solution)/shard_map/all_to_all | solution.py:395
  1077.1 167.1 %collective-permute-start.50 = (f32[2,2,2,2,55680]{4,3,2,1,0:T(2,128)}, f32[2,2,2,2,55680]{4,3,2,1,0:T(2,128)}, u32[]{:S(2)}, u32[]{:S(2)}) collective-permute-start(f32[2,2,2,2,55680]{4,3,2,1,0:T(2,128)} %bitcast.509), channel_id=1, source_target_pairs={{0,8},{8,0},{16,24},{24,16},{1,9},{9,1},{17,25},{25,17},{2,10},{10... | collective-permute-start | bytes 10690568 | tf_op jit(solution)/shard_map/ppermute | solution.py:141
  1089.4 64.5 %all-to-all-start.7 = ((bf16[4,1024,1,192]{3,0,2,1:T(4,128)(2,1)}), bf16[4,1024,1,192]{3,0,2,1:T(4,128)(2,1)}, u32[]{:S(2)}, u32[]{:S(2)}) async-start(bf16[4,1024,1,192]{3,0,2,1:T(4,128)(2,1)} %copy.439), calls=%async_computation.7 | async-start | bytes 4194304 | tf_op jit(solution)/shard_map/all_to_all | solution.py:396
  1107.5 145.2 %collective-permute-start.45 = (f32[2,2,2,2,55680]{4,3,2,1,0:T(2,128)}, f32[2,2,2,2,55680]{4,3,2,1,0:T(2,128)}, u32[]{:S(2)}, u32[]{:S(2)}) collective-permute-start(f32[2,2,2,2,55680]{4,3,2,1,0:T(2,128)} %bitcast.510), channel_id=1, source_target_pairs={{0,8},{8,0},{16,24},{24,16},{1,9},{9,1},{17,25},{25,17},{2,10},{10... | collective-permute-start | bytes 10690568 | tf_op jit(solution)/shard_map/ppermute | solution.py:141
  1189.7 36.4 %collective-permute-start.30 = (f32[2,2,2,2,18560]{4,3,2,1,0:T(2,128)}, f32[2,2,2,2,18560]{4,3,2,1,0:T(2,128)}, u32[]{:S(2)}, u32[]{:S(2)}) collective-permute-start(f32[2,2,2,2,18560]{4,3,2,1,0:T(2,128)} %bitcast.514), channel_id=1, source_target_pairs={{0,8},{8,0},{16,24},{24,16},{1,9},{9,1},{17,25},{25,17},{2,10},{10... | collective-permute-start | bytes 3563528 | tf_op jit(solution)/shard_map/ppermute | solution.py:141
  1201.2 28.9 %collective-permute-start.40 = (f32[2,2,2,2,18560]{4,3,2,1,0:T(2,128)}, f32[2,2,2,2,18560]{4,3,2,1,0:T(2,128)}, u32[]{:S(2)}, u32[]{:S(2)}) collective-permute-start(f32[2,2,2,2,18560]{4,3,2,1,0:T(2,128)} %bitcast.512), channel_id=1, source_target_pairs={{0,8},{8,0},{16,24},{24,16},{1,9},{9,1},{17,25},{25,17},{2,10},{10... | collective-permute-start | bytes 3563528 | tf_op jit(solution)/shard_map/ppermute | solution.py:141
  1230.1 29.7 %collective-permute-start.31 = (f32[2,2,2,18560]{3,2,1,0:T(2,128)S(1)}, f32[2,2,2,18560]{3,2,1,0:T(2,128)S(1)}, u32[]{:S(2)}, u32[]{:S(2)}) collective-permute-start(f32[2,2,2,18560]{3,2,1,0:T(2,128)S(1)} %bitcast.659), channel_id=1, source_target_pairs={{0,16},{8,24},{16,0},{24,8},{1,17},{9,25},{17,1},{25,9},{2,18},{10... | collective-permute-start | bytes 1781768 | tf_op jit(solution)/shard_map/ppermute | solution.py:141
  1234.4 27.2 %collective-permute-start.41 = (f32[2,2,2,18560]{3,2,1,0:T(2,128)S(1)}, f32[2,2,2,18560]{3,2,1,0:T(2,128)S(1)}, u32[]{:S(2)}, u32[]{:S(2)}) collective-permute-start(f32[2,2,2,18560]{3,2,1,0:T(2,128)S(1)} %dynamic-slice_bitcast_fusion.12), channel_id=1, source_target_pairs={{0,1},{1,0},{2,3},{3,2},{4,5},{5,4},{6,7},{7,6},{8,9},{9,8},{10,11... | collective-permute-start | bytes 1781768 | tf_op jit(solution)/shard_map/ppermute | solution.py:141
  1236.8 25.7 %collective-permute-start.36 = (f32[2,2,2,18560]{3,2,1,0:T(2,128)S(1)}, f32[2,2,2,18560]{3,2,1,0:T(2,128)S(1)}, u32[]{:S(2)}, u32[]{:S(2)}) collective-permute-start(f32[2,2,2,18560]{3,2,1,0:T(2,128)S(1)} %dynamic-slice_bitcast_fusion.13), channel_id=1, source_target_pairs={{0,2},{1,3},{2,0},{3,1},{4,6},{5,7},{6,4},{7,5},{8,10},{9,11},{10,... | collective-permute-start | bytes 1781768 | tf_op jit(solution)/shard_map/ppermute | solution.py:141
  1244.3 74.6 %collective-permute-start.56 = (f32[2,2,2,55680]{3,2,1,0:T(2,128)}, f32[2,2,2,55680]{3,2,1,0:T(2,128)}, u32[]{:S(2)}, u32[]{:S(2)}) collective-permute-start(f32[2,2,2,55680]{3,2,1,0:T(2,128)} %dynamic-slice_bitcast_fusion.9), channel_id=1, source_target_pairs={{0,1},{1,0},{2,3},{3,2},{4,5},{5,4},{6,7},{7,6},{8,9},{9,8},{10,11... | collective-permute-start | bytes 5345288 | tf_op jit(solution)/shard_map/ppermute | solution.py:141
  1252.6 71.0 %collective-permute-start.51 = (f32[2,2,2,55680]{3,2,1,0:T(2,128)}, f32[2,2,2,55680]{3,2,1,0:T(2,128)}, u32[]{:S(2)}, u32[]{:S(2)}) collective-permute-start(f32[2,2,2,55680]{3,2,1,0:T(2,128)} %dynamic-slice_bitcast_fusion.10), channel_id=1, source_target_pairs={{0,2},{1,3},{2,0},{3,1},{4,6},{5,7},{6,4},{7,5},{8,10},{9,11},{10,... | collective-permute-start | bytes 5345288 | tf_op jit(solution)/shard_map/ppermute | solution.py:141
  1261.0 33.2 %collective-permute-start.32 = (f32[2,2,18560]{2,1,0:T(2,128)S(1)}, f32[2,2,18560]{2,1,0:T(2,128)S(1)}, u32[]{:S(2)}, u32[]{:S(2)}) collective-permute-start(f32[2,2,18560]{2,1,0:T(2,128)S(1)} %bitcast.664), channel_id=1, source_target_pairs={{0,1},{1,0},{2,3},{3,2},{4,5},{5,4},{6,7},{7,6},{8,9},{9,8},{10,11... | collective-permute-start | bytes 890888 | tf_op jit(solution)/shard_map/ppermute | solution.py:141
  1261.9 38.9 %collective-permute-start.42 = (f32[2,2,18560]{2,1,0:T(2,128)S(1)}, f32[2,2,18560]{2,1,0:T(2,128)S(1)}, u32[]{:S(2)}, u32[]{:S(2)}) collective-permute-start(f32[2,2,18560]{2,1,0:T(2,128)S(1)} %dynamic-slice_bitcast_fusion.14), channel_id=1, source_target_pairs={{0,2},{1,3},{2,0},{3,1},{4,6},{5,7},{6,4},{7,5},{8,10},{9,11},{10,... | collective-permute-start | bytes 890888 | tf_op jit(solution)/shard_map/ppermute | solution.py:141
  1263.5 38.1 %collective-permute-start.37 = (f32[2,2,18560]{2,1,0:T(2,128)S(1)}, f32[2,2,18560]{2,1,0:T(2,128)S(1)}, u32[]{:S(2)}, u32[]{:S(2)}) collective-permute-start(f32[2,2,18560]{2,1,0:T(2,128)S(1)} %bitcast.663), channel_id=1, source_target_pairs={{0,16},{8,24},{16,0},{24,8},{1,17},{9,25},{17,1},{25,9},{2,18},{10... | collective-permute-start | bytes 890888 | tf_op jit(solution)/shard_map/ppermute | solution.py:141
  1315.9 42.1 %collective-permute-start.46 = (f32[2,2,2,55680]{3,2,1,0:T(2,128)}, f32[2,2,2,55680]{3,2,1,0:T(2,128)}, u32[]{:S(2)}, u32[]{:S(2)}) collective-permute-start(f32[2,2,2,55680]{3,2,1,0:T(2,128)} %bitcast.511), channel_id=1, source_target_pairs={{0,16},{8,24},{16,0},{24,8},{1,17},{9,25},{17,1},{25,9},{2,18},{10... | collective-permute-start | bytes 5345288 | tf_op jit(solution)/shard_map/ppermute | solution.py:141
  1322.2 41.0 %collective-permute-start.57 = (f32[2,2,55680]{2,1,0:T(2,128)S(1)}, f32[2,2,55680]{2,1,0:T(2,128)S(1)}, u32[]{:S(2)}, u32[]{:S(2)}) collective-permute-start(f32[2,2,55680]{2,1,0:T(2,128)S(1)} %dynamic-slice_bitcast_fusion.11), channel_id=1, source_target_pairs={{0,2},{1,3},{2,0},{3,1},{4,6},{5,7},{6,4},{7,5},{8,10},{9,11},{10,... | collective-permute-start | bytes 2672648 | tf_op jit(solution)/shard_map/ppermute | solution.py:141
  1328.5 47.7 %collective-permute-start.52 = (f32[2,2,55680]{2,1,0:T(2,128)S(1)}, f32[2,2,55680]{2,1,0:T(2,128)S(1)}, u32[]{:S(2)}, u32[]{:S(2)}) collective-permute-start(f32[2,2,55680]{2,1,0:T(2,128)S(1)} %bitcast.658), channel_id=1, source_target_pairs={{0,16},{8,24},{16,0},{24,8},{1,17},{9,25},{17,1},{25,9},{2,18},{10... | collective-permute-start | bytes 2672648 | tf_op jit(solution)/shard_map/ppermute | solution.py:141
  (206 other events, 1748.8 us)

commit v2 on v1

--- a/solution.py
+++ b/solution.py
@@ -69,6 +69,12 @@
     return [(axis, b) for b in range(bits)]
 
 
+def canonical_bits():
+    return [("dp", b) for b in reversed(range(len(axis_bits("dp"))))] + [
+        ("seq", b) for b in reversed(range(len(axis_bits("seq"))))
+    ]
+
+
 def bit_orders(n_parts):
     seq_bits, dp_bits = axis_bits("seq"), axis_bits("dp")
     first, last = seq_bits[:1], dp_bits[-1:]
@@ -80,12 +86,6 @@
     return orders
 
 
-def layout_bits():
-    return [("dp", b) for b in reversed(range(len(axis_bits("dp"))))] + [
-        ("seq", b) for b in reversed(range(len(axis_bits("seq"))))
-    ]
-
-
 def my_bit(bit):
     axis, b = bit
     return (lax.axis_index(axis) >> b) & 1
@@ -93,78 +93,142 @@
 
 def partner(bit):
     axis, b = bit
-    size = lax.axis_size(axis)
-    return [(i, i ^ (1 << b)) for i in range(size)]
-
-
-def split_parts(flat, n_parts):
-    width = flat.shape[-1]
-    step = -(-width // (n_parts * 128)) * 128
-    pad = step * n_parts - width
+    return [(i, i ^ (1 << b)) for i in range(lax.axis_size(axis))]
+
+
+N_PARTS = 3
+LANES = 128
+
+
+def to_order(blocked, order):
+    canon = canonical_bits()
+    rest = blocked.shape[1:]
+    x = blocked.reshape([2] * len(canon) + list(rest))
+    perm = [canon.index(bit) for bit in order] + list(range(len(canon), len(canon) + len(rest)))
+    return x.transpose(perm).reshape(blocked.shape)
+
+
+def from_order(blocked, order):
+    canon = canonical_bits()
+    rest = blocked.shape[1:]
+    x = blocked.reshape([2] * len(canon) + list(rest))
+    perm = [order.index(bit) for bit in canon] + list(range(len(canon), len(canon) + len(rest)))
+    return x.transpose(perm).reshape(blocked.shape)
+
+
+def lane_rows(flat_blocks):
+    n, width = flat_blocks.shape
+    rows = -(-width // LANES)
+    pad = rows * LANES - width
     if pad:
-        flat = jnp.concatenate([flat, jnp.zeros(flat.shape[:-1] + (pad,), flat.dtype)], axis=-1)
-    return [flat[..., i * step:(i + 1) * step] for i in range(n_parts)], width
-
-
-def gather_blocks(flat, n_parts=3):
-    order_all = layout_bits()
-    parts, width = split_parts(flat, n_parts)
+        flat_blocks = jnp.concatenate([flat_blocks, jnp.zeros((n, pad), flat_blocks.dtype)], axis=1)
+    return flat_blocks.reshape(n, rows, LANES)
+
+
+def gather_parts(parts, orders):
     out = []
-    for part, order in zip(parts, bit_orders(n_parts)):
-        present = []
-        buf = part
+    for buf, order in zip(parts, orders):
+        buf = buf[None]
         for bit in reversed(order):
             got = lax.ppermute(buf, bit[0], partner(bit))
             mine = my_bit(bit) == 0
-            low = jnp.where(mine, buf, got)
-            high = jnp.where(mine, got, buf)
-            present.append(bit)
-            present.sort(key=order_all.index)
-            buf = jnp.stack([low, high], axis=present.index(bit))
-        out.append(buf.reshape(-1, buf.shape[-1]))
-    return jnp.concatenate(out, axis=-1)[:, :width]
-
-
-def reduce_blocks(blocked, n_parts=3):
-    order_all = layout_bits()
-    shape = [2] * len(order_all)
-    parts, width = split_parts(blocked, n_parts)
+            buf = jnp.concatenate([jnp.where(mine, buf, got), jnp.where(mine, got, buf)], axis=0)
+        out.append(buf)
+    return out
+
+
+def reduce_parts(parts, orders):
     out = []
-    for part, order in zip(parts, bit_orders(n_parts)):
-        present = list(order_all)
-        buf = part.reshape(shape + [part.shape[-1]])
+    for buf, order in zip(parts, orders):
         for bit in order:
-            axis = present.index(bit)
+            half = buf.reshape((2, buf.shape[0] // 2) + buf.shape[1:])
             mine = my_bit(bit)
-            keep = lax.dynamic_index_in_dim(buf, mine, axis, keepdims=False)
-            send = lax.dynamic_index_in_dim(buf, 1 - mine, axis, keepdims=False)
+            keep = lax.dynamic_index_in_dim(half, mine, 0, keepdims=False)
+            send = lax.dynamic_index_in_dim(half, 1 - mine, 0, keepdims=False)
             buf = keep + lax.ppermute(send, bit[0], partner(bit))
-            present.remove(bit)
-        out.append(buf)
-    return jnp.concatenate(out, axis=-1)[:width]
-
-
-def to_blocks(matrix_block):
-    return matrix_block.reshape(-1)
-
-
-def from_blocks(gathered, n_dp, n_seq, rows, cols):
-    return (
-        gathered.reshape(n_dp, n_seq, rows, cols).transpose(0, 2, 1, 3).reshape(n_dp * rows, n_seq * cols)
-    )
+        out.append(buf[0])
+    return out
+
+
+def gather_weights(matrices, vectors):
+    n_dp, n_seq = lax.axis_size("dp"), lax.axis_size("seq")
+    orders = bit_orders(N_PARTS)
+    parts, layout = [], []
+    for part in range(N_PARTS):
+        items = []
+        for m in matrices:
+            third = m.shape[0] // N_PARTS
+            items.append(m[part * third:(part + 1) * third].reshape(-1))
+        if part == 0:
+            items += [v.reshape(-1) for v in vectors]
+        sizes = [item.size for item in items]
+        parts.append(lane_rows(jnp.concatenate(items)[None])[0])
+        layout.append(sizes)
+    got = gather_parts(parts, orders)
+    canon = []
+    for buf, order, sizes in zip(got, orders, layout):
+        flat = from_order(buf, order).reshape(n_dp * n_seq, -1)
+        pieces, offset = [], 0
+        for size in sizes:
+            pieces.append(flat[:, offset:offset + size])
+            offset += size
+        canon.append(pieces)
+    full = []
+    for index, m in enumerate(matrices):
+        third = m.shape[0] // N_PARTS
+        stacked = jnp.stack(
+            [canon[part][index].reshape(n_dp, n_seq, third, m.shape[1]) for part in range(N_PARTS)], axis=2
+        )
+        full.append(stacked.transpose(0, 2, 3, 1, 4).reshape(n_dp * m.shape[0], n_seq * m.shape[1]))
+    vecs = []
+    for index, v in enumerate(vectors):
+        piece = canon[0][len(matrices) + index]
+        vecs.append(piece.reshape(n_dp, n_seq, v.size)[:, 0].reshape(-1))
+    return full, vecs
 
 
 def blocked_grad(left, right, n_dp, n_seq):
     tokens = left.shape[0]
     a = left.reshape(tokens, n_dp, left.shape[1] // n_dp)
     b = right.reshape(tokens, n_seq, right.shape[1] // n_seq)
-    g = jnp.einsum("tar,tbc->abrc", a, b, preferred_element_type=jnp.float32)
-    return g.reshape(n_dp * n_seq, -1)
-
-
-def blocked_vector(vector, n_dp, n_seq):
-    v = vector.reshape(n_dp, 1, -1)
-    return jnp.broadcast_to(v, (n_dp, n_seq, v.shape[-1])).reshape(n_dp * n_seq, -1)
+    return jnp.einsum("tar,tbc->abrc", a, b, preferred_element_type=jnp.float32)
+
+
+def reduce_grads(matrices, vectors):
+    n_dp, n_seq = lax.axis_size("dp"), lax.axis_size("seq")
+    orders = bit_orders(N_PARTS)
+    parts, layout = [], []
+    for part in range(N_PARTS):
+        items = []
+        for m in matrices:
+            third = m.shape[2] // N_PARTS
+            items.append(m[:, :, part * third:(part + 1) * third].reshape(n_dp * n_seq, -1))
+        if part == 0:
+            for v in vectors:
+                v = v.reshape(n_dp, 1, -1)
+                items.append(jnp.broadcast_to(v, (n_dp, n_seq, v.shape[-1])).reshape(n_dp * n_seq, -1))
+        sizes = [item.shape[1] for item in items]
+        parts.append(to_order(lane_rows(jnp.concatenate(items, axis=1)), orders[part]))
+        layout.append(sizes)
+    summed = reduce_parts(parts, orders)
+    pieces_by_part = []
+    for buf, sizes in zip(summed, layout):
+        flat = buf.reshape(-1)
+        pieces, offset = [], 0
+        for size in sizes:
+            pieces.append(flat[offset:offset + size])
+            offset += size
+        pieces_by_part.append(pieces)
+    own = []
+    for index, m in enumerate(matrices):
+        third = m.shape[2] // N_PARTS
+        own.append(
+            jnp.concatenate(
+                [pieces_by_part[part][index].reshape(third, m.shape[3]) for part in range(N_PARTS)], axis=0
+            )
+        )
+    vecs = [pieces_by_part[0][len(matrices) + index] for index in range(len(vectors))]
+    return own, vecs
 
 
 def shards(
@@ -198,27 +262,12 @@
     n_blocks = seq_len // QB
     scale = HD ** (-0.5)
     n_dp = lax.axis_size("dp")
-    first_group = [w_query, w_key, w_value, b_query, b_value]
-    second_group = [w_out, w_up, w_down, b_out, gain_one, shift_one, b_up, b_down, gain_two, shift_two]
-
-    def gather_group(items):
-        flat = jnp.concatenate([item.reshape(-1) for item in items])
-        got = gather_blocks(flat)
-        pieces, offset = [], 0
-        for item in items:
-            size = item.size
-            piece = got[:, offset:offset + size]
-            offset += size
-            if item.ndim == 2:
-                pieces.append(from_blocks(piece, n_dp, n_seq, item.shape[0], item.shape[1]))
-            else:
-                pieces.append(piece.reshape(n_dp, n_seq, size)[:, 0].reshape(-1))
-        return pieces
-
-    full_query, full_key, full_value, g_b_query, g_b_value = gather_group(first_group)
-    (
-        full_out, full_up, full_down, g_b_out, g_gain_one, g_shift_one, g_b_up, g_b_down, g_gain_two, g_shift_two,
-    ) = gather_group(second_group)
+    (full_query, full_key, full_value), (g_b_query, g_b_value) = gather_weights(
+        [w_query, w_key, w_value], [b_query, b_value]
+    )
+    (full_out, full_up, full_down), (
+        g_b_out, g_gain_one, g_shift_one, g_b_up, g_b_down, g_gain_two, g_shift_two,
+    ) = gather_weights([w_out, w_up, w_down], [b_out, gain_one, shift_one, b_up, b_down, gain_two, shift_two])
     (
         vec_query,
         vec_value,
@@ -324,11 +373,12 @@
     grad_branch = grad_hidden.astype(jnp.bfloat16)
     grad_b_out = jnp.sum(grad_branch.astype(jnp.float32), axis=0)
     grad_w_out = blocked_grad(context_tok, grad_branch, n_dp, n_seq)
-    group_a = [grad_w_out, grad_w_up, grad_w_down] + [
-        blocked_vector(item, n_dp, n_seq)
-        for item in (grad_b_out, grad_gain_one, grad_shift_one, grad_b_up, grad_b_down, grad_gain_two, grad_shift_two)
-    ]
-    summed_a = reduce_blocks(jnp.concatenate(group_a, axis=1))
+    (own_w_out, own_w_up, own_w_down), (
+        own_b_out, own_gain_one, own_shift_one, own_b_up, own_b_down, own_gain_two, own_shift_two,
+    ) = reduce_grads(
+        [grad_w_out, grad_w_up, grad_w_down],
+        [grad_b_out, grad_gain_one, grad_shift_one, grad_b_up, grad_b_down, grad_gain_two, grad_shift_two],
+    )
     grad_context = times_back(grad_branch, back_out).astype(jnp.bfloat16)
     grad_heads = lax.all_to_all(
         token_split(grad_context), "seq", split_axis=2, concat_axis=1, tiled=True
@@ -405,33 +455,14 @@
     grad_w_key = blocked_grad(flat, grad_k, n_dp, n_seq)
     grad_w_value = blocked_grad(flat, grad_v, n_dp, n_seq)
     grad_b_value = jnp.sum(grad_v.astype(jnp.float32), axis=0)
-    group_b = [grad_w_query, grad_w_key, grad_w_value] + [
-        blocked_vector(item, n_dp, n_seq) for item in (grad_b_query, grad_b_value)
-    ]
-    summed_b = reduce_blocks(jnp.concatenate(group_b, axis=1))
+    (own_w_query, own_w_key, own_w_value), (own_b_query, own_b_value) = reduce_grads(
+        [grad_w_query, grad_w_key, grad_w_value], [grad_b_query, grad_b_value]
+    )
     grad_inputs = (
         grad_hidden
         + times_back(grad_q, back_query)
         + times_back(grad_k, back_key)
         + times_back(grad_v, back_value)
-    )
-    def unpack(summed, shapes):
-        pieces, offset = [], 0
-        for shape in shapes:
-            size = 1
-            for dim in shape:
-                size *= dim
-            pieces.append(summed[offset:offset + size].reshape(shape))
-            offset += size
-        return pieces
-
-    (
-        own_w_out, own_w_up, own_w_down, own_b_out, own_gain_one, own_shift_one, own_b_up, own_b_down,
-        own_gain_two, own_shift_two,
-    ) = unpack(summed_a, [w_out.shape, w_up.shape, w_down.shape, b_out.shape, gain_one.shape, shift_one.shape,
-                          b_up.shape, b_down.shape, gain_two.shape, shift_two.shape])
-    own_w_query, own_w_key, own_w_value, own_b_query, own_b_value = unpack(
-        summed_b, [w_query.shape, w_key.shape, w_value.shape, b_query.shape, b_value.shape]
     )
     return (
         output.reshape(seqs_here, shard_len, width),

time: 1420 us -> 1280 us (0.901)
  other arithmetic: 231 us -> 156 us
  local copies, waits for them, and re-layouts: 626 us -> 552 us
    another operation x68 -> x19, other arithmetic: 92.8 us -> 10.1 us  [the longest x1 5.15 us: gather_weights(): jnp.stack([canon[part][index].reshape(n_dp, n_seq, third, m.shape[1]) for...]
    reshape x39 -> x58, local copies, waits for them, and re-layouts: 135 us -> 62 us  [the longest x15 27.5 us: reduce_grads(): m[:, :, part * third:(part + 1) * third].reshape(n_dp * n_seq, -1)]
    dynamic_slice x24 -> x2, local copies, waits for them, and re-layouts: 63.9 us -> 0.12 us  [the longest x1 0.11 us: reduce_parts(): keep = lax.dynamic_index_in_dim(half, mine, 0, keepdims=False)]
    slice x20 -> x58, local copies, waits for them, and re-layouts: 17.7 us -> 57.2 us  [the longest x24 35.6 us: reduce_grads(): m[:, :, part * third:(part + 1) * third].reshape(n_dp * n_seq, -1)]
    ppermute x60, waiting for transfers between devices: 102 us -> 133 us  [the longest x30 123 us: reduce_parts(): buf = keep + lax.ppermute(send, bit[0], partner(bit))]
    another operation x24 -> x28, local copies, waits for them, and re-layouts: 29.2 us -> 52.4 us  [the longest x21 44.1 us: gather_weights(): jnp.stack([canon[part][index].reshape(n_dp, n_seq, third, m.shape[1]) for...]
    all_to_all x1, waiting for transfers between devices: 16.9 us -> 0.01 us  [shards(): lax.all_to_all(token_split(queries), 'seq', split_axis=2, concat_axis=1,...]
    transpose x7 -> x16, local copies, waits for them, and re-layouts: 39.4 us -> 23.7 us  [the longest x4 14.8 us: gather_weights(): stacked.transpose(0, 2, 3, 1, 4)]
  transfers between devices with their start and end apart: 68 -> 68, of which waited for: 16 -> 24; matrix products, arithmetic and copies ran while one was open for 48% -> 44% of each run, Pallas kernels for 0% -> 0%
where the time goes in v2:
time: 1280 us; the launch traced here: 1270 us
  local copies, waits for them, and re-layouts  552 us (43%)
  matrix products  293 us (23%)
  other arithmetic  156 us (12%)
  waiting for transfers between devices  134 us (10%)
  starting transfers between devices  102 us (8%)
  loops' own time  29.6 us (2%)
    ppermute x30, waiting for transfers between devices, reduce_parts(): buf = keep + lax.ppermute(send, bit[0], partner(bit))  123 us
    unnamed x309, local copies, waits for them, and re-layouts  75.8 us
    dot_general x16, matrix products, one_block(): jnp.einsum('qhd,khd->hqk', query_rows, keys_s, preferred_element_type=jnp...  63.3 us
    another operation x21, local copies, waits for them, and re-layouts, gather_weights(): jnp.stack([canon[part][index].reshape(n_dp, n_seq, third, m.shape[1]) for...  44.1 us
    dot_general x6, matrix products, times_back(): lax.dot_general(left, matrix, (((1,), (1,)), ((), ())), preferred_element...  37.2 us
    dot_general x1, matrix products, shards(): jnp.dot(normed_low, full_up, preferred_element_type=jnp.float32) + vec_up  36.7 us
    slice x24, local copies, waits for them, and re-layouts, reduce_grads(): m[:, :, part * third:(part + 1) * third].reshape(n_dp * n_seq, -1)  35.6 us
    ppermute x30, starting transfers between devices, reduce_parts(): buf = keep + lax.ppermute(send, bit[0], partner(bit))  34.7 us
  transfers between devices with their start and end apart: 68, of which 24 were waited for; matrix products, arithmetic and copies ran while one was open for 44% of the time, Pallas kernels for 0%

profile of v2, /device:TPU:0, one launch (start us, length us, event | category | flops | bytes accessed | tf_op | source)
XLA Modules:
  0.0 1271.6 jit_solution(4395458984040094404)
XLA Ops:
  14.2 6.3 concatenate.173
  209.2 114.4 %while.94 = (s32[]{:T(128)}, bf16[4,1024,3,64]{1,3,2,0:T(8,128)(2,1)}, f32[4,2,3,512]{3,2,1,0:T(4,128)}, s32[4,1024]{1,0:T(4,128)S(1)}, s32[4,1024]{1,0:T(4,128)...) while((s32[]{:T(128)}, ...), condition=%wide.region_8.9_spmd, body=%wide.region_2.8_spmd.sunk | while | flops 424790912 | bytes 34466940 | solution.py:335
  212.4 22.9 %while.97 = (s32[]{:T(128)}, bf16[2,512,3,64]{1,3,2,0:T(8,128)(2,1)S(1)}, f32[2,3,512]{2,1,0:T(4,128)S(1)}, s32[2]{0:T(128)S(1)}, s32[1024]{0:T(1024)S(1)}, /*in...) while((s32[]{:T(128)}, ...), condition=%wide.region_7.7_spmd, body=%wide.region_3.6_spmd.sunk | while | flops 424790912 | bytes 29693712 | solution.py:332
  240.9 22.9 %while.97 = (s32[]{:T(128)}, bf16[2,512,3,64]{1,3,2,0:T(8,128)(2,1)S(1)}, f32[2,3,512]{2,1,0:T(4,128)S(1)}, s32[2]{0:T(128)S(1)}, s32[1024]{0:T(1024)S(1)}, /*in...) while((s32[]{:T(128)}, ...), condition=%wide.region_7.7_spmd, body=%wide.region_3.6_spmd.sunk | while | flops 424790912 | bytes 29693712 | solution.py:332
  269.5 22.9 %while.97 = (s32[]{:T(128)}, bf16[2,512,3,64]{1,3,2,0:T(8,128)(2,1)S(1)}, f32[2,3,512]{2,1,0:T(4,128)S(1)}, s32[2]{0:T(128)S(1)}, s32[1024]{0:T(1024)S(1)}, /*in...) while((s32[]{:T(128)}, ...), condition=%wide.region_7.7_spmd, body=%wide.region_3.6_spmd.sunk | while | flops 424790912 | bytes 29693712 | solution.py:332
  298.0 22.9 %while.97 = (s32[]{:T(128)}, bf16[2,512,3,64]{1,3,2,0:T(8,128)(2,1)S(1)}, f32[2,3,512]{2,1,0:T(4,128)S(1)}, s32[2]{0:T(128)S(1)}, s32[1024]{0:T(1024)S(1)}, /*in...) while((s32[]{:T(128)}, ...), condition=%wide.region_7.7_spmd, body=%wide.region_3.6_spmd.sunk | while | flops 424790912 | bytes 29693712 | solution.py:332
  385.5 8.3 copy.569
  393.7 11.6 reshape.1190
  405.3 5.7 copy.666
  427.3 36.7 %multiply_convert_fusion.1 = (bf16[1024,3072]{1,0:T(8,128)(2,1)S(1)}, f32[1024,3072]{1,0:T(8,128)}, f32[1024,3072]{1,0:T(8,128)}) fusion(f32[3072]{0:T(1024)S(1)} %bitcast.792, bf16[1024,768]{0,1:T(8,128)(2,1)S(1)} %fusion.62, bf16[768,3072]{1,0:T(8,128)(2,1)S(1)} %bitcast.730), kind=kOutput, calls=%fused_computation.113 | convolution fusion | flops 5039456256 | bytes 37761024 | tf_op jit(solution)/shard_map/dot_general | solution.py:353
  464.1 5.9 fusion.113
  478.7 18.1 %convert_reduce_fusion = (f32[3072]{0:T(1024)}, bf16[1024,3072]{1,0:T(8,128)(2,1)}) fusion(f32[1024,3072]{1,0:T(8,128)} %get-tuple-element.1149, bf16[1024,768]{0,1:T(8,128)(2,1)S(1)} %get-tuple-element.1141, bf16[3072,768]{1,0:T(8,128)(2,1)} %reshape.1190, f32[1024,3072]{1,0:T(8,128)} %get-tuple-element.1319, f32[3072]{0:T(1024)S(1)} %bitcast.793), kind=kOutput, calls=%fused_computation.111 | convolution fusion | flops 4885312512 | bytes 37773312 | tf_op jit(solution)/shard_map/dot_general | solution.py:60
  496.8 12.3 reshape.1235
  509.1 11.8 multiply_reduce_fusion.2
  524.7 8.3 fusion.58
  562.1 7.1 fusion.61
  590.1 290.0 %while.96 = (s32[]{:T(128)}, bf16[4,1024,3,64]{1,3,2,0:T(8,128)(2,1)}, bf16[4,1024,3,64]{1,3,2,0:T(8,128)(2,1)}, bf16[4,1024,3,64]{1,3,2,0:T(8,128)(2,1)}, s32[4...) while((s32[]{:T(128)}, ...), condition=%wide.region_22.23_spmd, body=%wide.region_17.22_spmd.sunk | while | flops 1031719808 | bytes 148861008 | solution.py:436
  598.0 59.3 %while.98 = (s32[]{:T(128)}, f32[1024,3,64]{0,2,1:T(8,128)}, f32[1024,3,64]{0,2,1:T(8,128)}, bf16[2,512,3,64]{1,3,2,0:T(8,128)(2,1)}, s32[2]{0:T(128)S(1)}, /*in...) while((s32[]{:T(128)}, f32[1024,3,64]{0,2,1:T(8,128)}, ...), condition=%wide.region_21.21_spmd.clone, body=%wide.region_18.20_spmd.clone.sunk | while | flops 1031326592 | bytes 140946064 | solution.py:426
  610.4 5.6 multiply_reduce_fusion.8
  639.7 5.6 multiply_reduce_fusion.8
  670.5 59.3 %while.98 = (s32[]{:T(128)}, f32[1024,3,64]{0,2,1:T(8,128)}, f32[1024,3,64]{0,2,1:T(8,128)}, bf16[2,512,3,64]{1,3,2,0:T(8,128)(2,1)}, s32[2]{0:T(128)S(1)}, /*in...) while((s32[]{:T(128)}, f32[1024,3,64]{0,2,1:T(8,128)}, ...), condition=%wide.region_21.21_spmd.clone, body=%wide.region_18.20_spmd.clone.sunk | while | flops 1031326592 | bytes 140946064 | solution.py:426
  682.8 5.6 multiply_reduce_fusion.8
  712.2 5.6 multiply_reduce_fusion.8
  743.0 59.3 %while.98 = (s32[]{:T(128)}, f32[1024,3,64]{0,2,1:T(8,128)}, f32[1024,3,64]{0,2,1:T(8,128)}, bf16[2,512,3,64]{1,3,2,0:T(8,128)(2,1)}, s32[2]{0:T(128)S(1)}, /*in...) while((s32[]{:T(128)}, f32[1024,3,64]{0,2,1:T(8,128)}, ...), condition=%wide.region_21.21_spmd.clone, body=%wide.region_18.20_spmd.clone.sunk | while | flops 1031326592 | bytes 140946064 | solution.py:426
  784.7 5.6 multiply_reduce_fusion.8
  815.4 59.3 %while.98 = (s32[]{:T(128)}, f32[1024,3,64]{0,2,1:T(8,128)}, f32[1024,3,64]{0,2,1:T(8,128)}, bf16[2,512,3,64]{1,3,2,0:T(8,128)(2,1)}, s32[2]{0:T(128)S(1)}, /*in...) while((s32[]{:T(128)}, f32[1024,3,64]{0,2,1:T(8,128)}, ...), condition=%wide.region_21.21_spmd.clone, body=%wide.region_18.20_spmd.clone.sunk | while | flops 1031326592 | bytes 140946064 | solution.py:426
  827.8 5.6 multiply_reduce_fusion.8
  857.2 5.6 multiply_reduce_fusion.8
  1100.1 35.6 %collective-permute-done.36 = f32[8,144,128]{2,1,0:T(8,128)S(1)} collective-permute-done((f32[8,144,128]{2,1,0:T(8,128)S(1)}, f32[8,144,128]{2,1,0:T(8,128)S(1)}, u32[]{:S(2)}, u32[]{:S(2)}) %collective-permute-start.36) | collective-permute-done | bytes 589856 | tf_op jit(solution)/shard_map/ppermute | solution.py:148
  1149.1 34.0 %collective-permute-done.42 = f32[4,144,128]{2,1,0:T(8,128)S(1)} collective-permute-done((f32[4,144,128]{2,1,0:T(8,128)S(1)}, f32[4,144,128]{2,1,0:T(8,128)S(1)}, u32[]{:S(2)}, u32[]{:S(2)}) %collective-permute-start.42) | collective-permute-done | bytes 294944 | tf_op jit(solution)/shard_map/ppermute | solution.py:148
  1219.7 7.3 collective-permute-done.52
  1252.8 7.0 collective-permute-done.54
  (1448 shorter events, 983.0 us)
Async XLA Ops:
  5.7 54.6 %collective-permute-start.20 = (bf16[1,432,128]{2,1,0:T(8,128)(2,1)}, bf16[1,432,128]{2,1,0:T(8,128)(2,1)}, u32[]{:S(2)}, u32[]{:S(2)}) collective-permute-start(bf16[1,432,128]{2,1,0:T(8,128)(2,1)} %maximum_bitcast_fusion.9), channel_id=1, source_target_pairs={{0,4},{1,5},{2,6},{3,7},{4,0},{5,1},{6,2},{7,3},{8,12},{9,13},{10,... | collective-permute-start | bytes 331784 | tf_op jit(solution)/shard_map/ppermute | solution.py:133
  12.3 49.8 %collective-permute-start.25 = (bf16[1,432,128]{2,1,0:T(8,128)(2,1)}, bf16[1,432,128]{2,1,0:T(8,128)(2,1)}, u32[]{:S(2)}, u32[]{:S(2)}) collective-permute-start(bf16[1,432,128]{2,1,0:T(8,128)(2,1)} %maximum_bitcast_fusion.10), channel_id=1, source_target_pairs={{0,4},{1,5},{2,6},{3,7},{4,0},{5,1},{6,2},{7,3},{8,12},{9,13},{10,... | collective-permute-start | bytes 331784 | tf_op jit(solution)/shard_map/ppermute | solution.py:133
  21.3 46.2 %collective-permute-start.15 = (bf16[1,440,128]{2,1,0:T(8,128)(2,1)S(1)}, bf16[1,440,128]{2,1,0:T(8,128)(2,1)}, u32[]{:S(2)}, u32[]{:S(2)}) collective-permute-start(bf16[1,440,128]{2,1,0:T(8,128)(2,1)S(1)} %bitcast.772), channel_id=1, source_target_pairs={{0,4},{1,5},{2,6},{3,7},{4,0},{5,1},{6,2},{7,3},{8,12},{9,13},{10,... | collective-permute-start | bytes 337928 | tf_op jit(solution)/shard_map/ppermute | solution.py:133
  72.0 40.5 %collective-permute-start.16 = (bf16[2,440,128]{2,1,0:T(8,128)(2,1)}, bf16[2,440,128]{2,1,0:T(8,128)(2,1)}, u32[]{:S(2)}, u32[]{:S(2)}) collective-permute-start(bf16[2,440,128]{2,1,0:T(8,128)(2,1)} %pad_maximum_fusion.24), channel_id=1, source_target_pairs={{0,2},{1,3},{2,0},{3,1},{4,6},{5,7},{6,4},{7,5},{8,10},{9,11},{10,... | collective-permute-start | bytes 675848 | tf_op jit(solution)/shard_map/ppermute | solution.py:133
  78.2 37.4 %collective-permute-start.22 = (bf16[4,432,128]{2,1,0:T(8,128)(2,1)}, bf16[4,432,128]{2,1,0:T(8,128)(2,1)}, u32[]{:S(2)}, u32[]{:S(2)}) collective-permute-start(bf16[4,432,128]{2,1,0:T(8,128)(2,1)} %pad_maximum_fusion.17), channel_id=1, source_target_pairs={{0,2},{1,3},{2,0},{3,1},{4,6},{5,7},{6,4},{7,5},{8,10},{9,11},{10,... | collective-permute-start | bytes 1327112 | tf_op jit(solution)/shard_map/ppermute | solution.py:133
  79.9 67.5 %collective-permute-start.27 = (bf16[4,432,128]{2,1,0:T(8,128)(2,1)}, bf16[4,432,128]{2,1,0:T(8,128)(2,1)}, u32[]{:S(2)}, u32[]{:S(2)}) collective-permute-start(bf16[4,432,128]{2,1,0:T(8,128)(2,1)} %pad_maximum_fusion.18), channel_id=1, source_target_pairs={{0,16},{8,24},{16,0},{24,8},{1,17},{9,25},{17,1},{25,9},{2,18},{10... | collective-permute-start | bytes 1327112 | tf_op jit(solution)/shard_map/ppermute | solution.py:133
  108.9 33.9 %all-to-all-start.2 = ((bf16[4,256,4,192]{1,0,3,2:T(4,128)(2,1)}), bf16[4,256,4,192]{1,0,3,2:T(4,128)(2,1)S(1)}, u32[]{:S(2)}, u32[]{:S(2)}) async-start(bf16[4,256,4,192]{1,0,3,2:T(4,128)(2,1)} %reshape.1168), calls=%async_computation.2 | async-start | bytes 3145728 | tf_op jit(solution)/shard_map/all_to_all | solution.py:303
  114.4 35.8 %collective-permute-start.17 = (bf16[4,440,128]{2,1,0:T(8,128)(2,1)}, bf16[4,440,128]{2,1,0:T(8,128)(2,1)}, u32[]{:S(2)}, u32[]{:S(2)}) collective-permute-start(bf16[4,440,128]{2,1,0:T(8,128)(2,1)} %pad_maximum_fusion.16), channel_id=1, source_target_pairs={{0,1},{1,0},{2,3},{3,2},{4,5},{5,4},{6,7},{7,6},{8,9},{9,8},{10,11... | collective-permute-start | bytes 1351688 | tf_op jit(solution)/shard_map/ppermute | solution.py:133
  118.7 63.7 %collective-permute-start.23 = (bf16[8,432,128]{2,1,0:T(8,128)(2,1)}, bf16[8,432,128]{2,1,0:T(8,128)(2,1)}, u32[]{:S(2)}, u32[]{:S(2)}) collective-permute-start(bf16[8,432,128]{2,1,0:T(8,128)(2,1)} %pad_maximum_fusion.11), channel_id=1, source_target_pairs={{0,1},{1,0},{2,3},{3,2},{4,5},{5,4},{6,7},{7,6},{8,9},{9,8},{10,11... | collective-permute-start | bytes 2654216 | tf_op jit(solution)/shard_map/ppermute | solution.py:133
  142.8 35.7 %all-to-all-start.1 = ((bf16[4,256,4,192]{1,0,3,2:T(4,128)(2,1)}), bf16[4,256,4,192]{1,0,3,2:T(4,128)(2,1)}, u32[]{:S(2)}, u32[]{:S(2)}) async-start(bf16[4,256,4,192]{1,0,3,2:T(4,128)(2,1)} %reshape.1164), calls=%async_computation.1 | async-start | bytes 3145728 | tf_op jit(solution)/shard_map/all_to_all | solution.py:302
  149.8 36.3 %collective-permute-start.28 = (bf16[8,432,128]{2,1,0:T(8,128)(2,1)}, bf16[8,432,128]{2,1,0:T(8,128)(2,1)}, u32[]{:S(2)}, u32[]{:S(2)}) collective-permute-start(bf16[8,432,128]{2,1,0:T(8,128)(2,1)} %pad_maximum_fusion.12), channel_id=1, source_target_pairs={{0,2},{1,3},{2,0},{3,1},{4,6},{5,7},{6,4},{7,5},{8,10},{9,11},{10,... | collective-permute-start | bytes 2654216 | tf_op jit(solution)/shard_map/ppermute | solution.py:133
  153.1 36.1 %collective-permute-start.18 = (bf16[8,440,128]{2,1,0:T(8,128)(2,1)}, bf16[8,440,128]{2,1,0:T(8,128)(2,1)}, u32[]{:S(2)}, u32[]{:S(2)}) collective-permute-start(bf16[8,440,128]{2,1,0:T(8,128)(2,1)} %pad_maximum_fusion.10), channel_id=1, source_target_pairs={{0,16},{8,24},{16,0},{24,8},{1,17},{9,25},{17,1},{25,9},{2,18},{10... | collective-permute-start | bytes 2703368 | tf_op jit(solution)/shard_map/ppermute | solution.py:133
  185.6 147.3 %collective-permute-start.24 = (bf16[16,432,128]{2,1,0:T(8,128)(2,1)}, bf16[16,432,128]{2,1,0:T(8,128)(2,1)}, u32[]{:S(2)}, u32[]{:S(2)}) collective-permute-start(bf16[16,432,128]{2,1,0:T(8,128)(2,1)} %pad_maximum_fusion.5), channel_id=1, source_target_pairs={{0,8},{8,0},{16,24},{24,16},{1,9},{9,1},{17,25},{25,17},{2,10},{10... | collective-permute-start | bytes 5308424 | tf_op jit(solution)/shard_map/ppermute | solution.py:133
  188.8 148.7 %collective-permute-start.29 = (bf16[16,432,128]{2,1,0:T(8,128)(2,1)}, bf16[16,432,128]{2,1,0:T(8,128)(2,1)}, u32[]{:S(2)}, u32[]{:S(2)}) collective-permute-start(bf16[16,432,128]{2,1,0:T(8,128)(2,1)} %pad_maximum_fusion.6), channel_id=1, source_target_pairs={{0,8},{8,0},{16,24},{24,16},{1,9},{9,1},{17,25},{25,17},{2,10},{10... | collective-permute-start | bytes 5308424 | tf_op jit(solution)/shard_map/ppermute | solution.py:133
  192.8 172.3 %collective-permute-start.19 = (bf16[16,440,128]{2,1,0:T(8,128)(2,1)}, bf16[16,440,128]{2,1,0:T(8,128)(2,1)}, u32[]{:S(2)}, u32[]{:S(2)}) collective-permute-start(bf16[16,440,128]{2,1,0:T(8,128)(2,1)} %pad_maximum_fusion.4), channel_id=1, source_target_pairs={{0,8},{8,0},{16,24},{24,16},{1,9},{9,1},{17,25},{25,17},{2,10},{10... | collective-permute-start | bytes 5406728 | tf_op jit(solution)/shard_map/ppermute | solution.py:133
  327.9 90.8 %all-to-all-start.3 = ((bf16[4,1024,1,192]{3,0,2,1:T(4,128)(2,1)}), bf16[4,1024,1,192]{3,0,2,1:T(4,128)(2,1)}, u32[]{:S(2)}, u32[]{:S(2)}) async-start(bf16[4,1024,1,192]{3,0,2,1:T(4,128)(2,1)} %copy.554), calls=%async_computation.3 | async-start | bytes 4194304 | tf_op jit(solution)/shard_map/all_to_all | solution.py:338
  884.4 30.2 %all-to-all-start.5 = ((bf16[4,1024,1,192]{3,0,2,1:T(4,128)(2,1)}), bf16[4,1024,1,192]{3,0,2,1:T(4,128)(2,1)}, u32[]{:S(2)}, u32[]{:S(2)}) async-start(bf16[4,1024,1,192]{3,0,2,1:T(4,128)(2,1)} %copy.577), calls=%async_computation.5 | async-start | bytes 4194304 | tf_op jit(solution)/shard_map/all_to_all | solution.py:444
  914.6 70.1 %all-to-all-start.6 = ((bf16[4,1024,1,192]{3,0,2,1:T(4,128)(2,1)}), bf16[4,1024,1,192]{3,0,2,1:T(4,128)(2,1)}, u32[]{:S(2)}, u32[]{:S(2)}) async-start(bf16[4,1024,1,192]{3,0,2,1:T(4,128)(2,1)} %copy.581), calls=%async_computation.6 | async-start | bytes 4194304 | tf_op jit(solution)/shard_map/all_to_all | solution.py:445
  923.7 172.3 %collective-permute-start.45 = (f32[16,440,128]{2,1,0:T(8,128)}, f32[16,440,128]{2,1,0:T(8,128)}, u32[]{:S(2)}, u32[]{:S(2)}) collective-permute-start(f32[16,440,128]{2,1,0:T(8,128)} %dynamic-slice_bitcast_fusion.9), channel_id=1, source_target_pairs={{0,8},{8,0},{16,24},{24,16},{1,9},{9,1},{17,25},{25,17},{2,10},{10... | collective-permute-start | bytes 10813448 | tf_op jit(solution)/shard_map/ppermute | solution.py:148
  948.3 128.3 %collective-permute-start.50 = (f32[16,432,128]{2,1,0:T(8,128)}, f32[16,432,128]{2,1,0:T(8,128)}, u32[]{:S(2)}, u32[]{:S(2)}) collective-permute-start(f32[16,432,128]{2,1,0:T(8,128)} %dynamic-slice_bitcast_fusion.11), channel_id=1, source_target_pairs={{0,8},{8,0},{16,24},{24,16},{1,9},{9,1},{17,25},{25,17},{2,10},{10... | collective-permute-start | bytes 10616840 | tf_op jit(solution)/shard_map/ppermute | solution.py:148
  972.3 110.1 %collective-permute-start.55 = (f32[16,432,128]{2,1,0:T(8,128)}, f32[16,432,128]{2,1,0:T(8,128)}, u32[]{:S(2)}, u32[]{:S(2)}) collective-permute-start(f32[16,432,128]{2,1,0:T(8,128)} %dynamic-slice_bitcast_fusion.10), channel_id=1, source_target_pairs={{0,8},{8,0},{16,24},{24,16},{1,9},{9,1},{17,25},{25,17},{2,10},{10... | collective-permute-start | bytes 10616840 | tf_op jit(solution)/shard_map/ppermute | solution.py:148
  984.7 30.8 %all-to-all-start.7 = ((bf16[4,1024,1,192]{3,0,2,1:T(4,128)(2,1)}), bf16[4,1024,1,192]{3,0,2,1:T(4,128)(2,1)}, u32[]{:S(2)}, u32[]{:S(2)}) async-start(bf16[4,1024,1,192]{3,0,2,1:T(4,128)(2,1)} %copy.585), calls=%async_computation.7 | async-start | bytes 4194304 | tf_op jit(solution)/shard_map/all_to_all | solution.py:446
  1047.4 45.4 %collective-permute-start.30 = (f32[16,146,128]{2,0,1:T(8,128)}, f32[16,146,128]{2,0,1:T(8,128)}, u32[]{:S(2)}, u32[]{:S(2)}) collective-permute-start(f32[16,146,128]{2,0,1:T(8,128)} %dynamic-slice_bitcast_fusion.15), channel_id=1, source_target_pairs={{0,8},{8,0},{16,24},{24,16},{1,9},{9,1},{17,25},{25,17},{2,10},{10... | collective-permute-start | bytes 3588104 | tf_op jit(solution)/shard_map/ppermute | solution.py:148
  1055.7 32.1 %collective-permute-start.35 = (f32[16,144,128]{2,1,0:T(8,128)}, f32[16,144,128]{2,1,0:T(8,128)}, u32[]{:S(2)}, u32[]{:S(2)}) collective-permute-start(f32[16,144,128]{2,1,0:T(8,128)} %dynamic-slice_bitcast_fusion.17), channel_id=1, source_target_pairs={{0,8},{8,0},{16,24},{24,16},{1,9},{9,1},{17,25},{25,17},{2,10},{10... | collective-permute-start | bytes 3538952 | tf_op jit(solution)/shard_map/ppermute | solution.py:148
  1082.4 122.7 %collective-permute-start.51 = (f32[8,432,128]{2,1,0:T(8,128)}, f32[8,432,128]{2,1,0:T(8,128)}, u32[]{:S(2)}, u32[]{:S(2)}) collective-permute-start(f32[8,432,128]{2,1,0:T(8,128)} %dynamic-slice_bitcast_fusion.14), channel_id=1, source_target_pairs={{0,1},{1,0},{2,3},{3,2},{4,5},{5,4},{6,7},{7,6},{8,9},{9,8},{10,11... | collective-permute-start | bytes 5308424 | tf_op jit(solution)/shard_map/ppermute | solution.py:148
  1087.8 121.9 %collective-permute-start.56 = (f32[8,432,128]{2,1,0:T(8,128)}, f32[8,432,128]{2,1,0:T(8,128)}, u32[]{:S(2)}, u32[]{:S(2)}) collective-permute-start(f32[8,432,128]{2,1,0:T(8,128)} %dynamic-slice_bitcast_fusion.13), channel_id=1, source_target_pairs={{0,2},{1,3},{2,0},{3,1},{4,6},{5,7},{6,4},{7,5},{8,10},{9,11},{10,... | collective-permute-start | bytes 5308424 | tf_op jit(solution)/shard_map/ppermute | solution.py:148
  1092.1 43.6 %collective-permute-start.36 = (f32[8,144,128]{2,1,0:T(8,128)S(1)}, f32[8,144,128]{2,1,0:T(8,128)S(1)}, u32[]{:S(2)}, u32[]{:S(2)}) collective-permute-start(f32[8,144,128]{2,1,0:T(8,128)S(1)} %dynamic-slice_bitcast_fusion.23), channel_id=1, source_target_pairs={{0,1},{1,0},{2,3},{3,2},{4,5},{5,4},{6,7},{7,6},{8,9},{9,8},{10,11... | collective-permute-start | bytes 1769480 | tf_op jit(solution)/shard_map/ppermute | solution.py:148
  1092.8 48.0 %collective-permute-start.41 = (f32[8,144,128]{2,1,0:T(8,128)S(1)}, f32[8,144,128]{2,1,0:T(8,128)S(1)}, u32[]{:S(2)}, u32[]{:S(2)}) collective-permute-start(f32[8,144,128]{2,1,0:T(8,128)S(1)} %dynamic-slice_bitcast_fusion.22), channel_id=1, source_target_pairs={{0,2},{1,3},{2,0},{3,1},{4,6},{5,7},{6,4},{7,5},{8,10},{9,11},{10,... | collective-permute-start | bytes 1769480 | tf_op jit(solution)/shard_map/ppermute | solution.py:148
  1096.0 46.2 %collective-permute-start.31 = (f32[8,146,128]{2,0,1:T(8,128)S(1)}, f32[8,146,128]{2,0,1:T(8,128)S(1)}, u32[]{:S(2)}, u32[]{:S(2)}) collective-permute-start(f32[8,146,128]{2,0,1:T(8,128)S(1)} %dynamic-slice_bitcast_fusion.21), channel_id=1, source_target_pairs={{0,16},{8,24},{16,0},{24,8},{1,17},{9,25},{17,1},{25,9},{2,18},{10... | collective-permute-start | bytes 1794056 | tf_op jit(solution)/shard_map/ppermute | solution.py:148
  1135.7 78.5 %collective-permute-start.46 = (f32[8,440,128]{2,1,0:T(8,128)S(1)}, f32[8,440,128]{2,1,0:T(8,128)}, u32[]{:S(2)}, u32[]{:S(2)}) collective-permute-start(f32[8,440,128]{2,1,0:T(8,128)S(1)} %dynamic-slice_bitcast_fusion.12), channel_id=1, source_target_pairs={{0,16},{8,24},{16,0},{24,8},{1,17},{9,25},{17,1},{25,9},{2,18},{10... | collective-permute-start | bytes 5406728 | tf_op jit(solution)/shard_map/ppermute | solution.py:148
  1142.2 40.9 %collective-permute-start.42 = (f32[4,144,128]{2,1,0:T(8,128)S(1)}, f32[4,144,128]{2,1,0:T(8,128)S(1)}, u32[]{:S(2)}, u32[]{:S(2)}) collective-permute-start(f32[4,144,128]{2,1,0:T(8,128)S(1)} %dynamic-slice_bitcast_fusion.28), channel_id=1, source_target_pairs={{0,16},{8,24},{16,0},{24,8},{1,17},{9,25},{17,1},{25,9},{2,18},{10... | collective-permute-start | bytes 884744 | tf_op jit(solution)/shard_map/ppermute | solution.py:148
  1148.6 36.3 %collective-permute-start.32 = (f32[4,146,128]{2,0,1:T(4,128)S(1)}, f32[4,146,128]{2,0,1:T(4,128)S(1)}, u32[]{:S(2)}, u32[]{:S(2)}) collective-permute-start(f32[4,146,128]{2,0,1:T(4,128)S(1)} %dynamic-slice_bitcast_fusion.27), channel_id=1, source_target_pairs={{0,1},{1,0},{2,3},{3,2},{4,5},{5,4},{6,7},{7,6},{8,9},{9,8},{10,11... | collective-permute-start | bytes 897032 | tf_op jit(solution)/shard_map/ppermute | solution.py:148
  (252 other events, 1882.4 us)

commit v3 on v2

--- a/solution.py
+++ b/solution.py
@@ -3,6 +3,8 @@
 import jax
 import jax.numpy as jnp
 from jax import lax
+from jax.experimental import pallas as pl
+from jax.experimental.pallas import tpu as pltpu
 from jax.sharding import PartitionSpec as P
 
 H = 12
@@ -231,6 +233,146 @@
     return own, vecs
 
 
+TQ = 256
+SCALE = HD ** (-0.5)
+
+
+def row_table(segment_row, pad_row, random_heads):
+    length = segment_row.shape[0]
+    n_blocks = length // BLK
+    assert n_blocks <= 31
+    places = jnp.arange(length, dtype=jnp.int32)
+    inside = segment_inside(segment_row)
+    lo = places - inside
+    ends = jnp.concatenate([segment_row[1:] != segment_row[:-1], jnp.ones((1,), dtype=jnp.bool_)])
+    hi = lax.cummin(jnp.where(ends, places + 1, length), axis=0, reverse=True)
+    hi = jnp.where(pad_row == 1, hi, lo)
+    glim = jnp.where(inside < NGLOB * BLK, length, lo + NGLOB * BLK)
+    query_block = jnp.arange(n_blocks, dtype=jnp.int32)
+    key_block = jnp.arange(n_blocks, dtype=jnp.int32)
+    near = jnp.abs(query_block[:, None] - key_block[None, :]) <= 1
+    picked = jnp.any(random_heads[:, :, :, None] == key_block[None, None, None, :], axis=2)
+    chosen = near[None] | picked
+    bits = jnp.sum(jnp.where(chosen, jnp.left_shift(1, key_block)[None, None, :], 0), axis=2).astype(jnp.int32)
+    bits = jnp.repeat(bits, BLK, axis=1)
+    heads = random_heads.shape[0]
+    per_row = jnp.stack([lo, hi, glim], axis=-1)
+    per_row = jnp.broadcast_to(per_row[None], (heads, length, 3))
+    return jnp.concatenate([per_row, bits[:, :, None]], axis=-1)
+
+
+def allowed_tile(info, row0, rows, length):
+    lo = info[:, 0:1]
+    hi = info[:, 1:2]
+    glim = info[:, 2:3]
+    bits = info[:, 3:4]
+    col = lax.broadcasted_iota(jnp.int32, (rows, length), 1)
+    row = row0 + lax.broadcasted_iota(jnp.int32, (rows, length), 0)
+    picked = (lax.shift_right_logical(bits, col // BLK) & 1) == 1
+    return ((col >= lo) & (col < hi) & (picked | (col < glim))) | (col == row)
+
+
+def attn_fwd_kernel(info_ref, q_ref, k_ref, v_ref, ctx_ref, lse_ref):
+    rows = q_ref.shape[0]
+    length = k_ref.shape[0]
+    row0 = pl.program_id(1) * rows
+    s = lax.dot_general(
+        q_ref[...], k_ref[...], (((1,), (1,)), ((), ())), preferred_element_type=jnp.float32
+    ) * SCALE
+    s = jnp.where(allowed_tile(info_ref[...], row0, rows, length), s, -1e30)
+    top = jnp.max(s, axis=1, keepdims=True)
+    w = jnp.exp(s - top)
+    total = jnp.sum(w, axis=1, keepdims=True)
+    probs = (w * (1.0 / total)).astype(jnp.bfloat16)
+    ctx = jnp.dot(probs, v_ref[...], preferred_element_type=jnp.float32)
+    ctx_ref[...] = ctx.astype(ctx_ref.dtype)
+    lse_ref[...] = top + jnp.log(total)
+
+
+def attn_bwd_kernel(info_ref, q_ref, k_ref, v_ref, do_ref, lse_ref, dq_ref, dk_ref, dv_ref, dk_acc, dv_acc):
+    qi = pl.program_id(1)
+    rows = q_ref.shape[0]
+    length = k_ref.shape[0]
+    row0 = qi * rows
+
+    @pl.when(qi == 0)
+    def _():
+        dk_acc[...] = jnp.zeros_like(dk_acc)
+        dv_acc[...] = jnp.zeros_like(dv_acc)
+
+    q = q_ref[...]
+    k = k_ref[...]
+    do = do_ref[...]
+    s = lax.dot_general(q, k, (((1,), (1,)), ((), ())), preferred_element_type=jnp.float32) * SCALE
+    allowed = allowed_tile(info_ref[...], row0, rows, length)
+    p = jnp.where(allowed, jnp.exp(s - lse_ref[...]), 0.0)
+    dv_acc[...] += lax.dot_general(
+        p.astype(jnp.bfloat16), do, (((0,), (0,)), ((), ())), preferred_element_type=jnp.float32
+    )
+    dp = lax.dot_general(do, v_ref[...], (((1,), (1,)), ((), ())), preferred_element_type=jnp.float32)
+    inner = jnp.sum(p * dp, axis=1, keepdims=True)
+    ds = (p * (dp - inner)).astype(jnp.bfloat16)
+    dq = jnp.dot(ds, k, preferred_element_type=jnp.float32) * SCALE
+    dq_ref[...] = dq.astype(dq_ref.dtype)
+    dk_acc[...] += lax.dot_general(ds, q, (((0,), (0,)), ((), ())), preferred_element_type=jnp.float32) * SCALE
+
+    @pl.when(qi == pl.num_programs(1) - 1)
+    def _():
+        dk_ref[...] = dk_acc[...].astype(dk_ref.dtype)
+        dv_ref[...] = dv_acc[...].astype(dv_ref.dtype)
+
+
+def attention_forward(info, q, k, v):
+    batch, length, depth = q.shape
+    rows = min(TQ, length)
+    row_spec = pl.BlockSpec((None, rows, depth), lambda b, i: (b, i, 0))
+    whole_spec = pl.BlockSpec((None, length, depth), lambda b, i: (b, 0, 0))
+    return pl.pallas_call(
+        attn_fwd_kernel,
+        grid=(batch, length // rows),
+        in_specs=[pl.BlockSpec((None, rows, 4), lambda b, i: (b, i, 0)), row_spec, whole_spec, whole_spec],
+        out_specs=[row_spec, pl.BlockSpec((None, rows, 1), lambda b, i: (b, i, 0))],
+        out_shape=[
+            jax.ShapeDtypeStruct((batch, length, depth), jnp.bfloat16),
+            jax.ShapeDtypeStruct((batch, length, 1), jnp.float32),
+        ],
+        compiler_params=pltpu.CompilerParams(dimension_semantics=("arbitrary", "arbitrary")),
+        cost_estimate=pl.CostEstimate(
+            flops=4 * batch * length * length * depth,
+            transcendentals=batch * length * length,
+            bytes_accessed=4 * batch * length * depth * 2,
+        ),
+    )(info, q, k, v)
+
+
+def attention_backward(info, q, k, v, do, lse):
+    batch, length, depth = q.shape
+    rows = min(TQ, length)
+    row_spec = pl.BlockSpec((None, rows, depth), lambda b, i: (b, i, 0))
+    whole_spec = pl.BlockSpec((None, length, depth), lambda b, i: (b, 0, 0))
+    return pl.pallas_call(
+        attn_bwd_kernel,
+        grid=(batch, length // rows),
+        in_specs=[
+            pl.BlockSpec((None, rows, 4), lambda b, i: (b, i, 0)),
+            row_spec,
+            whole_spec,
+            whole_spec,
+            row_spec,
+            pl.BlockSpec((None, rows, 1), lambda b, i: (b, i, 0)),
+        ],
+        out_specs=[row_spec, whole_spec, whole_spec],
+        out_shape=[jax.ShapeDtypeStruct((batch, length, depth), jnp.bfloat16)] * 3,
+        scratch_shapes=[pltpu.VMEM((length, depth), jnp.float32), pltpu.VMEM((length, depth), jnp.float32)],
+        compiler_params=pltpu.CompilerParams(dimension_semantics=("arbitrary", "arbitrary")),
+        cost_estimate=pl.CostEstimate(
+            flops=10 * batch * length * length * depth,
+            transcendentals=batch * length * length,
+            bytes_accessed=8 * batch * length * depth * 2,
+        ),
+    )(info, q, k, v, do, lse)
+
+
 def shards(
     inputs,
     cotangent,
@@ -303,38 +445,21 @@
         lax.all_to_all(token_split(values), "seq", split_axis=2, concat_axis=1, tiled=True),
     )
     head_q, head_k, head_v = (head_form(head_q), head_form(head_k), head_form(head_v))
-    insides = jax.vmap(segment_inside)(segments)
     own_random = lax.dynamic_slice_in_dim(
         random_blocks, lax.axis_index("seq") * heads_here, heads_here, 0
     )
-
-    def attend_sequence(items):
-        queries_s, keys_s, values_s, segment_row, pad_row, inside_row = items
-
-        def one_block(block_index):
-            row_start = block_index * QB
-            mask = allowed_mask(segment_row, pad_row, inside_row, own_random, row_start, QB)
-            query_rows = lax.dynamic_slice_in_dim(queries_s, row_start, QB, 0)
-            scores = (
-                jnp.einsum("qhd,khd->hqk", query_rows, keys_s, preferred_element_type=jnp.float32)
-                * scale
-            )
-            scores = jnp.where(mask, scores, -1e30)
-            top = jnp.max(scores, axis=2, keepdims=True)
-            weights = jnp.exp(scores - top)
-            total = jnp.sum(weights, axis=2, keepdims=True)
-            probs = (weights / total).astype(jnp.bfloat16)
-            context = jnp.einsum(
-                "hqk,khd->qhd", probs, values_s, preferred_element_type=jnp.float32
-            ).astype(jnp.bfloat16)
-            return (context, (top + jnp.log(total))[:, :, 0])
-
-        contexts, sums = lax.map(one_block, jnp.arange(n_blocks, dtype=jnp.int32))
-        return (contexts.reshape(seq_len, heads_here, HD), sums)
-
-    contexts, lse_all = lax.map(
-        attend_sequence, (head_q, head_k, head_v, segments, padding, insides)
-    )
+    info = jax.vmap(lambda s, p: row_table(s, p, own_random))(segments, padding)
+    info = info.reshape(seqs_here * heads_here, seq_len, 4)
+
+    def to_bh(array):
+        return array.transpose(0, 2, 1, 3).reshape(seqs_here * heads_here, seq_len, HD)
+
+    def from_bh(array):
+        return array.reshape(seqs_here, heads_here, seq_len, HD).transpose(0, 2, 1, 3)
+
+    bh_q, bh_k, bh_v = to_bh(head_q), to_bh(head_k), to_bh(head_v)
+    bh_ctx, bh_lse = attention_forward(info, bh_q, bh_k, bh_v)
+    contexts = from_bh(bh_ctx)
     context_tok = lax.all_to_all(
         contexts.reshape(seqs_here, seq_len, 1, heads_here * HD),
         "seq",
@@ -385,57 +510,8 @@
     )
     grad_heads = head_form(grad_heads)
 
-    def attend_back(items):
-        queries_s, keys_s, values_s, grads_s, sums_s, segment_row, pad_row, inside_row = items
-
-        def one_block(carry, block_index):
-            grad_keys, grad_values = carry
-            row_start = block_index * QB
-            mask = allowed_mask(segment_row, pad_row, inside_row, own_random, row_start, QB)
-            query_rows = lax.dynamic_slice_in_dim(queries_s, row_start, QB, 0)
-            grad_rows = lax.dynamic_slice_in_dim(grads_s, row_start, QB, 0)
-            lse = lax.dynamic_index_in_dim(sums_s, block_index, 0, keepdims=False)
-            scores = (
-                jnp.einsum("qhd,khd->hqk", query_rows, keys_s, preferred_element_type=jnp.float32)
-                * scale
-            )
-            probs = jnp.where(mask, jnp.exp(scores - lse[:, :, None]), 0.0)
-            probs_low = probs.astype(jnp.bfloat16)
-            grad_values = grad_values + jnp.einsum(
-                "hqk,qhd->khd", probs_low, grad_rows, preferred_element_type=jnp.float32
-            )
-            grad_probs = jnp.einsum(
-                "qhd,khd->hqk", grad_rows, values_s, preferred_element_type=jnp.float32
-            )
-            inner = jnp.sum(probs * grad_probs, axis=2, keepdims=True)
-            grad_scores = (probs * (grad_probs - inner)).astype(jnp.bfloat16)
-            grad_query = (
-                jnp.einsum("hqk,khd->qhd", grad_scores, keys_s, preferred_element_type=jnp.float32)
-                * scale
-            )
-            grad_keys = (
-                grad_keys
-                + jnp.einsum(
-                    "hqk,qhd->khd", grad_scores, query_rows, preferred_element_type=jnp.float32
-                )
-                * scale
-            )
-            return ((grad_keys, grad_values), grad_query)
-
-        zeros = jnp.zeros(keys_s.shape, jnp.float32)
-        (grad_keys, grad_values), grad_queries = lax.scan(
-            one_block, (zeros, zeros), jnp.arange(n_blocks, dtype=jnp.int32)
-        )
-        grad_queries = grad_queries.reshape(keys_s.shape)
-        return (
-            grad_queries.astype(jnp.bfloat16),
-            grad_keys.astype(jnp.bfloat16),
-            grad_values.astype(jnp.bfloat16),
-        )
-
-    grad_q, grad_k, grad_v = lax.map(
-        attend_back, (head_q, head_k, head_v, grad_heads, lse_all, segments, padding, insides)
-    )
+    bh_dq, bh_dk, bh_dv = attention_backward(info, bh_q, bh_k, bh_v, to_bh(grad_heads), bh_lse)
+    grad_q, grad_k, grad_v = from_bh(bh_dq), from_bh(bh_dk), from_bh(bh_dv)
 
     def head_split(array):
         return array.reshape(seqs_here, seq_len, 1, heads_here * HD)

time: 1280 us -> 1150 us (0.90)
  matrix products: 293 us -> 118 us
  Pallas kernels: 0 us -> 172 us
  local copies, waits for them, and re-layouts: 552 us -> 492 us
  other arithmetic: 156 us -> 104 us
  loops' own time: 29.6 us -> 0 us
  waiting for transfers between devices: 134 us -> 156 us
    dot_general x56 -> x0, matrix products: 173 us -> none  [the longest x16 63.3 us: one_block(): jnp.einsum('qhd,khd->hqk', query_rows, keys_s, preferred_element_type=jnp...]
    pallas_call x0 -> x2, Pallas kernels: none -> 172 us  [the longest x1 93.9 us: attention_backward(): pl.pallas_call(attn_bwd_kernel, grid=(batch, length // rows), in_specs=[p...]
    squeeze x28 -> x0, local copies, waits for them, and re-layouts: 31.1 us -> none  [the longest x24 28.2 us: shards(): lax.map(attend_sequence, (head_q, head_k, head_v, segments, padding, insi...]
    another operation x10 -> x0, loops' own time: 29.6 us -> none  [the longest x4 22.5 us: attend_back(): lax.scan(one_block, (zeros, zeros), jnp.arange(n_blocks, dtype=jnp.int32))]
    and x16 -> x0, other arithmetic: 27.9 us -> none  [allowed_mask(): return (same & plain)[None] | same[None] & picked | diagonal[None]]
    while x164 -> x0, local copies, waits for them, and re-layouts: 24.4 us -> none
    dynamic_slice x68 -> x0, local copies, waits for them, and re-layouts: 24.3 us -> none  [the longest x20 11.7 us: shards(): lax.map(attend_sequence, (head_q, head_k, head_v, segments, padding, insi...]
    slice x24, local copies, waits for them, and re-layouts: 35.6 us -> 53.9 us  [reduce_grads(): m[:, :, part * third:(part + 1) * third].reshape(n_dp * n_seq, -1)]
  transfers between devices with their start and end apart: 68 -> 68, of which waited for: 24 -> 26; matrix products, arithmetic and copies ran while one was open for 44% -> 50% of each run, Pallas kernels for 0% -> 15%
where the time goes in v3:
time: 1150 us; the launch traced here: 1140 us
  local copies, waits for them, and re-layouts  492 us (43%)
  Pallas kernels  172 us (15%)
  waiting for transfers between devices  156 us (14%)
  matrix products  118 us (10%)
  other arithmetic  104 us (9%)
  starting transfers between devices  96 us (8%)
    ppermute x30, waiting for transfers between devices, reduce_parts(): buf = keep + lax.ppermute(send, bit[0], partner(bit))  138 us
    pallas_call x1, Pallas kernels, attention_backward(): pl.pallas_call(attn_bwd_kernel, grid=(batch, length // rows), in_specs=[p...  93.9 us
    unnamed x230, local copies, waits for them, and re-layouts  80.6 us
    pallas_call x1, Pallas kernels, attention_forward(): pl.pallas_call(attn_fwd_kernel, grid=(batch, length // rows), in_specs=[p...  77.7 us
    slice x24, local copies, waits for them, and re-layouts, reduce_grads(): m[:, :, part * third:(part + 1) * third].reshape(n_dp * n_seq, -1)  53.9 us
    another operation x21, local copies, waits for them, and re-layouts, gather_weights(): jnp.stack([canon[part][index].reshape(n_dp, n_seq, third, m.shape[1]) for...  49.1 us
    reshape x15, local copies, waits for them, and re-layouts, reduce_grads(): m[:, :, part * third:(part + 1) * third].reshape(n_dp * n_seq, -1)  42.5 us
    dot_general x6, matrix products, times_back(): lax.dot_general(left, matrix, (((1,), (1,)), ((), ())), preferred_element...  36.9 us
  transfers between devices with their start and end apart: 68, of which 26 were waited for; matrix products, arithmetic and copies ran while one was open for 50% of the time, Pallas kernels for 15%

profile of v3, /device:TPU:0, one launch (start us, length us, event | category | flops | bytes accessed | tf_op | source)
XLA Modules:
  0.0 1140.8 jit_solution(654643597192481042)
XLA Ops:
  3.6 5.7 concatenate.181
  27.5 9.5 reduce-window.16
  131.1 4.8 all-to-all-start.1
  230.9 77.7 %shard_map.323 = (bf16[12,1024,64]{2,1,0:T(8,128)(2,1)}, f32[12,1024,1]{2,1,0:T(8,128)}) custom-call(s32[12,1024,4]{2,1,0:T(8,128)} %bitcast.583, bf16[12,1024,64]{2,1,0:T(8,128)(2,1)} %bitcast.636, bf16[12,1024,64]{2,1,0:T(8,128)(2,1)} %bitcast.638, bf16[12,1024,64]{2,1,0:T(8,128)(2,1)} %bitcast.640), custom_call_target="tpu_custom_call" | custom-call | flops 3221225472 | bytes 6291456 | tf_op jit(solution)/shard_map/pallas_call | solution.py:330
  317.1 4.7 all-to-all-start.3
  347.7 4.5 stack_reshape.71
  352.2 4.9 stack_reshape.70
  393.0 8.3 copy.572
  401.4 11.6 %reshape.819 = bf16[3072,768]{1,0:T(8,128)(2,1)} reshape(bf16[8,3,128,4,192]{4,3,2,1,0:T(4,128)(2,1)} %copy.572) | data formatting | bytes 9437184 | tf_op jit(solution)/shard_map/reshape | solution.py:184
  423.1 36.8 %multiply_convert_fusion = (bf16[1024,3072]{1,0:T(8,128)(2,1)S(1)}, f32[1024,3072]{1,0:T(8,128)}, f32[1024,3072]{1,0:T(8,128)}) fusion(f32[3072]{0:T(1024)S(1)} %bitcast.688, bf16[1024,768]{0,1:T(8,128)(2,1)S(1)} %fusion.14, bf16[768,3072]{1,0:T(8,128)(2,1)S(1)} %bitcast.616), kind=kOutput, calls=%fused_computation.4 | convolution fusion | flops 5039456256 | bytes 37761024 | tf_op jit(solution)/shard_map/dot_general | solution.py:478
  460.0 5.9 fusion.66
  474.0 18.8 %convert_reduce_fusion = (f32[3072]{0:T(1024)S(1)}, bf16[1024,3072]{1,0:T(8,128)(2,1)}) fusion(f32[1024,3072]{1,0:T(8,128)} %get-tuple-element.177, bf16[1024,768]{0,1:T(8,128)(2,1)} %get-tuple-element.169, bf16[3072,768]{1,0:T(8,128)(2,1)} %reshape.819, f32[1024,3072]{1,0:T(8,128)} %get-tuple-element.327, f32[3072]{0:T(1024)S(1)} %bitcast.689), kind=kOutput, calls=%fused_computation.2 | convolution fusion | flops 4885312512 | bytes 37773312 | tf_op jit(solution)/shard_map/dot_general | solution.py:62
  492.8 10.7 multiply_reduce_fusion.1
  503.5 12.4 %reshape.868 = bf16[1024,4,768]{2,1,0:T(4,128)(2,1)} reshape(bf16[1024,3072]{1,0:T(8,128)(2,1)} %get-tuple-element.332) | data formatting | bytes 12582912 | tf_op jit(solution)/shard_map/reshape | solution.py:195
  537.4 7.1 fusion.13
  548.6 5.0 copy.626
  558.0 7.8 fusion.10
  590.7 4.9 copy.622
  640.9 93.9 %shard_map.324 = (bf16[12,1024,64]{2,1,0:T(8,128)(2,1)}, bf16[12,1024,64]{2,1,0:T(8,128)(2,1)}, bf16[12,1024,64]{2,1,0:T(8,128)(2,1)}) custom-call(s32[12,1024,4]{2,1,0:T(8,128)} %bitcast.584, bf16[12,1024,64]{2,1,0:T(8,128)(2,1)} %bitcast.637, bf16[12,1024,64]{2,1,0:T(8,128)(2,1)} %bitcast.639, bf16[12,1024,64]{2,1,0:T(8,128)(2,1)} %bitcast.641, ...), custom_call_target="tpu_custom_call" | custom-call | flops 8053063680 | bytes 12582912 | tf_op jit(solution)/shard_map/pallas_call | solution.py:353
  766.7 6.8 all-to-all-done.7
  773.5 4.6 all-to-all-start.6
  815.3 4.7 all-to-all-start.5
  819.9 5.4 convolution_bitcast_fusion.1
  825.3 4.6 copy.646
  958.6 38.3 %collective-permute-done.41 = f32[8,144,128]{2,1,0:T(8,128)S(1)} collective-permute-done((f32[8,144,128]{2,1,0:T(8,128)S(1)}, f32[8,144,128]{2,1,0:T(8,128)S(1)}, u32[]{:S(2)}, u32[]{:S(2)}) %collective-permute-start.41) | collective-permute-done | bytes 589856 | tf_op jit(solution)/shard_map/ppermute | solution.py:150
  997.4 6.0 collective-permute-done.36
  1004.7 39.3 %collective-permute-done.42 = f32[4,144,128]{2,1,0:T(8,128)S(1)} collective-permute-done((f32[4,144,128]{2,1,0:T(8,128)S(1)}, f32[4,144,128]{2,1,0:T(8,128)S(1)}, u32[]{:S(2)}, u32[]{:S(2)}) %collective-permute-start.42) | collective-permute-done | bytes 294944 | tf_op jit(solution)/shard_map/ppermute | solution.py:150
  1046.2 7.1 collective-permute-done.32
  1087.0 8.1 collective-permute-done.57
  1101.0 4.9 collective-permute-done.47
  1113.9 4.7 collective-permute-done.48
  1121.9 8.2 collective-permute-done.59
  (785 shorter events, 659.7 us)
Async XLA Ops:
  10.1 40.0 %collective-permute-start.15 = (bf16[1,440,128]{2,1,0:T(8,128)(2,1)S(1)}, bf16[1,440,128]{2,1,0:T(8,128)(2,1)S(1)}, u32[]{:S(2)}, u32[]{:S(2)}) collective-permute-start(bf16[1,440,128]{2,1,0:T(8,128)(2,1)S(1)} %bitcast.667), channel_id=1, source_target_pairs={{0,4},{1,5},{2,6},{3,7},{4,0},{5,1},{6,2},{7,3},{8,12},{9,13},{10,... | collective-permute-start | bytes 337928 | tf_op jit(solution)/shard_map/ppermute | solution.py:135
  18.3 21.7 %collective-permute-start = (bf16[1,146,128]{2,0,1:T(2,128)(2,1)S(1)}, bf16[1,146,128]{2,0,1:T(2,128)(2,1)S(1)}, u32[]{:S(2)}, u32[]{:S(2)}) collective-permute-start(bf16[1,146,128]{2,0,1:T(2,128)(2,1)S(1)} %pad_bitcast_fusion), channel_id=1, source_target_pairs={{0,4},{1,5},{2,6},{3,7},{4,0},{5,1},{6,2},{7,3},{8,12},{9,13},{10,... | collective-permute-start | bytes 112136 | tf_op jit(solution)/shard_map/ppermute | solution.py:135
  22.5 24.1 %collective-permute-start.25 = (bf16[1,432,128]{2,1,0:T(8,128)(2,1)S(1)}, bf16[1,432,128]{2,1,0:T(8,128)(2,1)S(1)}, u32[]{:S(2)}, u32[]{:S(2)}) collective-permute-start(bf16[1,432,128]{2,1,0:T(8,128)(2,1)S(1)} %maximum_bitcast_fusion.10), channel_id=1, source_target_pairs={{0,4},{1,5},{2,6},{3,7},{4,0},{5,1},{6,2},{7,3},{8,12},{9,13},{10,... | collective-permute-start | bytes 331784 | tf_op jit(solution)/shard_map/ppermute | solution.py:135
  61.3 37.5 %collective-permute-start.27 = (bf16[4,432,128]{2,1,0:T(8,128)(2,1)}, bf16[4,432,128]{2,1,0:T(8,128)(2,1)}, u32[]{:S(2)}, u32[]{:S(2)}) collective-permute-start(bf16[4,432,128]{2,1,0:T(8,128)(2,1)} %pad_maximum_fusion.18), channel_id=1, source_target_pairs={{0,16},{8,24},{16,0},{24,8},{1,17},{9,25},{17,1},{25,9},{2,18},{10... | collective-permute-start | bytes 1327112 | tf_op jit(solution)/shard_map/ppermute | solution.py:135
  63.2 38.2 %collective-permute-start.22 = (bf16[4,432,128]{2,1,0:T(8,128)(2,1)}, bf16[4,432,128]{2,1,0:T(8,128)(2,1)}, u32[]{:S(2)}, u32[]{:S(2)}) collective-permute-start(bf16[4,432,128]{2,1,0:T(8,128)(2,1)} %pad_maximum_fusion.17), channel_id=1, source_target_pairs={{0,2},{1,3},{2,0},{3,1},{4,6},{5,7},{6,4},{7,5},{8,10},{9,11},{10,... | collective-permute-start | bytes 1327112 | tf_op jit(solution)/shard_map/ppermute | solution.py:135
  66.5 69.3 %collective-permute-start.17 = (bf16[4,440,128]{2,1,0:T(8,128)(2,1)}, bf16[4,440,128]{2,1,0:T(8,128)(2,1)}, u32[]{:S(2)}, u32[]{:S(2)}) collective-permute-start(bf16[4,440,128]{2,1,0:T(8,128)(2,1)} %pad_maximum_fusion.16), channel_id=1, source_target_pairs={{0,1},{1,0},{2,3},{3,2},{4,5},{5,4},{6,7},{7,6},{8,9},{9,8},{10,11... | collective-permute-start | bytes 1351688 | tf_op jit(solution)/shard_map/ppermute | solution.py:135
  95.2 35.8 %all-to-all-start = ((bf16[4,256,4,192]{1,3,0,2:T(8,128)(2,1)}), bf16[4,256,4,192]{1,3,0,2:T(8,128)(2,1)S(1)}, u32[]{:S(2)}, u32[]{:S(2)}) async-start(bf16[4,256,4,192]{1,3,0,2:T(8,128)(2,1)} %copy.545), calls=%async_computation | async-start | bytes 3145728 | tf_op jit(solution)/shard_map/all_to_all | solution.py:443
  101.3 54.6 %collective-permute-start.28 = (bf16[8,432,128]{2,1,0:T(8,128)(2,1)}, bf16[8,432,128]{2,1,0:T(8,128)(2,1)}, u32[]{:S(2)}, u32[]{:S(2)}) collective-permute-start(bf16[8,432,128]{2,1,0:T(8,128)(2,1)} %pad_maximum_fusion.12), channel_id=1, source_target_pairs={{0,2},{1,3},{2,0},{3,1},{4,6},{5,7},{6,4},{7,5},{8,10},{9,11},{10,... | collective-permute-start | bytes 2654216 | tf_op jit(solution)/shard_map/ppermute | solution.py:135
  104.4 69.4 %collective-permute-start.23 = (bf16[8,432,128]{2,1,0:T(8,128)(2,1)}, bf16[8,432,128]{2,1,0:T(8,128)(2,1)}, u32[]{:S(2)}, u32[]{:S(2)}) collective-permute-start(bf16[8,432,128]{2,1,0:T(8,128)(2,1)} %pad_maximum_fusion.11), channel_id=1, source_target_pairs={{0,1},{1,0},{2,3},{3,2},{4,5},{5,4},{6,7},{7,6},{8,9},{9,8},{10,11... | collective-permute-start | bytes 2654216 | tf_op jit(solution)/shard_map/ppermute | solution.py:135
  131.1 38.1 %all-to-all-start.1 = ((bf16[4,256,4,192]{1,3,0,2:T(8,128)(2,1)}), bf16[4,256,4,192]{1,3,0,2:T(8,128)(2,1)}, u32[]{:S(2)}, u32[]{:S(2)}) async-start(bf16[4,256,4,192]{1,3,0,2:T(8,128)(2,1)} %copy.549), calls=%async_computation.1 | async-start | bytes 3145728 | tf_op jit(solution)/shard_map/all_to_all | solution.py:444
  138.2 56.0 %collective-permute-start.18 = (bf16[8,440,128]{2,1,0:T(8,128)(2,1)}, bf16[8,440,128]{2,1,0:T(8,128)(2,1)}, u32[]{:S(2)}, u32[]{:S(2)}) collective-permute-start(bf16[8,440,128]{2,1,0:T(8,128)(2,1)} %pad_maximum_fusion.10), channel_id=1, source_target_pairs={{0,16},{8,24},{16,0},{24,8},{1,17},{9,25},{17,1},{25,9},{2,18},{10... | collective-permute-start | bytes 2703368 | tf_op jit(solution)/shard_map/ppermute | solution.py:135
  159.7 162.0 %collective-permute-start.29 = (bf16[16,432,128]{2,1,0:T(8,128)(2,1)}, bf16[16,432,128]{2,1,0:T(8,128)(2,1)}, u32[]{:S(2)}, u32[]{:S(2)}) collective-permute-start(bf16[16,432,128]{2,1,0:T(8,128)(2,1)} %pad_maximum_fusion.6), channel_id=1, source_target_pairs={{0,8},{8,0},{16,24},{24,16},{1,9},{9,1},{17,25},{25,17},{2,10},{10... | collective-permute-start | bytes 5308424 | tf_op jit(solution)/shard_map/ppermute | solution.py:135
  169.2 50.0 %all-to-all-start.2 = ((bf16[4,256,4,192]{1,3,0,2:T(8,128)(2,1)}), bf16[4,256,4,192]{1,3,0,2:T(8,128)(2,1)}, u32[]{:S(2)}, u32[]{:S(2)}) async-start(bf16[4,256,4,192]{1,3,0,2:T(8,128)(2,1)} %copy.553), calls=%async_computation.2 | async-start | bytes 3145728 | tf_op jit(solution)/shard_map/all_to_all | solution.py:445
  177.5 147.9 %collective-permute-start.24 = (bf16[16,432,128]{2,1,0:T(8,128)(2,1)}, bf16[16,432,128]{2,1,0:T(8,128)(2,1)}, u32[]{:S(2)}, u32[]{:S(2)}) collective-permute-start(bf16[16,432,128]{2,1,0:T(8,128)(2,1)} %pad_maximum_fusion.5), channel_id=1, source_target_pairs={{0,8},{8,0},{16,24},{24,16},{1,9},{9,1},{17,25},{25,17},{2,10},{10... | collective-permute-start | bytes 5308424 | tf_op jit(solution)/shard_map/ppermute | solution.py:135
  197.2 160.0 %collective-permute-start.19 = (bf16[16,440,128]{2,1,0:T(8,128)(2,1)}, bf16[16,440,128]{2,1,0:T(8,128)(2,1)}, u32[]{:S(2)}, u32[]{:S(2)}) collective-permute-start(bf16[16,440,128]{2,1,0:T(8,128)(2,1)} %pad_maximum_fusion.4), channel_id=1, source_target_pairs={{0,8},{8,0},{16,24},{24,16},{1,9},{9,1},{17,25},{25,17},{2,10},{10... | collective-permute-start | bytes 5406728 | tf_op jit(solution)/shard_map/ppermute | solution.py:135
  317.1 97.2 %all-to-all-start.3 = ((bf16[4,1024,1,192]{3,0,2,1:T(4,128)(2,1)}), bf16[4,1024,1,192]{3,0,2,1:T(4,128)(2,1)}, u32[]{:S(2)}, u32[]{:S(2)}) async-start(bf16[4,1024,1,192]{3,0,2,1:T(4,128)(2,1)} %copy.557), calls=%async_computation.3 | async-start | bytes 4194304 | tf_op jit(solution)/shard_map/all_to_all | solution.py:463
  533.0 96.1 %all-to-all-start.4 = ((bf16[4,256,4,192]{1,0,3,2:T(4,128)(2,1)}), bf16[4,256,4,192]{1,0,3,2:T(4,128)(2,1)}, u32[]{:S(2)}, u32[]{:S(2)}) async-start(bf16[4,256,4,192]{1,0,3,2:T(4,128)(2,1)} %reshape.824), calls=%async_computation.4 | async-start | bytes 3145728 | tf_op jit(solution)/shard_map/all_to_all | solution.py:508
  590.2 347.6 %collective-permute-start.55 = (f32[16,432,128]{2,1,0:T(8,128)}, f32[16,432,128]{2,1,0:T(8,128)}, u32[]{:S(2)}, u32[]{:S(2)}) collective-permute-start(f32[16,432,128]{2,1,0:T(8,128)} %dynamic-slice_bitcast_fusion.1), channel_id=1, source_target_pairs={{0,8},{8,0},{16,24},{24,16},{1,9},{9,1},{17,25},{25,17},{2,10},{10... | collective-permute-start | bytes 10616840 | tf_op jit(solution)/shard_map/ppermute | solution.py:150
  618.9 324.3 %collective-permute-start.50 = (f32[16,432,128]{2,1,0:T(8,128)}, f32[16,432,128]{2,1,0:T(8,128)}, u32[]{:S(2)}, u32[]{:S(2)}) collective-permute-start(f32[16,432,128]{2,1,0:T(8,128)} %dynamic-slice_bitcast_fusion.2), channel_id=1, source_target_pairs={{0,8},{8,0},{16,24},{24,16},{1,9},{9,1},{17,25},{25,17},{2,10},{10... | collective-permute-start | bytes 10616840 | tf_op jit(solution)/shard_map/ppermute | solution.py:150
  743.3 30.2 %all-to-all-start.7 = ((bf16[4,1024,1,192]{3,0,2,1:T(4,128)(2,1)}), bf16[4,1024,1,192]{3,0,2,1:T(4,128)(2,1)}, u32[]{:S(2)}, u32[]{:S(2)}) async-start(bf16[4,1024,1,192]{3,0,2,1:T(4,128)(2,1)} %copy.589), calls=%async_computation.7 | async-start | bytes 4194304 | tf_op jit(solution)/shard_map/all_to_all | solution.py:522
  773.5 41.8 %all-to-all-start.6 = ((bf16[4,1024,1,192]{3,0,2,1:T(4,128)(2,1)}), bf16[4,1024,1,192]{3,0,2,1:T(4,128)(2,1)}, u32[]{:S(2)}, u32[]{:S(2)}) async-start(bf16[4,1024,1,192]{3,0,2,1:T(4,128)(2,1)} %copy.584), calls=%async_computation.6 | async-start | bytes 4194304 | tf_op jit(solution)/shard_map/all_to_all | solution.py:521
  801.3 153.9 %collective-permute-start.45 = (f32[16,440,128]{2,1,0:T(8,128)}, f32[16,440,128]{2,1,0:T(8,128)}, u32[]{:S(2)}, u32[]{:S(2)}) collective-permute-start(f32[16,440,128]{2,1,0:T(8,128)} %dynamic-slice_bitcast_fusion), channel_id=1, source_target_pairs={{0,8},{8,0},{16,24},{24,16},{1,9},{9,1},{17,25},{25,17},{2,10},{10... | collective-permute-start | bytes 10813448 | tf_op jit(solution)/shard_map/ppermute | solution.py:150
  815.3 30.4 %all-to-all-start.5 = ((bf16[4,1024,1,192]{3,0,2,1:T(4,128)(2,1)}), bf16[4,1024,1,192]{3,0,2,1:T(4,128)(2,1)}, u32[]{:S(2)}, u32[]{:S(2)}) async-start(bf16[4,1024,1,192]{3,0,2,1:T(4,128)(2,1)} %copy.579), calls=%async_computation.5 | async-start | bytes 4194304 | tf_op jit(solution)/shard_map/all_to_all | solution.py:520
  883.1 65.3 %collective-permute-start.40 = (f32[16,144,128]{2,1,0:T(8,128)}, f32[16,144,128]{2,1,0:T(8,128)}, u32[]{:S(2)}, u32[]{:S(2)}) collective-permute-start(f32[16,144,128]{2,1,0:T(8,128)} %dynamic-slice_bitcast_fusion.7), channel_id=1, source_target_pairs={{0,8},{8,0},{16,24},{24,16},{1,9},{9,1},{17,25},{25,17},{2,10},{10... | collective-permute-start | bytes 3538952 | tf_op jit(solution)/shard_map/ppermute | solution.py:150
  943.2 129.8 %collective-permute-start.56 = (f32[8,432,128]{2,1,0:T(8,128)}, f32[8,432,128]{2,1,0:T(8,128)}, u32[]{:S(2)}, u32[]{:S(2)}) collective-permute-start(f32[8,432,128]{2,1,0:T(8,128)} %dynamic-slice_bitcast_fusion.4), channel_id=1, source_target_pairs={{0,2},{1,3},{2,0},{3,1},{4,6},{5,7},{6,4},{7,5},{8,10},{9,11},{10,... | collective-permute-start | bytes 5308424 | tf_op jit(solution)/shard_map/ppermute | solution.py:150
  949.7 129.1 %collective-permute-start.51 = (f32[8,432,128]{2,1,0:T(8,128)}, f32[8,432,128]{2,1,0:T(8,128)}, u32[]{:S(2)}, u32[]{:S(2)}) collective-permute-start(f32[8,432,128]{2,1,0:T(8,128)} %dynamic-slice_bitcast_fusion.5), channel_id=1, source_target_pairs={{0,1},{1,0},{2,3},{3,2},{4,5},{5,4},{6,7},{7,6},{8,9},{9,8},{10,11... | collective-permute-start | bytes 5308424 | tf_op jit(solution)/shard_map/ppermute | solution.py:150
  953.3 43.6 %collective-permute-start.41 = (f32[8,144,128]{2,1,0:T(8,128)S(1)}, f32[8,144,128]{2,1,0:T(8,128)S(1)}, u32[]{:S(2)}, u32[]{:S(2)}) collective-permute-start(f32[8,144,128]{2,1,0:T(8,128)S(1)} %dynamic-slice_bitcast_fusion.13), channel_id=1, source_target_pairs={{0,2},{1,3},{2,0},{3,1},{4,6},{5,7},{6,4},{7,5},{8,10},{9,11},{10,... | collective-permute-start | bytes 1769480 | tf_op jit(solution)/shard_map/ppermute | solution.py:150
  953.9 49.5 %collective-permute-start.36 = (f32[8,144,128]{2,1,0:T(8,128)S(1)}, f32[8,144,128]{2,1,0:T(8,128)S(1)}, u32[]{:S(2)}, u32[]{:S(2)}) collective-permute-start(f32[8,144,128]{2,1,0:T(8,128)S(1)} %dynamic-slice_bitcast_fusion.14), channel_id=1, source_target_pairs={{0,1},{1,0},{2,3},{3,2},{4,5},{5,4},{6,7},{7,6},{8,9},{9,8},{10,11... | collective-permute-start | bytes 1769480 | tf_op jit(solution)/shard_map/ppermute | solution.py:150
  955.2 48.7 %collective-permute-start.31 = (f32[8,146,128]{2,0,1:T(8,128)S(1)}, f32[8,146,128]{2,0,1:T(8,128)S(1)}, u32[]{:S(2)}, u32[]{:S(2)}) collective-permute-start(f32[8,146,128]{2,0,1:T(8,128)S(1)} %dynamic-slice_bitcast_fusion.12), channel_id=1, source_target_pairs={{0,16},{8,24},{16,0},{24,8},{1,17},{9,25},{17,1},{25,9},{2,18},{10... | collective-permute-start | bytes 1794056 | tf_op jit(solution)/shard_map/ppermute | solution.py:150
  996.9 84.6 %collective-permute-start.46 = (f32[8,440,128]{2,1,0:T(8,128)S(1)}, f32[8,440,128]{2,1,0:T(8,128)}, u32[]{:S(2)}, u32[]{:S(2)}) collective-permute-start(f32[8,440,128]{2,1,0:T(8,128)S(1)} %dynamic-slice_bitcast_fusion.3), channel_id=1, source_target_pairs={{0,16},{8,24},{16,0},{24,8},{1,17},{9,25},{17,1},{25,9},{2,18},{10... | collective-permute-start | bytes 5406728 | tf_op jit(solution)/shard_map/ppermute | solution.py:150
  1003.4 40.6 %collective-permute-start.42 = (f32[4,144,128]{2,1,0:T(8,128)S(1)}, f32[4,144,128]{2,1,0:T(8,128)S(1)}, u32[]{:S(2)}, u32[]{:S(2)}) collective-permute-start(f32[4,144,128]{2,1,0:T(8,128)S(1)} %dynamic-slice_bitcast_fusion.19), channel_id=1, source_target_pairs={{0,16},{8,24},{16,0},{24,8},{1,17},{9,25},{17,1},{25,9},{2,18},{10... | collective-permute-start | bytes 884744 | tf_op jit(solution)/shard_map/ppermute | solution.py:150
  1003.9 41.8 %collective-permute-start.37 = (f32[4,144,128]{2,1,0:T(8,128)S(1)}, f32[4,144,128]{2,1,0:T(8,128)S(1)}, u32[]{:S(2)}, u32[]{:S(2)}) collective-permute-start(f32[4,144,128]{2,1,0:T(8,128)S(1)} %dynamic-slice_bitcast_fusion.20), channel_id=1, source_target_pairs={{0,2},{1,3},{2,0},{3,1},{4,6},{5,7},{6,4},{7,5},{8,10},{9,11},{10,... | collective-permute-start | bytes 884744 | tf_op jit(solution)/shard_map/ppermute | solution.py:150
  (133 other events, 1025.9 us)

commit v4 on v3

v4 whole, which is shorter than its diff:
```python
from functools import partial

import jax
import jax.numpy as jnp
from jax import lax
from jax.experimental import pallas as pl
from jax.experimental.pallas import tpu as pltpu
from jax.sharding import PartitionSpec as P

H = 12
HD = 64
BLK = 64
NGLOB = 2
LEN = 1024
QB = 512


def layer_norm(hidden, gain, shift):
    mean_value = jnp.mean(hidden, axis=-1, keepdims=True)
    centered = hidden - mean_value
    spread = jnp.mean(centered * centered, axis=-1, keepdims=True)
    return centered * lax.rsqrt(spread + 1e-06) * gain + shift


def segment_inside(segment_row):
    places = jnp.arange(segment_row.shape[0], dtype=jnp.int32)
    begins = jnp.concatenate([jnp.ones((1,), dtype=jnp.bool_), segment_row[1:] != segment_row[:-1]])
    firsts = lax.cummax(jnp.where(begins, places, 0), axis=0)
    return places - firsts


def times_back(left, matrix):
    return lax.dot_general(
        left, matrix, (((1,), (1,)), ((), ())), preferred_element_type=jnp.float32
    )


def axis_bits(axis):
    size = lax.axis_size(axis)
    bits = size.bit_length() - 1
    assert 1 << bits == size
    return [(axis, b) for b in range(bits)]


def canonical_bits():
    return [("dp", b) for b in reversed(range(len(axis_bits("dp"))))] + [
        ("seq", b) for b in reversed(range(len(axis_bits("seq"))))
    ]


def bit_orders(n_parts):
    seq_bits, dp_bits = axis_bits("seq"), axis_bits("dp")
    first, last = seq_bits[:1], dp_bits[-1:]
    middle = seq_bits[1:] + dp_bits[:-1]
    orders = []
    for part in range(n_parts):
        shift = (part * len(middle)) // n_parts if middle else 0
        orders.append(first + middle[shift:] + middle[:shift] + last)
    return orders


def my_bit(bit):
    axis, b = bit
    return (lax.axis_index(axis) >> b) & 1


def partner(bit):
    axis, b = bit
    return [(i, i ^ (1 << b)) for i in range(lax.axis_size(axis))]


N_PARTS = 3
LANES = 128


def to_order(blocked, order):
    canon = canonical_bits()
    rest = blocked.shape[1:]
    x = blocked.reshape([2] * len(canon) + list(rest))
    perm = [canon.index(bit) for bit in order] + list(range(len(canon), len(canon) + len(rest)))
    return x.transpose(perm).reshape(blocked.shape)


def from_order(blocked, order):
    canon = canonical_bits()
    rest = blocked.shape[1:]
    x = blocked.reshape([2] * len(canon) + list(rest))
    perm = [order.index(bit) for bit in canon] + list(range(len(canon), len(canon) + len(rest)))
    return x.transpose(perm).reshape(blocked.shape)


def lane_rows(flat_blocks):
    n, width = flat_blocks.shape
    rows = -(-width // LANES)
    pad = rows * LANES - width
    if pad:
        flat_blocks = jnp.concatenate([flat_blocks, jnp.zeros((n, pad), flat_blocks.dtype)], axis=1)
    return flat_blocks.reshape(n, rows, LANES)


def gather_parts(parts, orders):
    out = []
    for buf, order in zip(parts, orders):
        buf = buf[None]
        for bit in reversed(order):
            got = lax.ppermute(buf, bit[0], partner(bit))
            mine = my_bit(bit) == 0
            buf = jnp.concatenate([jnp.where(mine, buf, got), jnp.where(mine, got, buf)], axis=0)
        out.append(buf)
    return out


def reduce_parts(parts, orders):
    out = []
    for buf, order in zip(parts, orders):
        for bit in order:
            half = buf.reshape((2, buf.shape[0] // 2) + buf.shape[1:])
            mine = my_bit(bit)
            keep = lax.dynamic_index_in_dim(half, mine, 0, keepdims=False)
            send = lax.dynamic_index_in_dim(half, 1 - mine, 0, keepdims=False)
            buf = keep + lax.ppermute(send, bit[0], partner(bit))
        out.append(buf[0])
    return out


def gather_weights(matrices, vectors):
    n_dp, n_seq = lax.axis_size("dp"), lax.axis_size("seq")
    orders = bit_orders(N_PARTS)
    parts, layout = [], []
    for part in range(N_PARTS):
        items = []
        for m in matrices:
            third = m.shape[0] // N_PARTS
            items.append(m[part * third:(part + 1) * third].reshape(-1))
        if part == 0:
            items += [v.reshape(-1) for v in vectors]
        sizes = [item.size for item in items]
        parts.append(lane_rows(jnp.concatenate(items)[None])[0])
        layout.append(sizes)
    got = gather_parts(parts, orders)
    canon = []
    for buf, order, sizes in zip(got, orders, layout):
        flat = from_order(buf, order).reshape(n_dp * n_seq, -1)
        pieces, offset = [], 0
        for size in sizes:
            pieces.append(flat[:, offset:offset + size])
            offset += size
        canon.append(pieces)
    full = []
    for index, m in enumerate(matrices):
        third = m.shape[0] // N_PARTS
        stacked = jnp.stack(
            [canon[part][index].reshape(n_dp, n_seq, third, m.shape[1]) for part in range(N_PARTS)], axis=2
        )
        full.append(stacked.transpose(0, 2, 3, 1, 4).reshape(n_dp * m.shape[0], n_seq * m.shape[1]))
    vecs = []
    for index, v in enumerate(vectors):
        piece = canon[0][len(matrices) + index]
        vecs.append(piece.reshape(n_dp, n_seq, v.size)[:, 0].reshape(-1))
    return full, vecs


def blocked_grad(left, right, n_dp, n_seq):
    tokens = left.shape[0]
    a = left.reshape(tokens, n_dp, left.shape[1] // n_dp)
    b = right.reshape(tokens, n_seq, right.shape[1] // n_seq)
    return jnp.einsum("tar,tbc->abrc", a, b, preferred_element_type=jnp.float32)


def reduce_grads(matrices, vectors):
    n_dp, n_seq = lax.axis_size("dp"), lax.axis_size("seq")
    orders = bit_orders(N_PARTS)
    parts, layout = [], []
    for part in range(N_PARTS):
        items = []
        for m in matrices:
            third = m.shape[2] // N_PARTS
            items.append(m[:, :, part * third:(part + 1) * third].reshape(n_dp * n_seq, -1))
        if part == 0:
            for v in vectors:
                v = v.reshape(n_dp, 1, -1)
                items.append(jnp.broadcast_to(v, (n_dp, n_seq, v.shape[-1])).reshape(n_dp * n_seq, -1))
        sizes = [item.shape[1] for item in items]
        parts.append(to_order(lane_rows(jnp.concatenate(items, axis=1)), orders[part]))
        layout.append(sizes)
    summed = reduce_parts(parts, orders)
    pieces_by_part = []
    for buf, sizes in zip(summed, layout):
        flat = buf.reshape(-1)
        pieces, offset = [], 0
        for size in sizes:
            pieces.append(flat[offset:offset + size])
            offset += size
        pieces_by_part.append(pieces)
    own = []
    for index, m in enumerate(matrices):
        third = m.shape[2] // N_PARTS
        own.append(
            jnp.concatenate(
                [pieces_by_part[part][index].reshape(third, m.shape[3]) for part in range(N_PARTS)], axis=0
            )
        )
    vecs = [pieces_by_part[0][len(matrices) + index] for index in range(len(vectors))]
    return own, vecs


TQ = 256
SCALE = HD ** (-0.5)
PAIR = 2 * HD


def row_bounds(segment_row, pad_row):
    length = segment_row.shape[0]
    places = jnp.arange(length, dtype=jnp.int32)
    inside = segment_inside(segment_row)
    lo = places - inside
    ends = jnp.concatenate([segment_row[1:] != segment_row[:-1], jnp.ones((1,), dtype=jnp.bool_)])
    hi = lax.cummin(jnp.where(ends, places + 1, length), axis=0, reverse=True)
    hi = jnp.where(pad_row == 1, hi, lo)
    glim = jnp.where(inside < NGLOB * BLK, length, lo + NGLOB * BLK)
    return jnp.stack([lo, hi, glim], axis=-1)


def block_bits(random_blocks, length):
    n_blocks = length // BLK
    assert n_blocks <= 31
    key_block = jnp.arange(n_blocks, dtype=jnp.int32)
    near = jnp.abs(key_block[:, None] - key_block[None, :]) <= 1
    picked = jnp.any(random_blocks[:, :, :, None] == key_block[None, None, None, :], axis=2)
    chosen = near[None] | picked
    bits = jnp.sum(jnp.where(chosen, jnp.left_shift(1, key_block)[None, None, :], 0), axis=2).astype(jnp.int32)
    return jnp.repeat(bits, BLK, axis=1)


def tile_masks(bounds, bits, row0, rows, length):
    lo = bounds[:, 0:1]
    hi = bounds[:, 1:2]
    glim = bounds[:, 2:3]
    col = lax.broadcasted_iota(jnp.int32, (rows, length), 1)
    row = row0 + lax.broadcasted_iota(jnp.int32, (rows, length), 0)
    inside = (col >= lo) & (col < hi)
    glob = col < glim
    diag = col == row
    block = col // BLK
    out = []
    for j in range(bits.shape[1]):
        picked = (lax.shift_right_logical(bits[:, j:j + 1], block) & 1) == 1
        out.append((inside & (picked | glob)) | diag)
    return out


def attn_fwd_kernel(bounds_ref, bits_ref, q_ref, k_ref, v_ref, ctx_ref, lse_ref):
    rows = q_ref.shape[0]
    length = k_ref.shape[0]
    row0 = pl.program_id(2) * rows
    masks = tile_masks(bounds_ref[...], bits_ref[...], row0, rows, length)
    q = q_ref[...]
    k = k_ref[...]
    v = v_ref[...]
    outs = []
    for j, allowed in enumerate(masks):
        cols = slice(j * HD, (j + 1) * HD)
        s = lax.dot_general(
            q[:, cols], k[:, cols], (((1,), (1,)), ((), ())), preferred_element_type=jnp.float32
        ) * SCALE
        s = jnp.where(allowed, s, -1e30)
        top = jnp.max(s, axis=1, keepdims=True)
        w = jnp.exp(s - top)
        total = jnp.sum(w, axis=1, keepdims=True)
        probs = (w * (1.0 / total)).astype(jnp.bfloat16)
        outs.append(jnp.dot(probs, v[:, cols], preferred_element_type=jnp.float32))
        lse_ref[j] = top + jnp.log(total)
    ctx_ref[...] = jnp.concatenate(outs, axis=1).astype(ctx_ref.dtype)


def attn_bwd_kernel(bounds_ref, bits_ref, q_ref, k_ref, v_ref, do_ref, lse_ref, dq_ref, dk_ref, dv_ref, dk_acc, dv_acc):
    qi = pl.program_id(2)
    rows = q_ref.shape[0]
    length = k_ref.shape[0]

    @pl.when(qi == 0)
    def _():
        dk_acc[...] = jnp.zeros_like(dk_acc)
        dv_acc[...] = jnp.zeros_like(dv_acc)

    masks = tile_masks(bounds_ref[...], bits_ref[...], qi * rows, rows, length)
    q = q_ref[...]
    k = k_ref[...]
    v = v_ref[...]
    do = do_ref[...]
    dqs, dks, dvs = [], [], []
    for j, allowed in enumerate(masks):
        cols = slice(j * HD, (j + 1) * HD)
        qj, kj, doj = q[:, cols], k[:, cols], do[:, cols]
        s = lax.dot_general(qj, kj, (((1,), (1,)), ((), ())), preferred_element_type=jnp.float32) * SCALE
        p = jnp.where(allowed, jnp.exp(s - lse_ref[j]), 0.0)
        dvs.append(
            lax.dot_general(p.astype(jnp.bfloat16), doj, (((0,), (0,)), ((), ())), preferred_element_type=jnp.float32)
        )
        dp = lax.dot_general(doj, v[:, cols], (((1,), (1,)), ((), ())), preferred_element_type=jnp.float32)
        inner = jnp.sum(p * dp, axis=1, keepdims=True)
        ds = (p * (dp - inner)).astype(jnp.bfloat16)
        dqs.append(jnp.dot(ds, kj, preferred_element_type=jnp.float32) * SCALE)
        dks.append(lax.dot_general(ds, qj, (((0,), (0,)), ((), ())), preferred_element_type=jnp.float32) * SCALE)
    dq_ref[...] = jnp.concatenate(dqs, axis=1).astype(dq_ref.dtype)
    dk_acc[...] += jnp.concatenate(dks, axis=1)
    dv_acc[...] += jnp.concatenate(dvs, axis=1)

    @pl.when(qi == pl.num_programs(2) - 1)
    def _():
        dk_ref[...] = dk_acc[...].astype(dk_ref.dtype)
        dv_ref[...] = dv_acc[...].astype(dv_ref.dtype)


def attn_specs(length, rows):
    row_spec = pl.BlockSpec((None, rows, PAIR), lambda b, h, i: (b, i, h))
    whole_spec = pl.BlockSpec((None, length, PAIR), lambda b, h, i: (b, 0, h))
    bounds_spec = pl.BlockSpec((None, rows, 3), lambda b, h, i: (b, i, 0))
    bits_spec = pl.BlockSpec((None, rows, 2), lambda b, h, i: (h, i, 0))
    lse_spec = pl.BlockSpec((None, 2, rows, 1), lambda b, h, i: (b, h, i, 0))
    return row_spec, whole_spec, bounds_spec, bits_spec, lse_spec


def attention_forward(bounds, bits, q, k, v):
    batch, length, width = q.shape
    rows = min(TQ, length)
    pairs = width // PAIR
    row_spec, whole_spec, bounds_spec, bits_spec, lse_spec = attn_specs(length, rows)
    return pl.pallas_call(
        attn_fwd_kernel,
        grid=(batch, pairs, length // rows),
        in_specs=[bounds_spec, bits_spec, row_spec, whole_spec, whole_spec],
        out_specs=[row_spec, lse_spec],
        out_shape=[
            jax.ShapeDtypeStruct((batch, length, width), jnp.bfloat16),
            jax.ShapeDtypeStruct((batch, 2 * pairs, length, 1), jnp.float32),
        ],
        compiler_params=pltpu.CompilerParams(dimension_semantics=("arbitrary", "arbitrary", "arbitrary")),
        cost_estimate=pl.CostEstimate(
            flops=4 * batch * length * length * width,
            transcendentals=batch * length * length * (width // HD),
            bytes_accessed=4 * batch * length * width * 2,
        ),
    )(bounds, bits, q, k, v)


def attention_backward(bounds, bits, q, k, v, do, lse):
    batch, length, width = q.shape
    rows = min(TQ, length)
    pairs = width // PAIR
    row_spec, whole_spec, bounds_spec, bits_spec, lse_spec = attn_specs(length, rows)
    return pl.pallas_call(
        attn_bwd_kernel,
        grid=(batch, pairs, length // rows),
        in_specs=[bounds_spec, bits_spec, row_spec, whole_spec, whole_spec, row_spec, lse_spec],
        out_specs=[row_spec, whole_spec, whole_spec],
        out_shape=[jax.ShapeDtypeStruct((batch, length, width), jnp.bfloat16)] * 3,
        scratch_shapes=[pltpu.VMEM((length, PAIR), jnp.float32), pltpu.VMEM((length, PAIR), jnp.float32)],
        compiler_params=pltpu.CompilerParams(dimension_semantics=("arbitrary", "arbitrary", "arbitrary")),
        cost_estimate=pl.CostEstimate(
            flops=10 * batch * length * length * width,
            transcendentals=batch * length * length * (width // HD),
            bytes_accessed=8 * batch * length * width * 2,
        ),
    )(bounds, bits, q, k, v, do, lse)


def times_back(left, matrix):
    return lax.dot_general(
        left, matrix, (((1,), (1,)), ((), ())), preferred_element_type=jnp.float32
    )


def shards(
    inputs,
    cotangent,
    segments,
    padding,
    random_blocks,
    w_query,
    b_query,
    w_key,
    w_value,
    b_value,
    w_out,
    b_out,
    gain_one,
    shift_one,
    w_up,
    b_up,
    w_down,
    b_down,
    gain_two,
    shift_two,
):
    n_seq = lax.axis_size("seq")
    n_dp = lax.axis_size("dp")
    seqs_here, shard_len, width = inputs.shape
    assert seqs_here % n_seq == 0
    mine = seqs_here // n_seq
    seq_len = shard_len * n_seq
    rows = mine * seq_len

    (full_query, full_key, full_value), (g_b_query, g_b_value) = gather_weights(
        [w_query, w_key, w_value], [b_query, b_value]
    )
    (full_out, full_up, full_down), (
        g_b_out, g_gain_one, g_shift_one, g_b_up, g_b_down, g_gain_two, g_shift_two,
    ) = gather_weights([w_out, w_up, w_down], [b_out, gain_one, shift_one, b_up, b_down, gain_two, shift_two])
    (
        vec_query, vec_value, vec_out, vec_gain_one, vec_shift_one, vec_up, vec_down, vec_gain_two, vec_shift_two,
    ) = [
        item.astype(jnp.float32)
        for item in (g_b_query, g_b_value, g_b_out, g_gain_one, g_shift_one, g_b_up, g_b_down, g_gain_two, g_shift_two)
    ]

    def whole_sequences(array):
        return lax.all_to_all(array, "seq", split_axis=0, concat_axis=1, tiled=True)

    def token_owners(array):
        return lax.all_to_all(array, "seq", split_axis=1, concat_axis=0, tiled=True)

    seq_inputs = whole_sequences(inputs)
    seq_cot = whole_sequences(cotangent)
    first = lax.axis_index("seq") * mine
    my_segments = lax.dynamic_slice_in_dim(segments, first, mine, 0)
    my_padding = lax.dynamic_slice_in_dim(padding, first, mine, 0)
    bounds = jax.vmap(row_bounds)(my_segments, my_padding)
    bits = block_bits(random_blocks, seq_len)
    bits = bits.reshape(H // 2, 2, seq_len).transpose(0, 2, 1)

    flat = seq_inputs.reshape(rows, width)
    queries = (jnp.dot(flat, full_query, preferred_element_type=jnp.float32) + vec_query).astype(jnp.bfloat16)
    keys = jnp.dot(flat, full_key, preferred_element_type=jnp.float32).astype(jnp.bfloat16)
    values = (jnp.dot(flat, full_value, preferred_element_type=jnp.float32) + vec_value).astype(jnp.bfloat16)

    def by_seq(array):
        return array.reshape(mine, seq_len, width)

    context, lse = attention_forward(bounds, bits, by_seq(queries), by_seq(keys), by_seq(values))
    context_tok = context.reshape(rows, width)
    hidden = (
        flat.astype(jnp.float32)
        + jnp.dot(context_tok, full_out, preferred_element_type=jnp.float32)
        + vec_out
    )
    normed = layer_norm(hidden, vec_gain_one, vec_shift_one)
    normed_low = normed.astype(jnp.bfloat16)
    upper = jnp.dot(normed_low, full_up, preferred_element_type=jnp.float32) + vec_up
    gelu_value, gelu_back = jax.vjp(partial(jax.nn.gelu, approximate=False), upper)
    active = gelu_value.astype(jnp.bfloat16)
    mixed = normed + jnp.dot(active, full_down, preferred_element_type=jnp.float32) + vec_down
    output = layer_norm(mixed, vec_gain_two, vec_shift_two).astype(jnp.bfloat16)
    out_tokens = token_owners(output.reshape(mine, seq_len, width))

    grad_out = seq_cot.reshape(rows, width).astype(jnp.float32)
    norm_two_back = jax.vjp(layer_norm, mixed, vec_gain_two, vec_shift_two)[1]
    grad_mixed, grad_gain_two, grad_shift_two = norm_two_back(grad_out)
    grad_lower = grad_mixed.astype(jnp.bfloat16)
    grad_b_down = jnp.sum(grad_lower.astype(jnp.float32), axis=0)
    grad_w_down = blocked_grad(active, grad_lower, n_dp, n_seq)
    grad_upper = gelu_back(times_back(grad_lower, full_down))[0].astype(jnp.bfloat16)
    grad_b_up = jnp.sum(grad_upper.astype(jnp.float32), axis=0)
    grad_w_up = blocked_grad(normed_low, grad_upper, n_dp, n_seq)
    grad_normed = grad_mixed + times_back(grad_upper, full_up)
    norm_one_back = jax.vjp(layer_norm, hidden, vec_gain_one, vec_shift_one)[1]
    grad_hidden, grad_gain_one, grad_shift_one = norm_one_back(grad_normed)
    grad_branch = grad_hidden.astype(jnp.bfloat16)
    grad_b_out = jnp.sum(grad_branch.astype(jnp.float32), axis=0)
    grad_w_out = blocked_grad(context_tok, grad_branch, n_dp, n_seq)
    (own_w_out, own_w_up, own_w_down), (
        own_b_out, own_gain_one, own_shift_one, own_b_up, own_b_down, own_gain_two, own_shift_two,
    ) = reduce_grads(
        [grad_w_out, grad_w_up, grad_w_down],
        [grad_b_out, grad_gain_one, grad_shift_one, grad_b_up, grad_b_down, grad_gain_two, grad_shift_two],
    )
    grad_context = times_back(grad_branch, full_out).astype(jnp.bfloat16)
    grad_q, grad_k, grad_v = attention_backward(
        bounds, bits, by_seq(queries), by_seq(keys), by_seq(values), by_seq(grad_context), lse
    )
    grad_q, grad_k, grad_v = (
        grad_q.reshape(rows, width),
        grad_k.reshape(rows, width),
        grad_v.reshape(rows, width),
    )
    grad_inputs = (
        grad_hidden
        + times_back(grad_q, full_query)
        + times_back(grad_k, full_key)
        + times_back(grad_v, full_value)
    )
    grad_tokens = token_owners(grad_inputs.reshape(mine, seq_len, width))
    grad_w_query = blocked_grad(flat, grad_q, n_dp, n_seq)
    grad_b_query = jnp.sum(grad_q.astype(jnp.float32), axis=0)
    grad_w_key = blocked_grad(flat, grad_k, n_dp, n_seq)
    grad_w_value = blocked_grad(flat, grad_v, n_dp, n_seq)
    grad_b_value = jnp.sum(grad_v.astype(jnp.float32), axis=0)
    (own_w_query, own_w_key, own_w_value), (own_b_query, own_b_value) = reduce_grads(
        [grad_w_query, grad_w_key, grad_w_value], [grad_b_query, grad_b_value]
    )
    return (
        out_tokens,
        grad_tokens,
        own_w_query,
        own_b_query,
        own_w_key,
        own_w_value,
        own_b_value,
        own_w_out,
        own_b_out,
        own_gain_one,
        own_shift_one,
        own_w_up,
        own_b_up,
        own_w_down,
        own_b_down,
        own_gain_two,
        own_shift_two,
    )


def solution(mesh):
    return jax.shard_map(
        shards,
        mesh=mesh,
        in_specs=(
            P("dp", "seq", None),
            P("dp", "seq", None),
            P("dp", None),
            P("dp", None),
            P(),
            P("dp", "seq"),
            P("dp"),
            P("dp", "seq"),
            P("dp", "seq"),
            P("dp"),
            P("dp", "seq"),
            P("dp"),
            P("dp"),
            P("dp"),
            P("dp", "seq"),
            P("dp"),
            P("dp", "seq"),
            P("dp"),
            P("dp"),
            P("dp"),
        ),
        out_specs=(
            P("dp", "seq", None),
            P("dp", "seq", None),
            P("dp", "seq"),
            P("dp"),
            P("dp", "seq"),
            P("dp", "seq"),
            P("dp"),
            P("dp", "seq"),
            P("dp"),
            P("dp"),
            P("dp"),
            P("dp", "seq"),
            P("dp"),
            P("dp", "seq"),
            P("dp"),
            P("dp"),
            P("dp"),
        ),
        check_vma=False,
    )
```

time: 1150 us -> 960 us (0.83)
  local copies, waits for them, and re-layouts: 492 us -> 353 us
  waiting for transfers between devices: 156 us -> 116 us
  matrix products: 118 us -> 131 us
  Pallas kernels: 172 us -> 159 us
  starting transfers between devices: 96 us -> 83.9 us
    reshape x21 -> x3, local copies, waits for them, and re-layouts: 68.3 us -> 18 us  [the longest x1 8.73 us: shards(): grad_tokens = token_owners(grad_inputs.reshape(mine, seq_len, width))]
    all_to_all x12 -> x1, local copies, waits for them, and re-layouts: 38.1 us -> 2.58 us  [whole_sequences(): return lax.all_to_all(array, 'seq', split_axis=0, concat_axis=1, tiled=True)]
    ppermute x30, waiting for transfers between devices: 138 us -> 105 us  [reduce_parts(): buf = keep + lax.ppermute(send, bit[0], partner(bit))]
    slice x24, local copies, waits for them, and re-layouts: 53.9 us -> 34.3 us  [reduce_grads(): m[:, :, part * third:(part + 1) * third].reshape(n_dp * n_seq, -1)]
    all_to_all x8 -> x4, starting transfers between devices: 35.6 us -> 17.4 us  [the longest x2 9.42 us: token_owners(): return lax.all_to_all(array, 'seq', split_axis=1, concat_axis=0, tiled=True)]
    transpose x4 -> x0, local copies, waits for them, and re-layouts: 16.6 us -> none  [to_bh(): array.transpose(0, 2, 1, 3).reshape(seqs_here * heads_here, seq_len, HD)]
    unnamed x230 -> x274, local copies, waits for them, and re-layouts: 80.6 us -> 67.1 us
    pallas_call x2, Pallas kernels: 172 us -> 159 us  [the longest x1 87.8 us: attention_backward(): pl.pallas_call(attn_bwd_kernel, grid=(batch, pairs, length // rows), in_s...]
  transfers between devices with their start and end apart: 68 -> 64, of which waited for: 26 -> 22; matrix products, arithmetic and copies ran while one was open for 50% -> 32% of each run, Pallas kernels for 15% -> 0%
where the time goes in v4:
time: 960 us; the launch traced here: 950 us
  local copies, waits for them, and re-layouts  353 us (37%)
  Pallas kernels  159 us (17%)
  matrix products  131 us (14%)
  waiting for transfers between devices  116 us (12%)
  other arithmetic  103 us (11%)
  starting transfers between devices  83.9 us (9%)
    ppermute x30, waiting for transfers between devices, reduce_parts(): buf = keep + lax.ppermute(send, bit[0], partner(bit))  105 us
    pallas_call x1, Pallas kernels, attention_backward(): pl.pallas_call(attn_bwd_kernel, grid=(batch, pairs, length // rows), in_s...  87.8 us
    pallas_call x1, Pallas kernels, attention_forward(): pl.pallas_call(attn_fwd_kernel, grid=(batch, pairs, length // rows), in_s...  71.1 us
    unnamed x274, local copies, waits for them, and re-layouts  67.1 us
    dot_general x6, matrix products, times_back(): lax.dot_general(left, matrix, (((1,), (1,)), ((), ())), preferred_element...  47.9 us
    another operation x21, local copies, waits for them, and re-layouts, gather_weights(): jnp.stack([canon[part][index].reshape(n_dp, n_seq, third, m.shape[1]) for...  46 us
    dot_general x1, matrix products, shards(): jnp.dot(normed_low, full_up, preferred_element_type=jnp.float32) + vec_up  37.2 us
    slice x24, local copies, waits for them, and re-layouts, reduce_grads(): m[:, :, part * third:(part + 1) * third].reshape(n_dp * n_seq, -1)  34.3 us
  transfers between devices with their start and end apart: 64, of which 22 were waited for; matrix products, arithmetic and copies ran while one was open for 32% of the time, Pallas kernels for 0%

profile of v4, /device:TPU:0, one launch (start us, length us, event | category | flops | bytes accessed | tf_op | source)
XLA Modules:
  0.0 950.1 jit_solution(11832117308193148102)
XLA Ops:
  30.9 5.7 concatenate.187
  57.4 5.3 collective-permute-done.2
  183.9 4.7 stack_reshape.70
  197.5 4.5 stack_reshape.71
  233.4 8.3 copy.477
  241.7 11.7 %reshape.905 = bf16[3072,768]{1,0:T(8,128)(2,1)} reshape(bf16[8,3,128,4,192]{4,3,2,1,0:T(4,128)(2,1)} %copy.477) | data formatting | bytes 9437184 | tf_op jit(solution)/shard_map/reshape | solution.py:155
  256.0 71.1 %shard_map.323 = (bf16[1,1024,768]{2,1,0:T(8,128)(2,1)}, f32[1,12,1024,1]{3,2,1,0:T(8,128)}) custom-call(s32[1,1024,3]{2,1,0:T(8,128)} %pad_add_fusion.bounds_ref, s32[6,1024,2]{2,1,0:T(8,128)} %bitcast.562, bf16[1,1024,768]{2,1,0:T(8,128)(2,1)} %fusion.24.q_ref, bf16[1,1024,768]{2,1,0:T(8,128)(2,1)} %fusion.23.k_ref, bf16[1,1024,768]{2,1,0:T(8,128)(2,1)} %fusion.25.v_ref), custom_call_target="tpu_custom_call" | custom-call | flops 3221225472 | bytes 6291456 | tf_op jit(solution)/shard_map/pallas_call | solution.py:329
  333.8 37.2 %multiply_convert_fusion = (bf16[1024,3072]{1,0:T(8,128)(2,1)S(1)}, f32[1024,3072]{1,0:T(8,128)}, f32[1024,3072]{1,0:T(8,128)}) fusion(f32[3072]{0:T(1024)S(1)} %bitcast.611, bf16[1024,768]{0,1:T(8,128)(2,1)S(1)} %fusion.14, bf16[768,3072]{1,0:T(8,128)(2,1)} %bitcast.542), kind=kOutput, calls=%fused_computation.4 | convolution fusion | flops 5039456256 | bytes 37761024 | tf_op jit(solution)/shard_map/dot_general | solution.py:449
  371.0 5.9 fusion.73
  383.8 18.9 %convert_reduce_fusion = (f32[3072]{0:T(1024)S(1)}, bf16[1024,3072]{1,0:T(8,128)(2,1)}) fusion(f32[1024,3072]{1,0:T(8,128)} %get-tuple-element.179, bf16[1024,768]{0,1:T(8,128)(2,1)} %get-tuple-element.171, bf16[3072,768]{1,0:T(8,128)(2,1)} %reshape.905, f32[1024,3072]{1,0:T(8,128)} %get-tuple-element.329, f32[3072]{0:T(1024)S(1)} %bitcast.612), kind=kOutput, calls=%fused_computation.2 | convolution fusion | flops 4885312512 | bytes 37773312 | tf_op jit(solution)/shard_map/dot_general | solution.py:369
  402.7 9.7 %multiply_reduce_fusion.1 = (f32[768]{0:T(1024)S(1)}, f32[1024]{0:T(1024)S(1)}, f32[768]{0:T(1024)S(1)}, f32[1024,768]{0,1:T(8,128)S(1)}) fusion(f32[1024,768]{0,1:T(8,128)S(1)} %get-tuple-element.328, f32[1024]{0:T(1024)S(1)} %fusion.39, f32[1024]{0:T(1024)S(1)} %broadcast_multiply_fusion.1, f32[768]{0:T(1024)S(1)} %reshape.986, ...), kind=kOutput, calls=%fused_computation.45 | convolution fusion | flops 4839699456 | bytes 20472832 | tf_op jit(solution)/shard_map/dot_general | solution.py:369
  417.2 87.8 %shard_map.324 = (bf16[1,1024,768]{2,1,0:T(8,128)(2,1)}, bf16[1,1024,768]{2,1,0:T(8,128)(2,1)}, bf16[1,1024,768]{2,1,0:T(8,128)(2,1)}) custom-call(s32[1,1024,3]{2,1,0:T(8,128)} %pad_add_fusion.bounds_ref, s32[6,1024,2]{2,1,0:T(8,128)} %bitcast.563, bf16[1,1024,768]{2,1,0:T(8,128)(2,1)} %fusion.24.q_ref, bf16[1,1024,768]{2,1,0:T(8,128)(2,1)} %fusion.23.k_ref, ...), custom_call_target="tpu_custom_call" | custom-call | flops 8053063680 | bytes 12582912 | tf_op jit(solution)/shard_map/pallas_call | solution.py:352
  507.6 4.9 fusion.17
  515.4 4.9 fusion.19
  523.2 12.3 %reshape.946 = bf16[1024,4,768]{2,1,0:T(4,128)(2,1)} reshape(bf16[1024,3072]{1,0:T(8,128)(2,1)} %get-tuple-element.334) | data formatting | bytes 12582912 | tf_op jit(solution)/shard_map/reshape | solution.py:166
  538.8 7.6 fusion.13
  550.3 4.9 copy.507
  555.3 4.6 reshape.951
  578.7 6.8 add_bitcast_fusion
  585.5 8.7 copy.483
  637.0 7.6 copy.478
  645.2 11.4 %reduce.45 = bf16[1024,768]{1,0:T(8,128)(2,1)} reduce(bf16[1024,1,768]{2,1,0:T(2,128)(2,1)S(1)} %bitcast.510, bf16[]{:T(256)} %broadcast.272), dimensions={1}, to_apply=%bitcast.425.reduce_sub_computation | reduce | bytes 3145730
  668.3 4.6 reshape.972
  679.5 10.1 %fusion.10 = f32[8,4,96,768]{3,2,0,1:T(8,128)} fusion(bf16[1024,8,96,1]{0,2,1,3:T(8,128)(2,1)} %bitcast.576, bf16[1024,4,768,1]{2,1,0,3:T(4,128)(2,1)} %bitcast.531), kind=kOutput, calls=%fused_computation.41 | convolution fusion | flops 4831838208 | bytes 17301504 | tf_op jit(solution)/shard_map/tar,tbc->abrc/dot_general | solution.py:167
  745.7 4.9 all-to-all-start.3
  761.6 9.4 collective-permute-done.36
  772.7 28.1 %collective-permute-done.31 = f32[8,146,128]{2,0,1:T(8,128)S(1)} collective-permute-done((f32[8,146,128]{2,0,1:T(8,128)S(1)}, f32[8,146,128]{2,0,1:T(8,128)S(1)}, u32[]{:S(2)}, u32[]{:S(2)}) %collective-permute-start.31) | collective-permute-done | bytes 598048 | tf_op jit(solution)/shard_map/ppermute | solution.py:121
  809.3 7.3 collective-permute-done.32
  867.2 4.8 collective-permute-done.56
  882.1 10.0 %collective-permute-done.46 = f32[8,440,128]{2,1,0:T(8,128)} collective-permute-done((f32[8,440,128]{2,1,0:T(8,128)}, f32[8,440,128]{2,1,0:T(8,128)}, u32[]{:S(2)}, u32[]{:S(2)}) %collective-permute-start.46) | collective-permute-done | bytes 1802272 | tf_op jit(solution)/shard_map/ppermute | solution.py:121
  921.0 4.6 collective-permute-done.48
  925.8 13.5 %collective-permute-done.59 = f32[1,432,128]{2,1,0:T(8,128)S(1)} collective-permute-done((f32[1,432,128]{2,1,0:T(8,128)S(1)}, f32[1,432,128]{2,1,0:T(8,128)S(1)}, u32[]{:S(2)}, u32[]{:S(2)}) %collective-permute-start.59) | collective-permute-done | bytes 221216 | tf_op jit(solution)/shard_map/ppermute | solution.py:121
  (784 shorter events, 504.5 us)
Async XLA Ops:
  0.8 108.2 %all-to-all-start = ((bf16[4,256,768]{2,1,0:T(8,128)(2,1)}), bf16[4,256,768]{2,1,0:T(8,128)(2,1)S(1)}, u32[]{:S(2)}, u32[]{:S(2)}) async-start(bf16[4,256,768]{2,1,0:T(8,128)(2,1)} %param.20), calls=%async_computation | async-start | bytes 3145728 | tf_op jit(solution)/shard_map/all_to_all | solution.py:418
  6.1 33.7 %collective-permute-start.5 = (bf16[1,144,128]{2,1,0:T(8,128)(2,1)}, bf16[1,144,128]{2,1,0:T(8,128)(2,1)}, u32[]{:S(2)}, u32[]{:S(2)}) collective-permute-start(bf16[1,144,128]{2,1,0:T(8,128)(2,1)} %maximum_bitcast_fusion.11), channel_id=1, source_target_pairs={{0,4},{1,5},{2,6},{3,7},{4,0},{5,1},{6,2},{7,3},{8,12},{9,13},{10,... | collective-permute-start | bytes 110600 | tf_op jit(solution)/shard_map/ppermute | solution.py:106
  10.5 29.4 %collective-permute-start.10 = (bf16[1,144,128]{2,1,0:T(8,128)(2,1)}, bf16[1,144,128]{2,1,0:T(8,128)(2,1)}, u32[]{:S(2)}, u32[]{:S(2)}) collective-permute-start(bf16[1,144,128]{2,1,0:T(8,128)(2,1)} %maximum_bitcast_fusion.12), channel_id=1, source_target_pairs={{0,4},{1,5},{2,6},{3,7},{4,0},{5,1},{6,2},{7,3},{8,12},{9,13},{10,... | collective-permute-start | bytes 110600 | tf_op jit(solution)/shard_map/ppermute | solution.py:106
  11.6 31.2 %collective-permute-start = (bf16[1,146,128]{2,0,1:T(2,128)(2,1)}, bf16[1,146,128]{2,0,1:T(2,128)(2,1)}, u32[]{:S(2)}, u32[]{:S(2)}) collective-permute-start(bf16[1,146,128]{2,0,1:T(2,128)(2,1)} %pad_bitcast_fusion), channel_id=1, source_target_pairs={{0,4},{1,5},{2,6},{3,7},{4,0},{5,1},{6,2},{7,3},{8,12},{9,13},{10,... | collective-permute-start | bytes 112136 | tf_op jit(solution)/shard_map/ppermute | solution.py:106
  16.3 32.8 %collective-permute-start.25 = (bf16[1,432,128]{2,1,0:T(8,128)(2,1)}, bf16[1,432,128]{2,1,0:T(8,128)(2,1)}, u32[]{:S(2)}, u32[]{:S(2)}) collective-permute-start(bf16[1,432,128]{2,1,0:T(8,128)(2,1)} %maximum_bitcast_fusion.10), channel_id=1, source_target_pairs={{0,4},{1,5},{2,6},{3,7},{4,0},{5,1},{6,2},{7,3},{8,12},{9,13},{10,... | collective-permute-start | bytes 331784 | tf_op jit(solution)/shard_map/ppermute | solution.py:106
  17.4 32.0 %collective-permute-start.20 = (bf16[1,432,128]{2,1,0:T(8,128)(2,1)}, bf16[1,432,128]{2,1,0:T(8,128)(2,1)}, u32[]{:S(2)}, u32[]{:S(2)}) collective-permute-start(bf16[1,432,128]{2,1,0:T(8,128)(2,1)} %maximum_bitcast_fusion.9), channel_id=1, source_target_pairs={{0,4},{1,5},{2,6},{3,7},{4,0},{5,1},{6,2},{7,3},{8,12},{9,13},{10,... | collective-permute-start | bytes 331784 | tf_op jit(solution)/shard_map/ppermute | solution.py:106
  76.5 23.8 %collective-permute-start.4 = (bf16[16,146,128]{2,0,1:T(8,128)(2,1)}, bf16[16,146,128]{2,0,1:T(8,128)(2,1)}, u32[]{:S(2)}, u32[]{:S(2)}) collective-permute-start(bf16[16,146,128]{2,0,1:T(8,128)(2,1)} %pad_maximum_fusion.13), channel_id=1, source_target_pairs={{0,8},{8,0},{16,24},{24,16},{1,9},{9,1},{17,25},{25,17},{2,10},{10... | collective-permute-start | bytes 1794056 | tf_op jit(solution)/shard_map/ppermute | solution.py:106
  77.8 63.5 %collective-permute-start.23 = (bf16[8,432,128]{2,1,0:T(8,128)(2,1)}, bf16[8,432,128]{2,1,0:T(8,128)(2,1)}, u32[]{:S(2)}, u32[]{:S(2)}) collective-permute-start(bf16[8,432,128]{2,1,0:T(8,128)(2,1)} %pad_maximum_fusion.11), channel_id=1, source_target_pairs={{0,1},{1,0},{2,3},{3,2},{4,5},{5,4},{6,7},{7,6},{8,9},{9,8},{10,11... | collective-permute-start | bytes 2654216 | tf_op jit(solution)/shard_map/ppermute | solution.py:106
  80.6 82.0 %collective-permute-start.28 = (bf16[8,432,128]{2,1,0:T(8,128)(2,1)}, bf16[8,432,128]{2,1,0:T(8,128)(2,1)}, u32[]{:S(2)}, u32[]{:S(2)}) collective-permute-start(bf16[8,432,128]{2,1,0:T(8,128)(2,1)} %pad_maximum_fusion.12), channel_id=1, source_target_pairs={{0,2},{1,3},{2,0},{3,1},{4,6},{5,7},{6,4},{7,5},{8,10},{9,11},{10,... | collective-permute-start | bytes 2654216 | tf_op jit(solution)/shard_map/ppermute | solution.py:106
  82.8 81.8 %collective-permute-start.18 = (bf16[8,440,128]{2,1,0:T(8,128)(2,1)}, bf16[8,440,128]{2,1,0:T(8,128)(2,1)}, u32[]{:S(2)}, u32[]{:S(2)}) collective-permute-start(bf16[8,440,128]{2,1,0:T(8,128)(2,1)} %pad_maximum_fusion.10), channel_id=1, source_target_pairs={{0,16},{8,24},{16,0},{24,8},{1,17},{9,25},{17,1},{25,9},{2,18},{10... | collective-permute-start | bytes 2703368 | tf_op jit(solution)/shard_map/ppermute | solution.py:106
  109.0 38.6 %all-to-all-start.2 = ((bf16[4,256,768]{2,1,0:T(8,128)(2,1)}), bf16[4,256,768]{2,1,0:T(8,128)(2,1)S(1)}, u32[]{:S(2)}, u32[]{:S(2)}) async-start(bf16[4,256,768]{2,1,0:T(8,128)(2,1)} %param.21), calls=%async_computation.2 | async-start | bytes 3145728 | tf_op jit(solution)/shard_map/all_to_all | solution.py:418
  144.6 23.0 %collective-permute-start.24 = (bf16[16,432,128]{2,1,0:T(8,128)(2,1)}, bf16[16,432,128]{2,1,0:T(8,128)(2,1)}, u32[]{:S(2)}, u32[]{:S(2)}) collective-permute-start(bf16[16,432,128]{2,1,0:T(8,128)(2,1)} %pad_maximum_fusion.5), channel_id=1, source_target_pairs={{0,8},{8,0},{16,24},{24,16},{1,9},{9,1},{17,25},{25,17},{2,10},{10... | collective-permute-start | bytes 5308424 | tf_op jit(solution)/shard_map/ppermute | solution.py:106
  167.4 34.6 %collective-permute-start.19 = (bf16[16,440,128]{2,1,0:T(8,128)(2,1)}, bf16[16,440,128]{2,1,0:T(8,128)(2,1)}, u32[]{:S(2)}, u32[]{:S(2)}) collective-permute-start(bf16[16,440,128]{2,1,0:T(8,128)(2,1)} %pad_maximum_fusion.4), channel_id=1, source_target_pairs={{0,8},{8,0},{16,24},{24,16},{1,9},{9,1},{17,25},{25,17},{2,10},{10... | collective-permute-start | bytes 5406728 | tf_op jit(solution)/shard_map/ppermute | solution.py:106
  628.0 110.8 %collective-permute-start.40 = (f32[16,144,128]{2,1,0:T(8,128)}, f32[16,144,128]{2,1,0:T(8,128)}, u32[]{:S(2)}, u32[]{:S(2)}) collective-permute-start(f32[16,144,128]{2,1,0:T(8,128)} %dynamic-slice_bitcast_fusion.7), channel_id=1, source_target_pairs={{0,8},{8,0},{16,24},{24,16},{1,9},{9,1},{17,25},{25,17},{2,10},{10... | collective-permute-start | bytes 3538952 | tf_op jit(solution)/shard_map/ppermute | solution.py:121
  628.3 114.5 %collective-permute-start.35 = (f32[16,144,128]{2,1,0:T(8,128)}, f32[16,144,128]{2,1,0:T(8,128)}, u32[]{:S(2)}, u32[]{:S(2)}) collective-permute-start(f32[16,144,128]{2,1,0:T(8,128)} %dynamic-slice_bitcast_fusion.8), channel_id=1, source_target_pairs={{0,8},{8,0},{16,24},{24,16},{1,9},{9,1},{17,25},{25,17},{2,10},{10... | collective-permute-start | bytes 3538952 | tf_op jit(solution)/shard_map/ppermute | solution.py:121
  630.2 124.9 %collective-permute-start.30 = (f32[16,146,128]{2,0,1:T(8,128)}, f32[16,146,128]{2,0,1:T(8,128)}, u32[]{:S(2)}, u32[]{:S(2)}) collective-permute-start(f32[16,146,128]{2,0,1:T(8,128)} %dynamic-slice_bitcast_fusion.6), channel_id=1, source_target_pairs={{0,8},{8,0},{16,24},{24,16},{1,9},{9,1},{17,25},{25,17},{2,10},{10... | collective-permute-start | bytes 3588104 | tf_op jit(solution)/shard_map/ppermute | solution.py:121
  660.4 85.3 %all-to-all-start.1 = ((bf16[4,2,98304]{2,1,0:T(2,128)(2,1)}), bf16[4,2,98304]{2,1,0:T(2,128)(2,1)}, u32[]{:S(2)}, u32[]{:S(2)}) async-start(bf16[4,2,98304]{2,1,0:T(2,128)(2,1)} %reshape.1051), calls=%async_computation.1 | async-start | bytes 3145728 | tf_op jit(solution)/shard_map/all_to_all | solution.py:421
  711.9 119.8 %collective-permute-start.55 = (f32[16,432,128]{2,1,0:T(8,128)}, f32[16,432,128]{2,1,0:T(8,128)}, u32[]{:S(2)}, u32[]{:S(2)}) collective-permute-start(f32[16,432,128]{2,1,0:T(8,128)} %dynamic-slice_bitcast_fusion.1), channel_id=1, source_target_pairs={{0,8},{8,0},{16,24},{24,16},{1,9},{9,1},{17,25},{25,17},{2,10},{10... | collective-permute-start | bytes 10616840 | tf_op jit(solution)/shard_map/ppermute | solution.py:121
  712.3 126.7 %collective-permute-start.50 = (f32[16,432,128]{2,1,0:T(8,128)}, f32[16,432,128]{2,1,0:T(8,128)}, u32[]{:S(2)}, u32[]{:S(2)}) collective-permute-start(f32[16,432,128]{2,1,0:T(8,128)} %dynamic-slice_bitcast_fusion.2), channel_id=1, source_target_pairs={{0,8},{8,0},{16,24},{24,16},{1,9},{9,1},{17,25},{25,17},{2,10},{10... | collective-permute-start | bytes 10616840 | tf_op jit(solution)/shard_map/ppermute | solution.py:121
  738.8 105.1 %collective-permute-start.45 = (f32[16,440,128]{2,1,0:T(8,128)}, f32[16,440,128]{2,1,0:T(8,128)}, u32[]{:S(2)}, u32[]{:S(2)}) collective-permute-start(f32[16,440,128]{2,1,0:T(8,128)} %dynamic-slice_bitcast_fusion), channel_id=1, source_target_pairs={{0,8},{8,0},{16,24},{24,16},{1,9},{9,1},{17,25},{25,17},{2,10},{10... | collective-permute-start | bytes 10813448 | tf_op jit(solution)/shard_map/ppermute | solution.py:121
  745.7 151.6 %all-to-all-start.3 = ((f32[1,1024,768]{2,0,1:T(1,128)}), f32[1,1024,768]{2,0,1:T(1,128)}, u32[]{:S(2)}, u32[]{:S(2)}) async-start(f32[1,1024,768]{2,0,1:T(1,128)} %copy.483), calls=%async_computation.3 | async-start | bytes 6291456 | tf_op jit(solution)/shard_map/all_to_all | solution.py:421
  758.3 42.5 %collective-permute-start.31 = (f32[8,146,128]{2,0,1:T(8,128)S(1)}, f32[8,146,128]{2,0,1:T(8,128)S(1)}, u32[]{:S(2)}, u32[]{:S(2)}) collective-permute-start(f32[8,146,128]{2,0,1:T(8,128)S(1)} %dynamic-slice_bitcast_fusion.12), channel_id=1, source_target_pairs={{0,16},{8,24},{16,0},{24,8},{1,17},{9,25},{17,1},{25,9},{2,18},{10... | collective-permute-start | bytes 1794056 | tf_op jit(solution)/shard_map/ppermute | solution.py:121
  770.9 35.7 %collective-permute-start.42 = (f32[4,144,128]{2,1,0:T(8,128)S(1)}, f32[4,144,128]{2,1,0:T(8,128)S(1)}, u32[]{:S(2)}, u32[]{:S(2)}) collective-permute-start(f32[4,144,128]{2,1,0:T(8,128)S(1)} %dynamic-slice_bitcast_fusion.19), channel_id=1, source_target_pairs={{0,16},{8,24},{16,0},{24,8},{1,17},{9,25},{17,1},{25,9},{2,18},{10... | collective-permute-start | bytes 884744 | tf_op jit(solution)/shard_map/ppermute | solution.py:121
  828.4 30.9 %collective-permute-start.34 = (f32[1,146,128]{2,1,0:T(8,128)}, f32[1,146,128]{2,1,0:T(8,128)}, u32[]{:S(2)}, u32[]{:S(2)}) collective-permute-start(f32[1,146,128]{2,1,0:T(8,128)} %constant_dynamic-slice_fusion.5), channel_id=1, source_target_pairs={{0,4},{1,5},{2,6},{3,7},{4,0},{5,1},{6,2},{7,3},{8,12},{9,13},{10,... | collective-permute-start | bytes 224264 | tf_op jit(solution)/shard_map/ppermute | solution.py:121
  835.7 36.3 %collective-permute-start.56 = (f32[8,432,128]{2,1,0:T(8,128)}, f32[8,432,128]{2,1,0:T(8,128)}, u32[]{:S(2)}, u32[]{:S(2)}) collective-permute-start(f32[8,432,128]{2,1,0:T(8,128)} %dynamic-slice_bitcast_fusion.4), channel_id=1, source_target_pairs={{0,2},{1,3},{2,0},{3,1},{4,6},{5,7},{6,4},{7,5},{8,10},{9,11},{10,... | collective-permute-start | bytes 5308424 | tf_op jit(solution)/shard_map/ppermute | solution.py:121
  843.0 34.3 %collective-permute-start.51 = (f32[8,432,128]{2,1,0:T(8,128)}, f32[8,432,128]{2,1,0:T(8,128)}, u32[]{:S(2)}, u32[]{:S(2)}) collective-permute-start(f32[8,432,128]{2,1,0:T(8,128)} %dynamic-slice_bitcast_fusion.5), channel_id=1, source_target_pairs={{0,1},{1,0},{2,3},{3,2},{4,5},{5,4},{6,7},{7,6},{8,9},{9,8},{10,11... | collective-permute-start | bytes 5308424 | tf_op jit(solution)/shard_map/ppermute | solution.py:121
  849.6 42.5 %collective-permute-start.46 = (f32[8,440,128]{2,1,0:T(8,128)}, f32[8,440,128]{2,1,0:T(8,128)}, u32[]{:S(2)}, u32[]{:S(2)}) collective-permute-start(f32[8,440,128]{2,1,0:T(8,128)} %dynamic-slice_bitcast_fusion.3), channel_id=1, source_target_pairs={{0,16},{8,24},{16,0},{24,8},{1,17},{9,25},{17,1},{25,9},{2,18},{10... | collective-permute-start | bytes 5406728 | tf_op jit(solution)/shard_map/ppermute | solution.py:121
  875.9 27.9 %collective-permute-start.57 = (f32[4,432,128]{2,1,0:T(8,128)}, f32[4,432,128]{2,1,0:T(8,128)}, u32[]{:S(2)}, u32[]{:S(2)}) collective-permute-start(f32[4,432,128]{2,1,0:T(8,128)} %dynamic-slice_bitcast_fusion.10), channel_id=1, source_target_pairs={{0,16},{8,24},{16,0},{24,8},{1,17},{9,25},{17,1},{25,9},{2,18},{10... | collective-permute-start | bytes 2654216 | tf_op jit(solution)/shard_map/ppermute | solution.py:121
  880.3 25.5 %collective-permute-start.52 = (f32[4,432,128]{2,1,0:T(8,128)}, f32[4,432,128]{2,1,0:T(8,128)}, u32[]{:S(2)}, u32[]{:S(2)}) collective-permute-start(f32[4,432,128]{2,1,0:T(8,128)} %dynamic-slice_bitcast_fusion.11), channel_id=1, source_target_pairs={{0,2},{1,3},{2,0},{3,1},{4,6},{5,7},{6,4},{7,5},{8,10},{9,11},{10,... | collective-permute-start | bytes 2654216 | tf_op jit(solution)/shard_map/ppermute | solution.py:121
  917.8 21.4 %collective-permute-start.59 = (f32[1,432,128]{2,1,0:T(8,128)S(1)}, f32[1,432,128]{2,1,0:T(8,128)S(1)}, u32[]{:S(2)}, u32[]{:S(2)}) collective-permute-start(f32[1,432,128]{2,1,0:T(8,128)S(1)} %constant_dynamic-slice_fusion), channel_id=1, source_target_pairs={{0,4},{1,5},{2,6},{3,7},{4,0},{5,1},{6,2},{7,3},{8,12},{9,13},{10,... | collective-permute-start | bytes 663560 | tf_op jit(solution)/shard_map/ppermute | solution.py:121
  919.3 24.2 %collective-permute-start.54 = (f32[1,432,128]{2,1,0:T(8,128)S(1)}, f32[1,432,128]{2,1,0:T(8,128)S(1)}, u32[]{:S(2)}, u32[]{:S(2)}) collective-permute-start(f32[1,432,128]{2,1,0:T(8,128)S(1)} %constant_dynamic-slice_fusion.1), channel_id=1, source_target_pairs={{0,4},{1,5},{2,6},{3,7},{4,0},{5,1},{6,2},{7,3},{8,12},{9,13},{10,... | collective-permute-start | bytes 663560 | tf_op jit(solution)/shard_map/ppermute | solution.py:121
  925.7 20.2 %collective-permute-start.49 = (f32[1,440,128]{2,1,0:T(8,128)S(1)}, f32[1,440,128]{2,1,0:T(8,128)S(1)}, u32[]{:S(2)}, u32[]{:S(2)}) collective-permute-start(f32[1,440,128]{2,1,0:T(8,128)S(1)} %constant_dynamic-slice_fusion.2), channel_id=1, source_target_pairs={{0,4},{1,5},{2,6},{3,7},{4,0},{5,1},{6,2},{7,3},{8,12},{9,13},{10,... | collective-permute-start | bytes 675848 | tf_op jit(solution)/shard_map/ppermute | solution.py:121
  (152 other events, 1396.3 us)

commit v5 on v4

--- a/solution.py
+++ b/solution.py
@@ -69,33 +69,28 @@
     return [(i, i ^ (1 << b)) for i in range(lax.axis_size(axis))]
 
 
-N_PARTS = 3
 LANES = 128
-
-
-def to_order(blocked, order):
+LETTERS = "ABCDEFGHIJKLMNOP"
+
+
+def letters():
     canon = canonical_bits()
-    rest = blocked.shape[1:]
-    x = blocked.reshape([2] * len(canon) + list(rest))
-    perm = [canon.index(bit) for bit in order] + list(range(len(canon), len(canon) + len(rest)))
-    return x.transpose(perm).reshape(blocked.shape)
-
-
-def from_order(blocked, order):
-    canon = canonical_bits()
-    rest = blocked.shape[1:]
-    x = blocked.reshape([2] * len(canon) + list(rest))
-    perm = [order.index(bit) for bit in canon] + list(range(len(canon), len(canon) + len(rest)))
-    return x.transpose(perm).reshape(blocked.shape)
-
-
-def lane_rows(flat_blocks):
-    n, width = flat_blocks.shape
-    rows = -(-width // LANES)
-    pad = rows * LANES - width
-    if pad:
-        flat_blocks = jnp.concatenate([flat_blocks, jnp.zeros((n, pad), flat_blocks.dtype)], axis=1)
-    return flat_blocks.reshape(n, rows, LANES)
+    return {bit: LETTERS[i] for i, bit in enumerate(canon)}
+
+
+def dp_letters():
+    names = letters()
+    return "".join(names[bit] for bit in canonical_bits() if bit[0] == "dp")
+
+
+def seq_letters():
+    names = letters()
+    return "".join(names[bit] for bit in canonical_bits() if bit[0] == "seq")
+
+
+def order_letters(order):
+    names = letters()
+    return "".join(names[bit] for bit in order)
 
 
 def gather_parts(parts, orders):
@@ -123,85 +118,78 @@
     return out
 
 
-def gather_weights(matrices, vectors):
-    n_dp, n_seq = lax.axis_size("dp"), lax.axis_size("seq")
-    orders = bit_orders(N_PARTS)
-    parts, layout = [], []
-    for part in range(N_PARTS):
-        items = []
-        for m in matrices:
-            third = m.shape[0] // N_PARTS
-            items.append(m[part * third:(part + 1) * third].reshape(-1))
-        if part == 0:
-            items += [v.reshape(-1) for v in vectors]
-        sizes = [item.size for item in items]
-        parts.append(lane_rows(jnp.concatenate(items)[None])[0])
-        layout.append(sizes)
-    got = gather_parts(parts, orders)
-    canon = []
-    for buf, order, sizes in zip(got, orders, layout):
-        flat = from_order(buf, order).reshape(n_dp * n_seq, -1)
-        pieces, offset = [], 0
-        for size in sizes:
-            pieces.append(flat[:, offset:offset + size])
-            offset += size
-        canon.append(pieces)
-    full = []
-    for index, m in enumerate(matrices):
-        third = m.shape[0] // N_PARTS
-        stacked = jnp.stack(
-            [canon[part][index].reshape(n_dp, n_seq, third, m.shape[1]) for part in range(N_PARTS)], axis=2
-        )
-        full.append(stacked.transpose(0, 2, 3, 1, 4).reshape(n_dp * m.shape[0], n_seq * m.shape[1]))
-    vecs = []
-    for index, v in enumerate(vectors):
-        piece = canon[0][len(matrices) + index]
-        vecs.append(piece.reshape(n_dp, n_seq, v.size)[:, 0].reshape(-1))
-    return full, vecs
-
-
-def blocked_grad(left, right, n_dp, n_seq):
-    tokens = left.shape[0]
-    a = left.reshape(tokens, n_dp, left.shape[1] // n_dp)
-    b = right.reshape(tokens, n_seq, right.shape[1] // n_seq)
-    return jnp.einsum("tar,tbc->abrc", a, b, preferred_element_type=jnp.float32)
-
-
-def reduce_grads(matrices, vectors):
-    n_dp, n_seq = lax.axis_size("dp"), lax.axis_size("seq")
-    orders = bit_orders(N_PARTS)
-    parts, layout = [], []
-    for part in range(N_PARTS):
-        items = []
-        for m in matrices:
-            third = m.shape[2] // N_PARTS
-            items.append(m[:, :, part * third:(part + 1) * third].reshape(n_dp * n_seq, -1))
-        if part == 0:
-            for v in vectors:
-                v = v.reshape(n_dp, 1, -1)
-                items.append(jnp.broadcast_to(v, (n_dp, n_seq, v.shape[-1])).reshape(n_dp * n_seq, -1))
-        sizes = [item.shape[1] for item in items]
-        parts.append(to_order(lane_rows(jnp.concatenate(items, axis=1)), orders[part]))
-        layout.append(sizes)
-    summed = reduce_parts(parts, orders)
-    pieces_by_part = []
-    for buf, sizes in zip(summed, layout):
-        flat = buf.reshape(-1)
-        pieces, offset = [], 0
-        for size in sizes:
-            pieces.append(flat[offset:offset + size])
-            offset += size
-        pieces_by_part.append(pieces)
-    own = []
-    for index, m in enumerate(matrices):
-        third = m.shape[2] // N_PARTS
-        own.append(
-            jnp.concatenate(
-                [pieces_by_part[part][index].reshape(third, m.shape[3]) for part in range(N_PARTS)], axis=0
-            )
-        )
-    vecs = [pieces_by_part[0][len(matrices) + index] for index in range(len(vectors))]
-    return own, vecs
+class Blocked:
+    def __init__(self, blocks, order):
+        self.blocks = blocks
+        self.order = order
+
+    def apply(self, x):
+        rb = self.blocks.shape[-2]
+        tokens = x.shape[0]
+        xs = x.reshape((tokens,) + (2,) * len(dp_letters()) + (rb,))
+        spec = f"t{dp_letters()}r,{order_letters(self.order)}rc->t{seq_letters()}c"
+        return jnp.einsum(spec, xs, self.blocks, preferred_element_type=jnp.float32).reshape(tokens, -1)
+
+    def apply_back(self, g):
+        cb = self.blocks.shape[-1]
+        tokens = g.shape[0]
+        gs = g.reshape((tokens,) + (2,) * len(seq_letters()) + (cb,))
+        spec = f"t{seq_letters()}c,{order_letters(self.order)}rc->t{dp_letters()}r"
+        return jnp.einsum(spec, gs, self.blocks, preferred_element_type=jnp.float32).reshape(tokens, -1)
+
+
+def lane_flat(array):
+    size = array.size
+    assert size % LANES == 0
+    return array.reshape(size // LANES, LANES)
+
+
+def gather_weights(matrices):
+    orders = bit_orders(len(matrices))
+    got = gather_parts([lane_flat(m) for m in matrices], orders)
+    n_bits = len(canonical_bits())
+    return [
+        Blocked(buf.reshape((2,) * n_bits + m.shape), order) for buf, m, order in zip(got, matrices, orders)
+    ]
+
+
+def gather_vectors(vectors):
+    flat = jnp.concatenate([v.reshape(-1) for v in vectors])
+    got = lax.all_gather(flat, "dp", axis=0, tiled=False)
+    out, offset = [], 0
+    for v in vectors:
+        out.append(got[:, offset:offset + v.size].reshape(-1))
+        offset += v.size
+    return out
+
+
+def reduce_grads(pairs):
+    orders = bit_orders(len(pairs))
+    parts = []
+    for (left, right), order in zip(pairs, orders):
+        tokens = left.shape[0]
+        rb = left.shape[1] // (1 << len(dp_letters()))
+        cb = right.shape[1] // (1 << len(seq_letters()))
+        ls = left.reshape((tokens,) + (2,) * len(dp_letters()) + (rb,))
+        rs = right.reshape((tokens,) + (2,) * len(seq_letters()) + (cb,))
+        spec = f"t{dp_letters()}r,t{seq_letters()}c->{order_letters(order)}rc"
+        g = jnp.einsum(spec, ls, rs, preferred_element_type=jnp.float32)
+        parts.append((g.reshape((-1, rb * cb // LANES, LANES)), (rb, cb)))
+    summed = reduce_parts([p for p, _ in parts], orders)
+    return [s.reshape(shape) for s, (_, shape) in zip(summed, parts)]
+
+
+def reduce_vectors(vectors):
+    flat = jnp.concatenate([v.reshape(-1) for v in vectors])
+    total = lax.psum(flat, ("dp", "seq"))
+    n_dp = lax.axis_size("dp")
+    me = lax.axis_index("dp")
+    out, offset = [], 0
+    for v in vectors:
+        piece = v.size // n_dp
+        out.append(lax.dynamic_slice_in_dim(total, offset + me * piece, piece, 0))
+        offset += v.size
+    return out
 
 
 TQ = 256
@@ -401,17 +389,15 @@
     seq_len = shard_len * n_seq
     rows = mine * seq_len
 
-    (full_query, full_key, full_value), (g_b_query, g_b_value) = gather_weights(
-        [w_query, w_key, w_value], [b_query, b_value]
-    )
-    (full_out, full_up, full_down), (
-        g_b_out, g_gain_one, g_shift_one, g_b_up, g_b_down, g_gain_two, g_shift_two,
-    ) = gather_weights([w_out, w_up, w_down], [b_out, gain_one, shift_one, b_up, b_down, gain_two, shift_two])
+    full_query, full_key, full_value = gather_weights([w_query, w_key, w_value])
+    full_out, full_up, full_down = gather_weights([w_out, w_up, w_down])
     (
         vec_query, vec_value, vec_out, vec_gain_one, vec_shift_one, vec_up, vec_down, vec_gain_two, vec_shift_two,
     ) = [
         item.astype(jnp.float32)
-        for item in (g_b_query, g_b_value, g_b_out, g_gain_one, g_shift_one, g_b_up, g_b_down, g_gain_two, g_shift_two)
+        for item in gather_vectors(
+            [b_query, b_value, b_out, gain_one, shift_one, b_up, b_down, gain_two, shift_two]
+        )
     ]
 
     def whole_sequences(array):
@@ -430,9 +416,9 @@
     bits = bits.reshape(H // 2, 2, seq_len).transpose(0, 2, 1)
 
     flat = seq_inputs.reshape(rows, width)
-    queries = (jnp.dot(flat, full_query, preferred_element_type=jnp.float32) + vec_query).astype(jnp.bfloat16)
-    keys = jnp.dot(flat, full_key, preferred_element_type=jnp.float32).astype(jnp.bfloat16)
-    values = (jnp.dot(flat, full_value, preferred_element_type=jnp.float32) + vec_value).astype(jnp.bfloat16)
+    queries = (full_query.apply(flat) + vec_query).astype(jnp.bfloat16)
+    keys = full_key.apply(flat).astype(jnp.bfloat16)
+    values = (full_value.apply(flat) + vec_value).astype(jnp.bfloat16)
 
     def by_seq(array):
         return array.reshape(mine, seq_len, width)
@@ -441,15 +427,15 @@
     context_tok = context.reshape(rows, width)
     hidden = (
         flat.astype(jnp.float32)
-        + jnp.dot(context_tok, full_out, preferred_element_type=jnp.float32)
+        + full_out.apply(context_tok)
         + vec_out
     )
     normed = layer_norm(hidden, vec_gain_one, vec_shift_one)
     normed_low = normed.astype(jnp.bfloat16)
-    upper = jnp.dot(normed_low, full_up, preferred_element_type=jnp.float32) + vec_up
+    upper = full_up.apply(normed_low) + vec_up
     gelu_value, gelu_back = jax.vjp(partial(jax.nn.gelu, approximate=False), upper)
     active = gelu_value.astype(jnp.bfloat16)
-    mixed = normed + jnp.dot(active, full_down, preferred_element_type=jnp.float32) + vec_down
+    mixed = normed + full_down.apply(active) + vec_down
     output = layer_norm(mixed, vec_gain_two, vec_shift_two).astype(jnp.bfloat16)
     out_tokens = token_owners(output.reshape(mine, seq_len, width))
 
@@ -458,23 +444,22 @@
     grad_mixed, grad_gain_two, grad_shift_two = norm_two_back(grad_out)
     grad_lower = grad_mixed.astype(jnp.bfloat16)
     grad_b_down = jnp.sum(grad_lower.astype(jnp.float32), axis=0)
-    grad_w_down = blocked_grad(active, grad_lower, n_dp, n_seq)
-    grad_upper = gelu_back(times_back(grad_lower, full_down))[0].astype(jnp.bfloat16)
+    grad_upper = gelu_back(full_down.apply_back(grad_lower))[0].astype(jnp.bfloat16)
     grad_b_up = jnp.sum(grad_upper.astype(jnp.float32), axis=0)
-    grad_w_up = blocked_grad(normed_low, grad_upper, n_dp, n_seq)
-    grad_normed = grad_mixed + times_back(grad_upper, full_up)
+    grad_normed = grad_mixed + full_up.apply_back(grad_upper)
     norm_one_back = jax.vjp(layer_norm, hidden, vec_gain_one, vec_shift_one)[1]
     grad_hidden, grad_gain_one, grad_shift_one = norm_one_back(grad_normed)
     grad_branch = grad_hidden.astype(jnp.bfloat16)
     grad_b_out = jnp.sum(grad_branch.astype(jnp.float32), axis=0)
-    grad_w_out = blocked_grad(context_tok, grad_branch, n_dp, n_seq)
-    (own_w_out, own_w_up, own_w_down), (
+    own_w_out, own_w_up, own_w_down = reduce_grads(
+        [(context_tok, grad_branch), (normed_low, grad_upper), (active, grad_lower)]
+    )
+    (
         own_b_out, own_gain_one, own_shift_one, own_b_up, own_b_down, own_gain_two, own_shift_two,
-    ) = reduce_grads(
-        [grad_w_out, grad_w_up, grad_w_down],
-        [grad_b_out, grad_gain_one, grad_shift_one, grad_b_up, grad_b_down, grad_gain_two, grad_shift_two],
-    )
-    grad_context = times_back(grad_branch, full_out).astype(jnp.bfloat16)
+    ) = reduce_vectors(
+        [grad_b_out, grad_gain_one, grad_shift_one, grad_b_up, grad_b_down, grad_gain_two, grad_shift_two]
+    )
+    grad_context = full_out.apply_back(grad_branch).astype(jnp.bfloat16)
     grad_q, grad_k, grad_v = attention_backward(
         bounds, bits, by_seq(queries), by_seq(keys), by_seq(values), by_seq(grad_context), lse
     )
@@ -485,19 +470,15 @@
     )
     grad_inputs = (
         grad_hidden
-        + times_back(grad_q, full_query)
-        + times_back(grad_k, full_key)
-        + times_back(grad_v, full_value)
+        + full_query.apply_back(grad_q)
+        + full_key.apply_back(grad_k)
+        + full_value.apply_back(grad_v)
     )
     grad_tokens = token_owners(grad_inputs.reshape(mine, seq_len, width))
-    grad_w_query = blocked_grad(flat, grad_q, n_dp, n_seq)
     grad_b_query = jnp.sum(grad_q.astype(jnp.float32), axis=0)
-    grad_w_key = blocked_grad(flat, grad_k, n_dp, n_seq)
-    grad_w_value = blocked_grad(flat, grad_v, n_dp, n_seq)
     grad_b_value = jnp.sum(grad_v.astype(jnp.float32), axis=0)
-    (own_w_query, own_w_key, own_w_value), (own_b_query, own_b_value) = reduce_grads(
-        [grad_w_query, grad_w_key, grad_w_value], [grad_b_query, grad_b_value]
-    )
+    own_w_query, own_w_key, own_w_value = reduce_grads([(flat, grad_q), (flat, grad_k), (flat, grad_v)])
+    own_b_query, own_b_value = reduce_vectors([grad_b_query, grad_b_value])
     return (
         out_tokens,
         grad_tokens,

time: 960 us -> 1060 us (1.10)
  other arithmetic: 103 us -> 211 us
  local copies, waits for them, and re-layouts: 353 us -> 275 us
  blocking collectives: 0 us -> 75.9 us
  matrix products: 131 us -> 89.7 us
  waiting for transfers between devices: 116 us -> 151 us
    convert_element_type x0 -> x8, other arithmetic: none -> 79.1 us  [the longest x1 33.7 us: shards(): gelu_back(full_down.apply_back(grad_lower))[0].astype(jnp.bfloat16)]
    reshape x62 -> x10, local copies, waits for them, and re-layouts: 102 us -> 43.3 us  [the longest x6 27 us: gather_weights(): buf.reshape((2,) * n_bits + m.shape)]
    slice x57 -> x0, local copies, waits for them, and re-layouts: 50.1 us -> none  [the longest x24 34.3 us: reduce_grads(): m[:, :, part * third:(part + 1) * third].reshape(n_dp * n_seq, -1)]
    psum x0 -> x1, blocking collectives: none -> 45.2 us  [reduce_vectors(): total = lax.psum(flat, ('dp', 'seq'))]
    dot_general x18, matrix products: 131 us -> 89.7 us  [the longest x6 31.1 us: reduce_grads(): g = jnp.einsum(spec, ls, rs, preferred_element_type=jnp.float32)]
    unnamed x274 -> x210, local copies, waits for them, and re-layouts: 67.1 us -> 33.9 us
    all_gather x0 -> x1, blocking collectives: none -> 30.7 us  [gather_vectors(): got = lax.all_gather(flat, 'dp', axis=0, tiled=False)]
    ppermute x30, waiting for transfers between devices: 105 us -> 132 us  [reduce_parts(): buf = keep + lax.ppermute(send, bit[0], partner(bit))]
  transfers between devices with their start and end apart: 64 -> 64, of which waited for: 22 -> 18; matrix products, arithmetic and copies ran while one was open for 32% -> 33% of each run, Pallas kernels for 0% -> 15%
where the time goes in v5:
time: 1060 us; the launch traced here: 1040 us
  local copies, waits for them, and re-layouts  275 us (26%)
  other arithmetic  211 us (20%)
  Pallas kernels  158 us (15%)
  waiting for transfers between devices  151 us (14%)
  matrix products  89.7 us (8%)
  starting transfers between devices  77.6 us (7%)
  blocking collectives  75.9 us (7%)
    ppermute x30, waiting for transfers between devices, reduce_parts(): buf = keep + lax.ppermute(send, bit[0], partner(bit))  132 us
    pallas_call x1, Pallas kernels, attention_backward(): pl.pallas_call(attn_bwd_kernel, grid=(batch, pairs, length // rows), in_s...  87.4 us
    pallas_call x1, Pallas kernels, attention_forward(): pl.pallas_call(attn_fwd_kernel, grid=(batch, pairs, length // rows), in_s...  70.7 us
    psum x1, blocking collectives, reduce_vectors(): total = lax.psum(flat, ('dp', 'seq'))  45.2 us
    another operation x6, local copies, waits for them, and re-layouts, reduce_parts(): half = buf.reshape((2, buf.shape[0] // 2) + buf.shape[1:])  35.5 us
    unnamed x210, local copies, waits for them, and re-layouts  33.9 us
    convert_element_type x1, other arithmetic, shards(): gelu_back(full_down.apply_back(grad_lower))[0].astype(jnp.bfloat16)  33.7 us
    ppermute x30, starting transfers between devices, gather_parts(): got = lax.ppermute(buf, bit[0], partner(bit))  31.7 us
  transfers between devices with their start and end apart: 64, of which 18 were waited for; matrix products, arithmetic and copies ran while one was open for 33% of the time, Pallas kernels for 15%

profile of v5, /device:TPU:0, one launch (start us, length us, event | category | flops | bytes accessed | tf_op | source)
XLA Modules:
  0.0 1042.4 jit_solution(2242547167342437032)
XLA Ops:
  22.6 30.7 %all-gather.1 = bf16[8,1,1152]{2,1,0:T(2,128)(2,1)S(1)} all-gather(bf16[1,1,1152]{2,1,0:T(2,128)(2,1)S(1)} %reshape.2310), channel_id=2, replica_groups=mesh['seq'=4,'dp'=8] {'dp'}, dimensions={0}, use_global_device_ids=true | all-gather | bytes 20736 | tf_op jit(solution)/shard_map/all_gather | solution.py:158
  111.1 5.3 collective-permute-done.22
  170.1 70.7 %shard_map.323 = (bf16[1,1024,768]{2,1,0:T(8,128)(2,1)}, f32[1,12,1024,1]{3,2,1,0:T(8,128)}) custom-call(s32[1,1024,3]{2,1,0:T(8,128)} %pad_add_fusion.bounds_ref, s32[6,1024,2]{2,1,0:T(8,128)} %bitcast.483, bf16[1,1024,768]{2,1,0:T(8,128)(2,1)} %add_convert_fusion.4.q_ref, bf16[1,1024,768]{2,1,0:T(8,128)(2,1)} %copy.519.k_ref, ...), custom_call_target="tpu_custom_call" | custom-call | flops 3221225472 | bytes 6291456 | tf_op jit(solution)/shard_map/pallas_call | solution.py:317
  279.8 5.3 reshape.2284
  309.7 10.2 reshape.2252
  325.0 9.4 reshape.2253
  334.5 7.5 fusion.37
  342.0 30.2 %fusion.29 = (bf16[1024,2,2,2,384,1,1]{0,4,3,2,1,6,5:T(8,128)(2,1)S(1)}, f32[1024,2,2,2,384]{0,4,3,2,1:T(8,128)}) fusion(f32[1024,2,2,2,384]{0,4,3,1,2:T(8,128)S(1)} %bitcast.439, f32[2,2,2,384]{3,2,1,0:T(2,128)S(1)} %reshape.2295), kind=kLoop, calls=%fused_computation.54 | loop fusion | flops 207618048 | bytes 31469568 | tf_op jit(solution)/shard_map/convert_element_type | solution.py:437
  372.2 9.5 fusion.34
  399.2 16.0 %fusion.114 = (f32[4,256]{1,0:T(4,128)S(1)}, f32[4,256,768]{1,0,2:T(4,128)}, f32[768]{0:T(1024)}) fusion(f32[4,256]{1,0:T(4,128)S(1)} %get-tuple-element.241, f32[4,256]{1,0:T(4,128)S(1)} %div.58, f32[768]{0:T(1024)S(1)} %reshape.2296, f32[4,256,768]{1,0,2:T(4,128)} %reshape.2258, f32[768]{0:T(1024)S(1)} %reshape.2291, f32[768]{0:T(1024)S(1)} %reshape.2290, ...), kind=kLoop, calls=%fused_computation.371 | loop fusion | flops 14153984 | bytes 12625920 | tf_op jit(solution)/shard_map/transpose(jvp())/reduce_sum | solution.py:20
  416.7 11.3 %fusion.70 = f32[2,2,2,384,1024,1,1]{4,3,2,1,5,0,6:T(8,128)} fusion(bf16[2,2,2,2,2,384,192]{6,5,4,3,2,1,0:T(8,128)(2,1)} %reshape.2252, bf16[1024,2,2,192,1,1,1]{0,3,2,1,6,5,4:T(8,128)(2,1)S(1)} %get-tuple-element.141), kind=kOutput, calls=%fused_computation.149 | convolution fusion | flops 4831838208 | bytes 18874368 | tf_op jit(solution)/shard_map/tDEc,EBDCArc->tABCr/dot_general | solution.py:138
  428.0 11.9 %copy.540 = f32[1024,2,2,2,384]{0,4,3,1,2:T(8,128)} copy(f32[1024,2,2,2,384]{0,4,1,3,2:T(8,128)} %bitcast.444) | data formatting | bytes 25165824 | tf_op jit(solution)/shard_map/tDEc,EBDCArc->tABCr/transpose | solution.py:138
  439.9 33.7 %fusion.5 = bf16[1024,2,2,768]{0,3,1,2:T(8,128)(2,1)S(1)} fusion(f32[1024,2,2,2,384]{0,4,3,1,2:T(8,128)} %copy.540, f32[2,2,768,1024,1,1,1]{3,2,4,1,0,6,5:T(8,128)} %copy-done, f32[2,2,768]{2,0,1:T(2,128)S(1)} %copy-done.67), kind=kLoop, calls=%fused_computation.7 | loop fusion | flops 229638144 | bytes 31469568 | tf_op jit(solution)/shard_map/convert_element_type | solution.py:447
  473.7 7.1 fusion.30
  480.7 7.4 fusion.39
  488.2 7.7 convolution_bitcast_fusion
  518.7 7.4 copy.534
  526.6 11.4 %reduce.32 = bf16[1024,768]{1,0:T(8,128)(2,1)} reduce(bf16[1024,1,768]{2,1,0:T(2,128)(2,1)S(1)} %bitcast.457, bf16[]{:T(256)} %broadcast.1370), dimensions={1}, to_apply=%bitcast.402.reduce_sub_computation | reduce | bytes 3145730
  546.5 11.6 %copy.578 = f32[2,2,2,2,2,384,192]{6,5,4,3,2,1,0:T(8,128)} copy(f32[2,2,2,2,2,384,192]{5,6,3,1,4,0,2:T(8,128)} %convolution_bitcast_fusion) | data formatting | bytes 18874368 | tf_op jit(solution)/shard_map/tABCr,tDEc->EBDCArc/transpose | solution.py:176
  558.0 13.5 %reshape_reshape.56 = f32[2,16,576,128]{3,2,1,0:T(8,128)} reshape(f32[2,2,2,2,2,384,192]{6,5,4,3,2,1,0:T(8,128)} %copy.578) | data formatting | bytes 18874368 | tf_op jit(solution)/shard_map/reshape;reshape | solution.py:112
  571.5 14.2 %convert_reduce_fusion = f32[2,2,2,384]{3,2,1,0:T(2,128)S(1)} fusion(f32[1024,2,2,2,384]{0,4,3,2,1:T(8,128)} %get-tuple-element.148, f32[2,2,2,384]{3,2,1,0:T(2,128)S(1)} %reshape.2295, f32[1024,2,2,2,384]{0,4,3,1,2:T(8,128)} %bitcast.440, f32[2,2,2,384,1024,1,1]{4,3,2,1,5,0,6:T(8,128)} %fusion.70), kind=kLoop, calls=%fused_computation.24 | loop fusion | flops 53474304 | bytes 37773312 | tf_op jit(solution)/shard_map/reduce_sum | solution.py:448
  585.8 8.2 copy.576
  593.9 11.0 %reshape_reshape.55 = f32[2,16,576,128]{3,2,1,0:T(8,128)} reshape(f32[2,2,2,2,2,96,768]{6,5,4,3,2,1,0:T(8,128)} %copy.576) | data formatting | bytes 18874368 | tf_op jit(solution)/shard_map/reshape;reshape | solution.py:112
  616.7 87.4 %shard_map.324 = (bf16[1,1024,768]{2,1,0:T(8,128)(2,1)}, bf16[1,1024,768]{2,1,0:T(8,128)(2,1)}, bf16[1,1024,768]{2,1,0:T(8,128)(2,1)}) custom-call(s32[1,1024,3]{2,1,0:T(8,128)} %pad_add_fusion.bounds_ref, s32[6,1024,2]{2,1,0:T(8,128)} %bitcast.484, bf16[1,1024,768]{2,1,0:T(8,128)(2,1)} %add_convert_fusion.4.q_ref, bf16[1,1024,768]{2,1,0:T(8,128)(2,1)} %copy.519.k_ref, ...), custom_call_target="tpu_custom_call" | custom-call | flops 8053063680 | bytes 12582912 | tf_op jit(solution)/shard_map/pallas_call | solution.py:340
  747.1 5.6 copy.561
  752.6 5.6 convolution_bitcast_fusion.4
  788.4 45.2 %all-reduce = (f32[1536]{0:T(1024)S(1)}, f32[7680]{0:T(1024)S(1)}) all-reduce(f32[1536]{0:T(1024)S(1)} %pad_maximum_fusion.30, f32[7680]{0:T(1024)S(1)} %constant_dynamic-update-slice_fusion), channel_id=1, replica_groups=mesh['seq'=4,'dp'=8] {'dp','seq'}, use_global_device_ids=true, to_apply=%region_16.17 | all-reduce | flops 9216 | bytes 73728 | tf_op jit(solution)/shard_map/psum | solution.py:184
  858.7 32.1 %collective-permute-done.46 = f32[8,144,128]{2,1,0:T(8,128)S(1)} collective-permute-done((f32[8,144,128]{2,1,0:T(8,128)S(1)}, f32[8,144,128]{2,1,0:T(8,128)S(1)}, u32[]{:S(2)}, u32[]{:S(2)}) %collective-permute-start.46) | collective-permute-done | bytes 589856 | tf_op jit(solution)/shard_map/ppermute | solution.py:116
  890.9 11.7 %collective-permute-done.31 = f32[8,144,128]{2,1,0:T(8,128)S(1)} collective-permute-done((f32[8,144,128]{2,1,0:T(8,128)S(1)}, f32[8,144,128]{2,1,0:T(8,128)S(1)}, u32[]{:S(2)}, u32[]{:S(2)}) %collective-permute-start.31) | collective-permute-done | bytes 589856 | tf_op jit(solution)/shard_map/ppermute | solution.py:116
  907.3 5.4 collective-permute-done.47
  930.8 42.1 %collective-permute-done.33 = f32[2,144,128]{2,1,0:T(8,128)S(1)} collective-permute-done((f32[2,144,128]{2,1,0:T(8,128)S(1)}, f32[2,144,128]{2,1,0:T(8,128)S(1)}, u32[]{:S(2)}, u32[]{:S(2)}) %collective-permute-start.33) | collective-permute-done | bytes 147488 | tf_op jit(solution)/shard_map/ppermute | solution.py:116
  983.8 18.8 %collective-permute-done.57 = f32[4,576,128]{2,1,0:T(8,128)S(1)} collective-permute-done((f32[4,576,128]{2,1,0:T(8,128)S(1)}, f32[4,576,128]{2,1,0:T(8,128)S(1)}, u32[]{:S(2)}, u32[]{:S(2)}) %collective-permute-start.57) | collective-permute-done | bytes 1179680 | tf_op jit(solution)/shard_map/ppermute | solution.py:116
  (611 shorter events, 434.3 us)
Async XLA Ops:
  1.6 75.3 %collective-permute-start = (bf16[1,144,128]{2,1,0:T(8,128)(2,1)S(1)}, bf16[1,144,128]{2,1,0:T(8,128)(2,1)S(1)}, u32[]{:S(2)}, u32[]{:S(2)}) collective-permute-start(bf16[1,144,128]{2,1,0:T(8,128)(2,1)S(1)} %broadcast_in_dim_reshape.18), channel_id=1, source_target_pairs={{0,4},{1,5},{2,6},{3,7},{4,0},{5,1},{6,2},{7,3},{8,12},{9,13},{10,... | collective-permute-start | bytes 110600 | tf_op jit(solution)/shard_map/ppermute | solution.py:101
  6.6 67.3 %collective-permute-start.15 = (bf16[1,144,128]{2,1,0:T(8,128)(2,1)S(1)}, bf16[1,144,128]{2,1,0:T(8,128)(2,1)}, u32[]{:S(2)}, u32[]{:S(2)}) collective-permute-start(bf16[1,144,128]{2,1,0:T(8,128)(2,1)S(1)} %broadcast_in_dim_reshape.21), channel_id=1, source_target_pairs={{0,4},{1,5},{2,6},{3,7},{4,0},{5,1},{6,2},{7,3},{8,12},{9,13},{10,... | collective-permute-start | bytes 110600 | tf_op jit(solution)/shard_map/ppermute | solution.py:101
  7.6 66.3 %collective-permute-start.10 = (bf16[1,144,128]{2,1,0:T(8,128)(2,1)S(1)}, bf16[1,144,128]{2,1,0:T(8,128)(2,1)}, u32[]{:S(2)}, u32[]{:S(2)}) collective-permute-start(bf16[1,144,128]{2,1,0:T(8,128)(2,1)S(1)} %broadcast_in_dim_reshape.20), channel_id=1, source_target_pairs={{0,4},{1,5},{2,6},{3,7},{4,0},{5,1},{6,2},{7,3},{8,12},{9,13},{10,... | collective-permute-start | bytes 110600 | tf_op jit(solution)/shard_map/ppermute | solution.py:101
  11.5 65.6 %collective-permute-start.5 = (bf16[1,144,128]{2,1,0:T(8,128)(2,1)S(1)}, bf16[1,144,128]{2,1,0:T(8,128)(2,1)}, u32[]{:S(2)}, u32[]{:S(2)}) collective-permute-start(bf16[1,144,128]{2,1,0:T(8,128)(2,1)S(1)} %broadcast_in_dim_reshape.19), channel_id=1, source_target_pairs={{0,4},{1,5},{2,6},{3,7},{4,0},{5,1},{6,2},{7,3},{8,12},{9,13},{10,... | collective-permute-start | bytes 110600 | tf_op jit(solution)/shard_map/ppermute | solution.py:101
  12.8 73.7 %collective-permute-start.25 = (bf16[1,576,128]{2,1,0:T(8,128)(2,1)S(1)}, bf16[1,576,128]{2,1,0:T(8,128)(2,1)}, u32[]{:S(2)}, u32[]{:S(2)}) collective-permute-start(bf16[1,576,128]{2,1,0:T(8,128)(2,1)S(1)} %broadcast_in_dim_reshape.23), channel_id=1, source_target_pairs={{0,4},{1,5},{2,6},{3,7},{4,0},{5,1},{6,2},{7,3},{8,12},{9,13},{10,... | collective-permute-start | bytes 442376 | tf_op jit(solution)/shard_map/ppermute | solution.py:101
  18.3 116.5 %all-to-all-start = ((bf16[4,256,768]{1,2,0:T(8,128)(2,1)}), bf16[4,256,768]{1,2,0:T(8,128)(2,1)S(1)}, u32[]{:S(2)}, u32[]{:S(2)}) async-start(bf16[4,256,768]{1,2,0:T(8,128)(2,1)} %copy.503), calls=%async_computation | async-start | bytes 3145728 | tf_op jit(solution)/shard_map/all_to_all | solution.py:404
  117.8 129.2 %collective-permute-start.23 = (bf16[8,576,128]{2,1,0:T(8,128)(2,1)}, bf16[8,576,128]{2,1,0:T(8,128)(2,1)}, u32[]{:S(2)}, u32[]{:S(2)}) collective-permute-start(bf16[8,576,128]{2,1,0:T(8,128)(2,1)} %pad_maximum_fusion.8), channel_id=1, source_target_pairs={{0,2},{1,3},{2,0},{3,1},{4,6},{5,7},{6,4},{7,5},{8,10},{9,11},{10,... | collective-permute-start | bytes 3538952 | tf_op jit(solution)/shard_map/ppermute | solution.py:101
  121.2 130.3 %collective-permute-start.28 = (bf16[8,576,128]{2,1,0:T(8,128)(2,1)}, bf16[8,576,128]{2,1,0:T(8,128)(2,1)}, u32[]{:S(2)}, u32[]{:S(2)}) collective-permute-start(bf16[8,576,128]{2,1,0:T(8,128)(2,1)} %pad_maximum_fusion.9), channel_id=1, source_target_pairs={{0,1},{1,0},{2,3},{3,2},{4,5},{5,4},{6,7},{7,6},{8,9},{9,8},{10,11... | collective-permute-start | bytes 3538952 | tf_op jit(solution)/shard_map/ppermute | solution.py:101
  134.8 121.3 %all-to-all-start.2 = ((bf16[4,256,768]{1,2,0:T(8,128)(2,1)}), bf16[4,256,768]{1,2,0:T(8,128)(2,1)}, u32[]{:S(2)}, u32[]{:S(2)}) async-start(bf16[4,256,768]{1,2,0:T(8,128)(2,1)} %copy.535), calls=%async_computation.2 | async-start | bytes 3145728 | tf_op jit(solution)/shard_map/all_to_all | solution.py:404
  251.0 54.1 %collective-permute-start.24 = (bf16[16,576,128]{2,1,0:T(8,128)(2,1)}, bf16[16,576,128]{2,1,0:T(8,128)(2,1)}, u32[]{:S(2)}, u32[]{:S(2)}) collective-permute-start(bf16[16,576,128]{2,1,0:T(8,128)(2,1)} %pad_maximum_fusion.2), channel_id=1, source_target_pairs={{0,8},{8,0},{16,24},{24,16},{1,9},{9,1},{17,25},{25,17},{2,10},{10... | collective-permute-start | bytes 7077896 | tf_op jit(solution)/shard_map/ppermute | solution.py:101
  255.6 64.2 %collective-permute-start.29 = (bf16[16,576,128]{2,1,0:T(8,128)(2,1)}, bf16[16,576,128]{2,1,0:T(8,128)(2,1)}, u32[]{:S(2)}, u32[]{:S(2)}) collective-permute-start(bf16[16,576,128]{2,1,0:T(8,128)(2,1)} %pad_maximum_fusion.3), channel_id=1, source_target_pairs={{0,8},{8,0},{16,24},{24,16},{1,9},{9,1},{17,25},{25,17},{2,10},{10... | collective-permute-start | bytes 7077896 | tf_op jit(solution)/shard_map/ppermute | solution.py:101
  541.7 294.8 %all-to-all-start.1 = ((bf16[4,2,98304]{2,1,0:T(2,128)(2,1)}), bf16[4,2,98304]{2,1,0:T(2,128)(2,1)}, u32[]{:S(2)}, u32[]{:S(2)}) async-start(bf16[4,2,98304]{2,1,0:T(2,128)(2,1)} %reshape.2350), calls=%async_computation.1 | async-start | bytes 3145728 | tf_op jit(solution)/shard_map/all_to_all | solution.py:407
  713.7 134.7 %collective-permute-start.45 = (f32[16,144,128]{2,1,0:T(8,128)}, f32[16,144,128]{2,1,0:T(8,128)}, u32[]{:S(2)}, u32[]{:S(2)}) collective-permute-start(f32[16,144,128]{2,1,0:T(8,128)} %dynamic-slice_bitcast_fusion.6), channel_id=1, source_target_pairs={{0,8},{8,0},{16,24},{24,16},{1,9},{9,1},{17,25},{25,17},{2,10},{10... | collective-permute-start | bytes 3538952 | tf_op jit(solution)/shard_map/ppermute | solution.py:116
  735.2 115.4 %collective-permute-start.30 = (f32[16,144,128]{2,1,0:T(8,128)}, f32[16,144,128]{2,1,0:T(8,128)}, u32[]{:S(2)}, u32[]{:S(2)}) collective-permute-start(f32[16,144,128]{2,1,0:T(8,128)} %dynamic-slice_bitcast_fusion.9), channel_id=1, source_target_pairs={{0,8},{8,0},{16,24},{24,16},{1,9},{9,1},{17,25},{25,17},{2,10},{10... | collective-permute-start | bytes 3538952 | tf_op jit(solution)/shard_map/ppermute | solution.py:116
  774.9 79.0 %collective-permute-start.35 = (f32[16,144,128]{2,1,0:T(8,128)}, f32[16,144,128]{2,1,0:T(8,128)}, u32[]{:S(2)}, u32[]{:S(2)}) collective-permute-start(f32[16,144,128]{2,1,0:T(8,128)} %dynamic-slice_bitcast_fusion.8), channel_id=1, source_target_pairs={{0,8},{8,0},{16,24},{24,16},{1,9},{9,1},{17,25},{25,17},{2,10},{10... | collective-permute-start | bytes 3538952 | tf_op jit(solution)/shard_map/ppermute | solution.py:116
  785.5 128.4 %collective-permute-start.55 = (f32[16,576,128]{2,1,0:T(8,128)}, f32[16,576,128]{2,1,0:T(8,128)}, u32[]{:S(2)}, u32[]{:S(2)}) collective-permute-start(f32[16,576,128]{2,1,0:T(8,128)} %dynamic-slice_bitcast_fusion), channel_id=1, source_target_pairs={{0,8},{8,0},{16,24},{24,16},{1,9},{9,1},{17,25},{25,17},{2,10},{10... | collective-permute-start | bytes 14155784 | tf_op jit(solution)/shard_map/ppermute | solution.py:116
  785.5 132.0 %collective-permute-start.50 = (f32[16,576,128]{2,1,0:T(8,128)}, f32[16,576,128]{2,1,0:T(8,128)}, u32[]{:S(2)}, u32[]{:S(2)}) collective-permute-start(f32[16,576,128]{2,1,0:T(8,128)} %dynamic-slice_bitcast_fusion.1), channel_id=1, source_target_pairs={{0,8},{8,0},{16,24},{24,16},{1,9},{9,1},{17,25},{25,17},{2,10},{10... | collective-permute-start | bytes 14155784 | tf_op jit(solution)/shard_map/ppermute | solution.py:116
  836.5 193.6 %all-to-all-start.3 = ((f32[1,1024,768]{2,0,1:T(1,128)}), f32[1,1024,768]{2,0,1:T(1,128)S(1)}, u32[]{:S(2)}, u32[]{:S(2)}) async-start(f32[1,1024,768]{2,0,1:T(1,128)} %copy.561), calls=%async_computation.3 | async-start | bytes 6291456 | tf_op jit(solution)/shard_map/all_to_all | solution.py:407
  850.6 40.1 %collective-permute-start.46 = (f32[8,144,128]{2,1,0:T(8,128)S(1)}, f32[8,144,128]{2,1,0:T(8,128)S(1)}, u32[]{:S(2)}, u32[]{:S(2)}) collective-permute-start(f32[8,144,128]{2,1,0:T(8,128)S(1)} %dynamic-slice_bitcast_fusion.12), channel_id=1, source_target_pairs={{0,16},{8,24},{16,0},{24,8},{1,17},{9,25},{17,1},{25,9},{2,18},{10... | collective-permute-start | bytes 1769480 | tf_op jit(solution)/shard_map/ppermute | solution.py:116
  853.9 48.7 %collective-permute-start.31 = (f32[8,144,128]{2,1,0:T(8,128)S(1)}, f32[8,144,128]{2,1,0:T(8,128)S(1)}, u32[]{:S(2)}, u32[]{:S(2)}) collective-permute-start(f32[8,144,128]{2,1,0:T(8,128)S(1)} %dynamic-slice_bitcast_fusion.15), channel_id=1, source_target_pairs={{0,16},{8,24},{16,0},{24,8},{1,17},{9,25},{17,1},{25,9},{2,18},{10... | collective-permute-start | bytes 1769480 | tf_op jit(solution)/shard_map/ppermute | solution.py:116
  856.1 49.6 %collective-permute-start.36 = (f32[8,144,128]{2,1,0:T(8,128)S(1)}, f32[8,144,128]{2,1,0:T(8,128)S(1)}, u32[]{:S(2)}, u32[]{:S(2)}) collective-permute-start(f32[8,144,128]{2,1,0:T(8,128)S(1)} %dynamic-slice_bitcast_fusion.14), channel_id=1, source_target_pairs={{0,1},{1,0},{2,3},{3,2},{4,5},{5,4},{6,7},{7,6},{8,9},{9,8},{10,11... | collective-permute-start | bytes 1769480 | tf_op jit(solution)/shard_map/ppermute | solution.py:116
  906.5 19.0 %collective-permute-start.37 = (f32[4,144,128]{2,1,0:T(8,128)}, f32[4,144,128]{2,1,0:T(8,128)}, u32[]{:S(2)}, u32[]{:S(2)}) collective-permute-start(f32[4,144,128]{2,1,0:T(8,128)} %dynamic-slice_bitcast_fusion.18), channel_id=1, source_target_pairs={{0,2},{1,3},{2,0},{3,1},{4,6},{5,7},{6,4},{7,5},{8,10},{9,11},{10,... | collective-permute-start | bytes 884744 | tf_op jit(solution)/shard_map/ppermute | solution.py:116
  917.5 58.5 %collective-permute-start.56 = (f32[8,576,128]{2,1,0:T(8,128)S(1)}, f32[8,576,128]{2,1,0:T(8,128)S(1)}, u32[]{:S(2)}, u32[]{:S(2)}) collective-permute-start(f32[8,576,128]{2,1,0:T(8,128)S(1)} %dynamic-slice_bitcast_fusion.2), channel_id=1, source_target_pairs={{0,2},{1,3},{2,0},{3,1},{4,6},{5,7},{6,4},{7,5},{8,10},{9,11},{10,... | collective-permute-start | bytes 7077896 | tf_op jit(solution)/shard_map/ppermute | solution.py:116
  922.4 55.6 %collective-permute-start.51 = (f32[8,576,128]{2,1,0:T(8,128)S(1)}, f32[8,576,128]{2,1,0:T(8,128)S(1)}, u32[]{:S(2)}, u32[]{:S(2)}) collective-permute-start(f32[8,576,128]{2,1,0:T(8,128)S(1)} %dynamic-slice_bitcast_fusion.3), channel_id=1, source_target_pairs={{0,1},{1,0},{2,3},{3,2},{4,5},{5,4},{6,7},{7,6},{8,9},{9,8},{10,11... | collective-permute-start | bytes 7077896 | tf_op jit(solution)/shard_map/ppermute | solution.py:116
  925.5 47.4 %collective-permute-start.33 = (f32[2,144,128]{2,1,0:T(8,128)S(1)}, f32[2,144,128]{2,1,0:T(8,128)S(1)}, u32[]{:S(2)}, u32[]{:S(2)}) collective-permute-start(f32[2,144,128]{2,1,0:T(8,128)S(1)} %dynamic-slice_bitcast_fusion.23), channel_id=1, source_target_pairs={{0,2},{1,3},{2,0},{3,1},{4,6},{5,7},{6,4},{7,5},{8,10},{9,11},{10,... | collective-permute-start | bytes 442376 | tf_op jit(solution)/shard_map/ppermute | solution.py:116
  927.1 47.4 %collective-permute-start.38 = (f32[2,144,128]{2,1,0:T(8,128)S(1)}, f32[2,144,128]{2,1,0:T(8,128)S(1)}, u32[]{:S(2)}, u32[]{:S(2)}) collective-permute-start(f32[2,144,128]{2,1,0:T(8,128)S(1)} %dynamic-slice_bitcast_fusion.22), channel_id=1, source_target_pairs={{0,16},{8,24},{16,0},{24,8},{1,17},{9,25},{17,1},{25,9},{2,18},{10... | collective-permute-start | bytes 442376 | tf_op jit(solution)/shard_map/ppermute | solution.py:116
  929.8 49.5 %collective-permute-start.43 = (f32[2,144,128]{2,1,0:T(8,128)S(1)}, f32[2,144,128]{2,1,0:T(8,128)S(1)}, u32[]{:S(2)}, u32[]{:S(2)}) collective-permute-start(f32[2,144,128]{2,1,0:T(8,128)S(1)} %dynamic-slice_bitcast_fusion.21), channel_id=1, source_target_pairs={{0,1},{1,0},{2,3},{3,2},{4,5},{5,4},{6,7},{7,6},{8,9},{9,8},{10,11... | collective-permute-start | bytes 442376 | tf_op jit(solution)/shard_map/ppermute | solution.py:116
  976.0 34.0 %collective-permute-start.39 = (f32[1,144,128]{2,1,0:T(8,128)S(1)}, f32[1,144,128]{2,1,0:T(8,128)S(1)}, u32[]{:S(2)}, u32[]{:S(2)}) collective-permute-start(f32[1,144,128]{2,1,0:T(8,128)S(1)} %constant_dynamic-slice_fusion.4), channel_id=1, source_target_pairs={{0,4},{1,5},{2,6},{3,7},{4,0},{5,1},{6,2},{7,3},{8,12},{9,13},{10,... | collective-permute-start | bytes 221192 | tf_op jit(solution)/shard_map/ppermute | solution.py:116
  978.0 24.6 %collective-permute-start.57 = (f32[4,576,128]{2,1,0:T(8,128)S(1)}, f32[4,576,128]{2,1,0:T(8,128)S(1)}, u32[]{:S(2)}, u32[]{:S(2)}) collective-permute-start(f32[4,576,128]{2,1,0:T(8,128)S(1)} %dynamic-slice_bitcast_fusion.4), channel_id=1, source_target_pairs={{0,16},{8,24},{16,0},{24,8},{1,17},{9,25},{17,1},{25,9},{2,18},{10... | collective-permute-start | bytes 3538952 | tf_op jit(solution)/shard_map/ppermute | solution.py:116
  979.3 29.7 %collective-permute-start.52 = (f32[4,576,128]{2,1,0:T(8,128)S(1)}, f32[4,576,128]{2,1,0:T(8,128)S(1)}, u32[]{:S(2)}, u32[]{:S(2)}) collective-permute-start(f32[4,576,128]{2,1,0:T(8,128)S(1)} %dynamic-slice_bitcast_fusion.5), channel_id=1, source_target_pairs={{0,2},{1,3},{2,0},{3,1},{4,6},{5,7},{6,4},{7,5},{8,10},{9,11},{10,... | collective-permute-start | bytes 3538952 | tf_op jit(solution)/shard_map/ppermute | solution.py:116
  980.9 43.0 %collective-permute-start.44 = (f32[1,144,128]{2,1,0:T(8,128)S(1)}, f32[1,144,128]{2,1,0:T(8,128)S(1)}, u32[]{:S(2)}, u32[]{:S(2)}) collective-permute-start(f32[1,144,128]{2,1,0:T(8,128)S(1)} %constant_dynamic-slice_fusion.3), channel_id=1, source_target_pairs={{0,4},{1,5},{2,6},{3,7},{4,0},{5,1},{6,2},{7,3},{8,12},{9,13},{10,... | collective-permute-start | bytes 221192 | tf_op jit(solution)/shard_map/ppermute | solution.py:116
  1014.7 20.6 %collective-permute-start.59 = (f32[1,576,128]{2,1,0:T(8,128)}, f32[1,576,128]{2,1,0:T(8,128)S(1)}, u32[]{:S(2)}, u32[]{:S(2)}) collective-permute-start(f32[1,576,128]{2,1,0:T(8,128)} %constant_dynamic-slice_fusion), channel_id=1, source_target_pairs={{0,4},{1,5},{2,6},{3,7},{4,0},{5,1},{6,2},{7,3},{8,12},{9,13},{10,... | collective-permute-start | bytes 884744 | tf_op jit(solution)/shard_map/ppermute | solution.py:116
  (128 other events, 1188.1 us)

commit v6 on v4

--- a/solution.py
+++ b/solution.py
@@ -69,33 +69,28 @@
     return [(i, i ^ (1 << b)) for i in range(lax.axis_size(axis))]
 
 
-N_PARTS = 3
 LANES = 128
-
-
-def to_order(blocked, order):
+LETTERS = "ABCDEFGHIJKLMNOP"
+
+
+def letters():
     canon = canonical_bits()
-    rest = blocked.shape[1:]
-    x = blocked.reshape([2] * len(canon) + list(rest))
-    perm = [canon.index(bit) for bit in order] + list(range(len(canon), len(canon) + len(rest)))
-    return x.transpose(perm).reshape(blocked.shape)
-
-
-def from_order(blocked, order):
-    canon = canonical_bits()
-    rest = blocked.shape[1:]
-    x = blocked.reshape([2] * len(canon) + list(rest))
-    perm = [order.index(bit) for bit in canon] + list(range(len(canon), len(canon) + len(rest)))
-    return x.transpose(perm).reshape(blocked.shape)
-
-
-def lane_rows(flat_blocks):
-    n, width = flat_blocks.shape
-    rows = -(-width // LANES)
-    pad = rows * LANES - width
-    if pad:
-        flat_blocks = jnp.concatenate([flat_blocks, jnp.zeros((n, pad), flat_blocks.dtype)], axis=1)
-    return flat_blocks.reshape(n, rows, LANES)
+    return {bit: LETTERS[i] for i, bit in enumerate(canon)}
+
+
+def dp_letters():
+    names = letters()
+    return "".join(names[bit] for bit in canonical_bits() if bit[0] == "dp")
+
+
+def seq_letters():
+    names = letters()
+    return "".join(names[bit] for bit in canonical_bits() if bit[0] == "seq")
+
+
+def order_letters(order):
+    names = letters()
+    return "".join(names[bit] for bit in order)
 
 
 def gather_parts(parts, orders):
@@ -123,85 +118,110 @@
     return out
 
 
+def lane_flat(array):
+    size = array.size
+    assert size % LANES == 0
+    return array.reshape(size // LANES, LANES)
+
+
+def lane_pad(flat):
+    rows = -(-flat.shape[-1] // LANES)
+    pad = rows * LANES - flat.shape[-1]
+    if pad:
+        flat = jnp.concatenate([flat, jnp.zeros(flat.shape[:-1] + (pad,), flat.dtype)], axis=-1)
+    return flat.reshape(flat.shape[:-1] + (rows, LANES))
+
+
+def full_matrix(blocks, order, rb, cb):
+    canon = canonical_bits()
+    kd = len(dp_letters())
+    x = blocks.reshape((2,) * len(canon) + (rb, cb))
+    dp_axes = [order.index(bit) for bit in canon[:kd]]
+    seq_axes = [order.index(bit) for bit in canon[kd:]]
+    n = len(canon)
+    x = x.transpose(dp_axes + [n] + seq_axes + [n + 1])
+    return x.reshape((1 << kd) * rb, (1 << (n - kd)) * cb)
+
+
+def part_blocks(matrix, order, rb, cb):
+    canon = canonical_bits()
+    kd = len(dp_letters())
+    n = len(canon)
+    x = matrix.reshape((2,) * kd + (rb,) + (2,) * (n - kd) + (cb,))
+    where = {bit: (i if i < kd else i + 1) for i, bit in enumerate(canon)}
+    x = x.transpose([where[bit] for bit in order] + [kd, n + 1])
+    return x.reshape(1 << n, rb * cb)
+
+
 def gather_weights(matrices, vectors):
+    orders = bit_orders(len(matrices))
+    parts = []
+    for index, m in enumerate(matrices):
+        flat = m.reshape(-1)
+        if index == 0 and vectors:
+            flat = jnp.concatenate([flat] + [v.reshape(-1) for v in vectors])
+        parts.append(lane_pad(flat))
+    got = gather_parts(parts, orders)
+    full = []
+    for index, (buf, m, order) in enumerate(zip(got, matrices, orders)):
+        rb, cb = m.shape
+        flat = buf.reshape(buf.shape[0], -1)
+        full.append(full_matrix(flat[:, :rb * cb], order, rb, cb))
+    vecs = []
+    if vectors:
+        flat = got[0].reshape(got[0].shape[0], -1)
+        offset = matrices[0].size
+        canon = canonical_bits()
+        kd = len(dp_letters())
+        n = len(canon)
+        for v in vectors:
+            piece = flat[:, offset:offset + v.size].reshape((2,) * n + (v.size,))
+            perm = [orders[0].index(bit) for bit in canon] + [n]
+            piece = piece.transpose(perm).reshape(1 << kd, 1 << (n - kd), v.size)[:, 0]
+            vecs.append(piece.reshape(-1))
+            offset += v.size
+    return full, vecs
+
+
+def inner_rows(left, right):
+    return lax.dot_general(left, right, (((0,), (0,)), ((), ())), preferred_element_type=jnp.float32)
+
+
+def reduce_grads(pairs, vectors):
     n_dp, n_seq = lax.axis_size("dp"), lax.axis_size("seq")
-    orders = bit_orders(N_PARTS)
-    parts, layout = [], []
-    for part in range(N_PARTS):
-        items = []
-        for m in matrices:
-            third = m.shape[0] // N_PARTS
-            items.append(m[part * third:(part + 1) * third].reshape(-1))
-        if part == 0:
-            items += [v.reshape(-1) for v in vectors]
-        sizes = [item.size for item in items]
-        parts.append(lane_rows(jnp.concatenate(items)[None])[0])
-        layout.append(sizes)
-    got = gather_parts(parts, orders)
-    canon = []
-    for buf, order, sizes in zip(got, orders, layout):
-        flat = from_order(buf, order).reshape(n_dp * n_seq, -1)
-        pieces, offset = [], 0
-        for size in sizes:
-            pieces.append(flat[:, offset:offset + size])
-            offset += size
-        canon.append(pieces)
-    full = []
-    for index, m in enumerate(matrices):
-        third = m.shape[0] // N_PARTS
-        stacked = jnp.stack(
-            [canon[part][index].reshape(n_dp, n_seq, third, m.shape[1]) for part in range(N_PARTS)], axis=2
-        )
-        full.append(stacked.transpose(0, 2, 3, 1, 4).reshape(n_dp * m.shape[0], n_seq * m.shape[1]))
+    orders = bit_orders(len(pairs))
+    parts, shapes = [], []
+    for index, ((left, right), order) in enumerate(zip(pairs, orders)):
+        rb, cb = left.shape[1] // n_dp, right.shape[1] // n_seq
+        blocks = part_blocks(inner_rows(left, right), order, rb, cb)
+        if index == 0 and vectors:
+            extra = []
+            for v in vectors:
+                piece = v.reshape(n_dp, 1, v.size // n_dp)
+                piece = jnp.broadcast_to(piece, (n_dp, n_seq, v.size // n_dp)).reshape(n_dp * n_seq, -1)
+                extra.append(part_blocks_rows(piece, order))
+            blocks = jnp.concatenate([blocks] + extra, axis=1)
+        parts.append(lane_pad(blocks))
+        shapes.append((rb, cb))
+    summed = reduce_parts(parts, orders)
+    own = [s.reshape(-1)[:rb * cb].reshape(rb, cb) for s, (rb, cb) in zip(summed, shapes)]
     vecs = []
-    for index, v in enumerate(vectors):
-        piece = canon[0][len(matrices) + index]
-        vecs.append(piece.reshape(n_dp, n_seq, v.size)[:, 0].reshape(-1))
-    return full, vecs
-
-
-def blocked_grad(left, right, n_dp, n_seq):
-    tokens = left.shape[0]
-    a = left.reshape(tokens, n_dp, left.shape[1] // n_dp)
-    b = right.reshape(tokens, n_seq, right.shape[1] // n_seq)
-    return jnp.einsum("tar,tbc->abrc", a, b, preferred_element_type=jnp.float32)
-
-
-def reduce_grads(matrices, vectors):
-    n_dp, n_seq = lax.axis_size("dp"), lax.axis_size("seq")
-    orders = bit_orders(N_PARTS)
-    parts, layout = [], []
-    for part in range(N_PARTS):
-        items = []
-        for m in matrices:
-            third = m.shape[2] // N_PARTS
-            items.append(m[:, :, part * third:(part + 1) * third].reshape(n_dp * n_seq, -1))
-        if part == 0:
-            for v in vectors:
-                v = v.reshape(n_dp, 1, -1)
-                items.append(jnp.broadcast_to(v, (n_dp, n_seq, v.shape[-1])).reshape(n_dp * n_seq, -1))
-        sizes = [item.shape[1] for item in items]
-        parts.append(to_order(lane_rows(jnp.concatenate(items, axis=1)), orders[part]))
-        layout.append(sizes)
-    summed = reduce_parts(parts, orders)
-    pieces_by_part = []
-    for buf, sizes in zip(summed, layout):
-        flat = buf.reshape(-1)
-        pieces, offset = [], 0
-        for size in sizes:
-            pieces.append(flat[offset:offset + size])
-            offset += size
-        pieces_by_part.append(pieces)
-    own = []
-    for index, m in enumerate(matrices):
-        third = m.shape[2] // N_PARTS
-        own.append(
-            jnp.concatenate(
-                [pieces_by_part[part][index].reshape(third, m.shape[3]) for part in range(N_PARTS)], axis=0
-            )
-        )
-    vecs = [pieces_by_part[0][len(matrices) + index] for index in range(len(vectors))]
+    if vectors:
+        flat = summed[0].reshape(-1)
+        offset = shapes[0][0] * shapes[0][1]
+        for v in vectors:
+            piece = v.size // n_dp
+            vecs.append(flat[offset:offset + piece])
+            offset += piece
     return own, vecs
+
+
+def part_blocks_rows(blocked, order):
+    canon = canonical_bits()
+    n = len(canon)
+    x = blocked.reshape((2,) * n + blocked.shape[1:])
+    x = x.transpose([canon.index(bit) for bit in order] + [n])
+    return x.reshape(blocked.shape)
 
 
 TQ = 256
@@ -363,12 +383,6 @@
             bytes_accessed=8 * batch * length * width * 2,
         ),
     )(bounds, bits, q, k, v, do, lse)
-
-
-def times_back(left, matrix):
-    return lax.dot_general(
-        left, matrix, (((1,), (1,)), ((), ())), preferred_element_type=jnp.float32
-    )
 
 
 def shards(
@@ -458,20 +472,17 @@
     grad_mixed, grad_gain_two, grad_shift_two = norm_two_back(grad_out)
     grad_lower = grad_mixed.astype(jnp.bfloat16)
     grad_b_down = jnp.sum(grad_lower.astype(jnp.float32), axis=0)
-    grad_w_down = blocked_grad(active, grad_lower, n_dp, n_seq)
     grad_upper = gelu_back(times_back(grad_lower, full_down))[0].astype(jnp.bfloat16)
     grad_b_up = jnp.sum(grad_upper.astype(jnp.float32), axis=0)
-    grad_w_up = blocked_grad(normed_low, grad_upper, n_dp, n_seq)
     grad_normed = grad_mixed + times_back(grad_upper, full_up)
     norm_one_back = jax.vjp(layer_norm, hidden, vec_gain_one, vec_shift_one)[1]
     grad_hidden, grad_gain_one, grad_shift_one = norm_one_back(grad_normed)
     grad_branch = grad_hidden.astype(jnp.bfloat16)
     grad_b_out = jnp.sum(grad_branch.astype(jnp.float32), axis=0)
-    grad_w_out = blocked_grad(context_tok, grad_branch, n_dp, n_seq)
     (own_w_out, own_w_up, own_w_down), (
         own_b_out, own_gain_one, own_shift_one, own_b_up, own_b_down, own_gain_two, own_shift_two,
     ) = reduce_grads(
-        [grad_w_out, grad_w_up, grad_w_down],
+        [(context_tok, grad_branch), (normed_low, grad_upper), (active, grad_lower)],
         [grad_b_out, grad_gain_one, grad_shift_one, grad_b_up, grad_b_down, grad_gain_two, grad_shift_two],
     )
     grad_context = times_back(grad_branch, full_out).astype(jnp.bfloat16)
@@ -490,13 +501,10 @@
         + times_back(grad_v, full_value)
     )
     grad_tokens = token_owners(grad_inputs.reshape(mine, seq_len, width))
-    grad_w_query = blocked_grad(flat, grad_q, n_dp, n_seq)
     grad_b_query = jnp.sum(grad_q.astype(jnp.float32), axis=0)
-    grad_w_key = blocked_grad(flat, grad_k, n_dp, n_seq)
-    grad_w_value = blocked_grad(flat, grad_v, n_dp, n_seq)
     grad_b_value = jnp.sum(grad_v.astype(jnp.float32), axis=0)
     (own_w_query, own_w_key, own_w_value), (own_b_query, own_b_value) = reduce_grads(
-        [grad_w_query, grad_w_key, grad_w_value], [grad_b_query, grad_b_value]
+        [(flat, grad_q), (flat, grad_k), (flat, grad_v)], [grad_b_query, grad_b_value]
     )
     return (
         out_tokens,

time: 960 us -> 966 us (level)
  waiting for transfers between devices: 116 us -> 158 us
  other arithmetic: 103 us -> 83.1 us
  local copies, waits for them, and re-layouts: 353 us -> 343 us
    reshape x59 -> x29, local copies, waits for them, and re-layouts: 83.5 us -> 134 us  [the longest x9 75 us: part_blocks(): x = matrix.reshape((2,) * kd + (rb,) + (2,) * (n - kd) + (cb,))]
    slice x57 -> x10, local copies, waits for them, and re-layouts: 50.1 us -> 4.25 us  [the longest x2 2.18 us: gather_weights(): full.append(full_matrix(flat[:, :rb * cb], order, rb, cb))]
    unnamed x274 -> x189, local copies, waits for them, and re-layouts: 67.1 us -> 28 us
    ppermute x30, waiting for transfers between devices: 105 us -> 132 us  [reduce_parts(): buf = keep + lax.ppermute(send, bit[0], partner(bit))]
    another operation x31 -> x23, local copies, waits for them, and re-layouts: 53.4 us -> 74.3 us  [the longest x5 36.5 us: reduce_parts(): half = buf.reshape((2, buf.shape[0] // 2) + buf.shape[1:])]
    transpose x5 -> x0, other arithmetic: 12.9 us -> none  [gather_weights(): stacked.transpose(0, 2, 3, 1, 4)]
    ppermute x30, waiting for transfers between devices: 10.6 us -> 22.4 us  [gather_parts(): got = lax.ppermute(buf, bit[0], partner(bit))]
    transpose x16 -> x14, local copies, waits for them, and re-layouts: 24.8 us -> 35.9 us  [the longest x4 19.2 us: full_matrix(): x = x.transpose(dp_axes + [n] + seq_axes + [n + 1])]
  transfers between devices with their start and end apart: 64 -> 64, of which waited for: 22 -> 24; matrix products, arithmetic and copies ran while one was open for 32% -> 35% of each run, Pallas kernels for 0% -> 7%
where the time goes in v6:
time: 966 us; the launch traced here: 951 us
  local copies, waits for them, and re-layouts  343 us (36%)
  waiting for transfers between devices  158 us (16%)
  Pallas kernels  158 us (16%)
  matrix products  124 us (13%)
  other arithmetic  83.1 us (9%)
  starting transfers between devices  81.5 us (8%)
    ppermute x30, waiting for transfers between devices, reduce_parts(): buf = keep + lax.ppermute(send, bit[0], partner(bit))  132 us
    pallas_call x1, Pallas kernels, attention_backward(): pl.pallas_call(attn_bwd_kernel, grid=(batch, pairs, length // rows), in_s...  87.6 us
    reshape x9, local copies, waits for them, and re-layouts, part_blocks(): x = matrix.reshape((2,) * kd + (rb,) + (2,) * (n - kd) + (cb,))  75 us
    pallas_call x1, Pallas kernels, attention_forward(): pl.pallas_call(attn_fwd_kernel, grid=(batch, pairs, length // rows), in_s...  70.9 us
    dot_general x6, matrix products, times_back(): lax.dot_general(left, matrix, (((1,), (1,)), ((), ())), preferred_element...  40.8 us
    reshape x6, local copies, waits for them, and re-layouts, full_matrix(): return x.reshape((1 << kd) * rb, (1 << n - kd) * cb)  39.3 us
    dot_general x1, matrix products, shards(): jnp.dot(normed_low, full_up, preferred_element_type=jnp.float32) + vec_up  37.6 us
    another operation x5, local copies, waits for them, and re-layouts, reduce_parts(): half = buf.reshape((2, buf.shape[0] // 2) + buf.shape[1:])  36.5 us
  transfers between devices with their start and end apart: 64, of which 24 were waited for; matrix products, arithmetic and copies ran while one was open for 35% of the time, Pallas kernels for 7%

profile of v6, /device:TPU:0, one launch (start us, length us, event | category | flops | bytes accessed | tf_op | source)
XLA Modules:
  0.0 951.3 jit_solution(18111469620576001199)
XLA Ops:
  139.4 70.9 %shard_map.323 = (bf16[1,1024,768]{2,1,0:T(8,128)(2,1)}, f32[1,12,1024,1]{3,2,1,0:T(8,128)}) custom-call(s32[1,1024,3]{2,1,0:T(8,128)} %pad_add_fusion.bounds_ref, s32[6,1024,2]{2,1,0:T(8,128)} %bitcast.430, bf16[1,1024,768]{2,1,0:T(8,128)(2,1)} %fusion.19.q_ref, bf16[1,1024,768]{2,1,0:T(8,128)(2,1)} %fusion.18.k_ref, bf16[1,1024,768]{2,1,0:T(8,128)(2,1)} %fusion.20.v_ref), custom_call_target="tpu_custom_call" | custom-call | flops 3221225472 | bytes 6291456 | tf_op jit(solution)/shard_map/pallas_call | solution.py:349
  242.4 9.6 %reshape_reshape.33 = bf16[2,2,2,2,2,96,768]{6,5,4,3,2,1,0:T(8,128)(2,1)} reshape(bf16[32,576,128]{2,1,0:T(8,128)(2,1)} %pad_maximum_fusion) | data formatting | bytes 9437184 | tf_op jit(solution)/shard_map/reshape;reshape | solution.py:138
  252.1 9.4 copy.334
  261.5 11.3 %reshape.756 = bf16[768,3072]{1,0:T(8,128)(2,1)} reshape(bf16[2,2,2,96,2,2,768]{6,5,4,3,2,1,0:T(2,128)(2,1)} %bitcast.380) | data formatting | bytes 9437184 | tf_op jit(solution)/shard_map/reshape | solution.py:143
  278.0 10.2 %reshape_reshape.34 = bf16[2,2,2,2,2,384,192]{6,5,4,3,2,1,0:T(8,128)(2,1)} reshape(bf16[32,576,128]{2,1,0:T(8,128)(2,1)} %pad_maximum_fusion.1) | data formatting | bytes 9437184 | tf_op jit(solution)/shard_map/reshape;reshape | solution.py:138
  288.2 12.0 %copy.270 = bf16[2,2,2,384,2,2,192]{3,2,1,0,6,5,4:T(2,128)(2,1)} copy(bf16[2,2,2,384,2,2,192]{6,3,0,2,4,1,5:T(8,128)(2,1)} %bitcast.379) | data formatting | bytes 9437184 | tf_op jit(solution)/shard_map/transpose | solution.py:142
  300.3 11.3 %reshape.759 = bf16[3072,768]{0,1:T(8,128)(2,1)} reshape(bf16[2,2,2,384,2,2,192]{3,2,1,0,6,5,4:T(2,128)(2,1)} %copy.270) | data formatting | bytes 9437184 | tf_op jit(solution)/shard_map/reshape | solution.py:143
  311.6 37.6 %multiply_convert_fusion = (bf16[1024,3072]{1,0:T(8,128)(2,1)S(1)}, f32[1024,3072]{1,0:T(8,128)}, f32[1024,3072]{1,0:T(8,128)}) fusion(f32[3072]{0:T(1024)S(1)} %reshape.813, bf16[768,3072]{1,0:T(8,128)(2,1)} %reshape.756, f32[1024,768]{0,1:T(8,128)S(1)} %get-tuple-element.230, f32[768]{0:T(1024)S(1)} %reshape.812, f32[768]{0:T(1024)S(1)} %reshape.811, ...), kind=kOutput, calls=%fused_computation.4 | convolution fusion | flops 5043388416 | bytes 39348224 | tf_op jit(solution)/shard_map/dot_general | solution.py:463
  361.4 19.5 %convert_reduce_fusion = (f32[3072]{0:T(1024)S(1)}, bf16[1024,3072]{1,0:T(8,128)(2,1)}) fusion(f32[1024,3072]{1,0:T(8,128)} %get-tuple-element.145, bf16[1024,768]{0,1:T(8,128)(2,1)} %get-tuple-element.137, bf16[3072,768]{0,1:T(8,128)(2,1)} %reshape.759, f32[1024,3072]{1,0:T(8,128)} %get-tuple-element.231, f32[3072]{0:T(1024)S(1)} %reshape.813), kind=kOutput, calls=%fused_computation.2 | convolution fusion | flops 4885312512 | bytes 37773312 | tf_op jit(solution)/shard_map/dot_general | solution.py:33
  381.0 9.2 multiply_reduce_fusion.1
  390.2 7.6 fusion.29
  404.5 87.6 %shard_map.324 = (bf16[1,1024,768]{2,1,0:T(8,128)(2,1)}, bf16[1,1024,768]{2,1,0:T(8,128)(2,1)}, bf16[1,1024,768]{2,1,0:T(8,128)(2,1)}) custom-call(s32[1,1024,3]{2,1,0:T(8,128)} %pad_add_fusion.bounds_ref, s32[6,1024,2]{2,1,0:T(8,128)} %bitcast.431, bf16[1,1024,768]{2,1,0:T(8,128)(2,1)} %fusion.19.q_ref, bf16[1,1024,768]{2,1,0:T(8,128)(2,1)} %fusion.18.k_ref, ...), custom_call_target="tpu_custom_call" | custom-call | flops 8053063680 | bytes 12582912 | tf_op jit(solution)/shard_map/pallas_call | solution.py:372
  506.4 7.5 fusion.42
  514.2 13.2 %reshape.800 = f32[2,2,2,96,2,2,768]{6,5,4,3,2,1,0:T(2,128)} reshape(f32[768,3072]{1,0:T(8,128)} %fusion.29) | data formatting | bytes 18874368 | tf_op jit(solution)/shard_map/reshape | solution.py:150
  527.4 9.1 copy.333
  536.4 10.9 %reshape_reshape_reshape.14 = f32[2,16,576,128]{3,2,1,0:T(8,128)} reshape(f32[2,2,2,2,2,96,768]{6,5,4,3,2,1,0:T(8,128)} %bitcast.375) | data formatting | bytes 18874368 | tf_op jit(solution)/shard_map/reshape;reshape;reshape | solution.py:112
  566.4 6.3 reshape.780
  572.8 6.7 copy.287
  592.9 6.7 copy.280
  610.4 6.7 reshape.784
  617.1 6.7 copy.288
  635.5 8.3 copy.274
  644.3 12.4 %reduce.11 = bf16[1024,768]{1,0:T(8,128)(2,1)} reduce(bf16[1024,1,768]{2,1,0:T(2,128)(2,1)} %bitcast.388, bf16[]{:T(256)} %broadcast.255), dimensions={1}, to_apply=%bitcast.335.reduce_sub_computation | reduce | bytes 3145730
  675.9 8.5 copy.279
  684.4 13.1 %reshape.804 = f32[2,2,2,384,2,2,192]{3,2,1,0,6,5,4:T(2,128)} reshape(f32[3072,768]{0,1:T(8,128)} %fusion.42) | data formatting | bytes 18874368 | tf_op jit(solution)/shard_map/reshape | solution.py:150
  697.5 14.6 %copy.300 = f32[2,2,2,2,2,384,192]{6,5,4,3,2,1,0:T(8,128)} copy(f32[2,2,2,2,2,384,192]{5,3,1,4,6,0,2:T(2,128)} %bitcast.376) | data formatting | bytes 18874368 | tf_op jit(solution)/shard_map/transpose | solution.py:152
  712.1 13.5 %reshape_reshape_reshape.15 = f32[2,16,576,128]{3,2,1,0:T(8,128)} reshape(f32[2,2,2,2,2,384,192]{6,5,4,3,2,1,0:T(8,128)} %copy.300) | data formatting | bytes 18874368 | tf_op jit(solution)/shard_map/reshape;reshape;reshape | solution.py:112
  762.3 23.5 %collective-permute-done.31 = f32[8,146,128]{2,0,1:T(8,128)S(1)} collective-permute-done((f32[8,146,128]{2,0,1:T(8,128)S(1)}, f32[8,146,128]{2,0,1:T(8,128)S(1)}, u32[]{:S(2)}, u32[]{:S(2)}) %collective-permute-start.31) | collective-permute-done | bytes 598048 | tf_op jit(solution)/shard_map/ppermute | solution.py:116
  786.0 13.1 %collective-permute-done.46 = f32[8,152,128]{2,1,0:T(8,128)S(1)} collective-permute-done((f32[8,152,128]{2,1,0:T(8,128)S(1)}, f32[8,152,128]{2,1,0:T(8,128)S(1)}, u32[]{:S(2)}, u32[]{:S(2)}) %collective-permute-start.46) | collective-permute-done | bytes 622624 | tf_op jit(solution)/shard_map/ppermute | solution.py:116
  828.7 48.5 %collective-permute-done.33 = f32[2,146,128]{2,1,0:T(8,128)S(1)} collective-permute-done((f32[2,146,128]{2,1,0:T(8,128)S(1)}, f32[2,146,128]{2,1,0:T(8,128)S(1)}, u32[]{:S(2)}, u32[]{:S(2)}) %collective-permute-start.33) | collective-permute-done | bytes 149536 | tf_op jit(solution)/shard_map/ppermute | solution.py:116
  903.4 7.6 collective-permute-done.52
  936.3 8.6 collective-permute-done.54
  (601 shorter events, 406.3 us)
Async XLA Ops:
  0.8 102.1 %all-to-all-start.2 = ((bf16[4,256,768]{2,1,0:T(8,128)(2,1)}), bf16[4,256,768]{2,1,0:T(8,128)(2,1)S(1)}, u32[]{:S(2)}, u32[]{:S(2)}) async-start(bf16[4,256,768]{2,1,0:T(8,128)(2,1)} %param.21), calls=%async_computation.2 | async-start | bytes 3145728 | tf_op jit(solution)/shard_map/all_to_all | solution.py:432
  5.3 22.0 %collective-permute-start.10 = (bf16[1,144,128]{2,1,0:T(8,128)(2,1)S(1)}, bf16[1,144,128]{2,1,0:T(8,128)(2,1)S(1)}, u32[]{:S(2)}, u32[]{:S(2)}) collective-permute-start(bf16[1,144,128]{2,1,0:T(8,128)(2,1)S(1)} %broadcast_in_dim_reshape_reshape.13), channel_id=1, source_target_pairs={{0,4},{1,5},{2,6},{3,7},{4,0},{5,1},{6,2},{7,3},{8,12},{9,13},{10,... | collective-permute-start | bytes 110600 | tf_op jit(solution)/shard_map/ppermute | solution.py:101
  9.3 23.6 %collective-permute-start.15 = (bf16[1,152,128]{2,1,0:T(8,128)(2,1)S(1)}, bf16[1,152,128]{2,1,0:T(8,128)(2,1)S(1)}, u32[]{:S(2)}, u32[]{:S(2)}) collective-permute-start(bf16[1,152,128]{2,1,0:T(8,128)(2,1)S(1)} %bitcast.456), channel_id=1, source_target_pairs={{0,4},{1,5},{2,6},{3,7},{4,0},{5,1},{6,2},{7,3},{8,12},{9,13},{10,... | collective-permute-start | bytes 116744 | tf_op jit(solution)/shard_map/ppermute | solution.py:101
  12.8 28.5 %collective-permute-start.20 = (bf16[1,576,128]{2,1,0:T(8,128)(2,1)S(1)}, bf16[1,576,128]{2,1,0:T(8,128)(2,1)}, u32[]{:S(2)}, u32[]{:S(2)}) collective-permute-start(bf16[1,576,128]{2,1,0:T(8,128)(2,1)S(1)} %broadcast_in_dim_reshape_reshape.14), channel_id=1, source_target_pairs={{0,4},{1,5},{2,6},{3,7},{4,0},{5,1},{6,2},{7,3},{8,12},{9,13},{10,... | collective-permute-start | bytes 442376 | tf_op jit(solution)/shard_map/ppermute | solution.py:101
  61.7 28.6 %collective-permute-start.14 = (bf16[16,144,128]{2,1,0:T(8,128)(2,1)}, bf16[16,144,128]{2,1,0:T(8,128)(2,1)}, u32[]{:S(2)}, u32[]{:S(2)}) collective-permute-start(bf16[16,144,128]{2,1,0:T(8,128)(2,1)} %pad_maximum_fusion.13), channel_id=1, source_target_pairs={{0,8},{8,0},{16,24},{24,16},{1,9},{9,1},{17,25},{25,17},{2,10},{10... | collective-permute-start | bytes 1769480 | tf_op jit(solution)/shard_map/ppermute | solution.py:101
  67.1 39.6 %collective-permute-start.4 = (bf16[16,146,128]{2,0,1:T(8,128)(2,1)}, bf16[16,146,128]{2,0,1:T(8,128)(2,1)}, u32[]{:S(2)}, u32[]{:S(2)}) collective-permute-start(bf16[16,146,128]{2,0,1:T(8,128)(2,1)} %copy.252), channel_id=1, source_target_pairs={{0,8},{8,0},{16,24},{24,16},{1,9},{9,1},{17,25},{25,17},{2,10},{10... | collective-permute-start | bytes 1794056 | tf_op jit(solution)/shard_map/ppermute | solution.py:101
  68.1 144.8 %collective-permute-start.19 = (bf16[16,152,128]{2,1,0:T(8,128)(2,1)}, bf16[16,152,128]{2,1,0:T(8,128)(2,1)}, u32[]{:S(2)}, u32[]{:S(2)}) collective-permute-start(bf16[16,152,128]{2,1,0:T(8,128)(2,1)} %pad_maximum_fusion.11), channel_id=1, source_target_pairs={{0,8},{8,0},{16,24},{24,16},{1,9},{9,1},{17,25},{25,17},{2,10},{10... | collective-permute-start | bytes 1867784 | tf_op jit(solution)/shard_map/ppermute | solution.py:101
  75.7 139.0 %collective-permute-start.23 = (bf16[8,576,128]{2,1,0:T(8,128)(2,1)}, bf16[8,576,128]{2,1,0:T(8,128)(2,1)}, u32[]{:S(2)}, u32[]{:S(2)}) collective-permute-start(bf16[8,576,128]{2,1,0:T(8,128)(2,1)} %pad_maximum_fusion.8), channel_id=1, source_target_pairs={{0,1},{1,0},{2,3},{3,2},{4,5},{5,4},{6,7},{7,6},{8,9},{9,8},{10,11... | collective-permute-start | bytes 3538952 | tf_op jit(solution)/shard_map/ppermute | solution.py:101
  78.3 140.1 %collective-permute-start.28 = (bf16[8,576,128]{2,1,0:T(8,128)(2,1)}, bf16[8,576,128]{2,1,0:T(8,128)(2,1)}, u32[]{:S(2)}, u32[]{:S(2)}) collective-permute-start(bf16[8,576,128]{2,1,0:T(8,128)(2,1)} %pad_maximum_fusion.9), channel_id=1, source_target_pairs={{0,2},{1,3},{2,0},{3,1},{4,6},{5,7},{6,4},{7,5},{8,10},{9,11},{10,... | collective-permute-start | bytes 3538952 | tf_op jit(solution)/shard_map/ppermute | solution.py:101
  102.9 23.7 %all-to-all-start = ((bf16[4,256,768]{2,1,0:T(8,128)(2,1)}), bf16[4,256,768]{2,1,0:T(8,128)(2,1)S(1)}, u32[]{:S(2)}, u32[]{:S(2)}) async-start(bf16[4,256,768]{2,1,0:T(8,128)(2,1)} %param.20), calls=%async_computation | async-start | bytes 3145728 | tf_op jit(solution)/shard_map/all_to_all | solution.py:432
  223.0 49.7 %collective-permute-start.29 = (bf16[16,576,128]{2,1,0:T(8,128)(2,1)}, bf16[16,576,128]{2,1,0:T(8,128)(2,1)}, u32[]{:S(2)}, u32[]{:S(2)}) collective-permute-start(bf16[16,576,128]{2,1,0:T(8,128)(2,1)} %pad_maximum_fusion.3), channel_id=1, source_target_pairs={{0,8},{8,0},{16,24},{24,16},{1,9},{9,1},{17,25},{25,17},{2,10},{10... | collective-permute-start | bytes 7077896 | tf_op jit(solution)/shard_map/ppermute | solution.py:101
  566.0 182.4 %collective-permute-start.45 = (f32[16,152,128]{2,1,0:T(8,128)}, f32[16,152,128]{2,1,0:T(8,128)}, u32[]{:S(2)}, u32[]{:S(2)}) collective-permute-start(f32[16,152,128]{2,1,0:T(8,128)} %dynamic-slice_bitcast_fusion.4), channel_id=1, source_target_pairs={{0,8},{8,0},{16,24},{24,16},{1,9},{9,1},{17,25},{25,17},{2,10},{10... | collective-permute-start | bytes 3735560 | tf_op jit(solution)/shard_map/ppermute | solution.py:116
  586.5 153.5 %collective-permute-start.35 = (f32[16,144,128]{2,1,0:T(8,128)}, f32[16,144,128]{2,1,0:T(8,128)}, u32[]{:S(2)}, u32[]{:S(2)}) collective-permute-start(f32[16,144,128]{2,1,0:T(8,128)} %dynamic-slice_bitcast_fusion.8), channel_id=1, source_target_pairs={{0,8},{8,0},{16,24},{24,16},{1,9},{9,1},{17,25},{25,17},{2,10},{10... | collective-permute-start | bytes 3538952 | tf_op jit(solution)/shard_map/ppermute | solution.py:116
  630.8 111.4 %collective-permute-start.40 = (f32[16,144,128]{2,1,0:T(8,128)}, f32[16,144,128]{2,1,0:T(8,128)}, u32[]{:S(2)}, u32[]{:S(2)}) collective-permute-start(f32[16,144,128]{2,1,0:T(8,128)} %dynamic-slice_bitcast_fusion.7), channel_id=1, source_target_pairs={{0,8},{8,0},{16,24},{24,16},{1,9},{9,1},{17,25},{25,17},{2,10},{10... | collective-permute-start | bytes 3538952 | tf_op jit(solution)/shard_map/ppermute | solution.py:116
  635.4 109.8 %collective-permute-start.30 = (f32[16,146,128]{2,0,1:T(8,128)}, f32[16,146,128]{2,0,1:T(8,128)}, u32[]{:S(2)}, u32[]{:S(2)}) collective-permute-start(f32[16,146,128]{2,0,1:T(8,128)} %bitcast.371), channel_id=1, source_target_pairs={{0,8},{8,0},{16,24},{24,16},{1,9},{9,1},{17,25},{25,17},{2,10},{10... | collective-permute-start | bytes 3588104 | tf_op jit(solution)/shard_map/ppermute | solution.py:116
  660.4 70.2 %all-to-all-start.1 = ((bf16[4,2,98304]{2,1,0:T(2,128)(2,1)}), bf16[4,2,98304]{2,1,0:T(2,128)(2,1)}, u32[]{:S(2)}, u32[]{:S(2)}) async-start(bf16[4,2,98304]{2,1,0:T(2,128)(2,1)} %reshape.824), calls=%async_computation.1 | async-start | bytes 3145728 | tf_op jit(solution)/shard_map/all_to_all | solution.py:435
  670.0 141.4 %collective-permute-start.50 = (f32[16,576,128]{2,1,0:T(8,128)}, f32[16,576,128]{2,1,0:T(8,128)}, u32[]{:S(2)}, u32[]{:S(2)}) collective-permute-start(f32[16,576,128]{2,1,0:T(8,128)} %dynamic-slice_bitcast_fusion.1), channel_id=1, source_target_pairs={{0,8},{8,0},{16,24},{24,16},{1,9},{9,1},{17,25},{25,17},{2,10},{10... | collective-permute-start | bytes 14155784 | tf_op jit(solution)/shard_map/ppermute | solution.py:116
  730.6 169.0 %all-to-all-start.3 = ((f32[1,1024,768]{2,0,1:T(1,128)}), f32[1,1024,768]{2,0,1:T(1,128)}, u32[]{:S(2)}, u32[]{:S(2)}) async-start(f32[1,1024,768]{2,0,1:T(1,128)} %copy.279), calls=%async_computation.3 | async-start | bytes 6291456 | tf_op jit(solution)/shard_map/all_to_all | solution.py:435
  739.9 77.5 %collective-permute-start.55 = (f32[16,576,128]{2,1,0:T(8,128)}, f32[16,576,128]{2,1,0:T(8,128)S(1)}, u32[]{:S(2)}, u32[]{:S(2)}) collective-permute-start(f32[16,576,128]{2,1,0:T(8,128)} %dynamic-slice_bitcast_fusion), channel_id=1, source_target_pairs={{0,8},{8,0},{16,24},{24,16},{1,9},{9,1},{17,25},{25,17},{2,10},{10... | collective-permute-start | bytes 14155784 | tf_op jit(solution)/shard_map/ppermute | solution.py:116
  748.5 37.3 %collective-permute-start.31 = (f32[8,146,128]{2,0,1:T(8,128)S(1)}, f32[8,146,128]{2,0,1:T(8,128)S(1)}, u32[]{:S(2)}, u32[]{:S(2)}) collective-permute-start(f32[8,146,128]{2,0,1:T(8,128)S(1)} %dynamic-slice_bitcast_fusion.10), channel_id=1, source_target_pairs={{0,16},{8,24},{16,0},{24,8},{1,17},{9,25},{17,1},{25,9},{2,18},{10... | collective-permute-start | bytes 1794056 | tf_op jit(solution)/shard_map/ppermute | solution.py:116
  758.1 41.0 %collective-permute-start.46 = (f32[8,152,128]{2,1,0:T(8,128)S(1)}, f32[8,152,128]{2,1,0:T(8,128)S(1)}, u32[]{:S(2)}, u32[]{:S(2)}) collective-permute-start(f32[8,152,128]{2,1,0:T(8,128)S(1)} %dynamic-slice_bitcast_fusion.9), channel_id=1, source_target_pairs={{0,16},{8,24},{16,0},{24,8},{1,17},{9,25},{17,1},{25,9},{2,18},{10... | collective-permute-start | bytes 1867784 | tf_op jit(solution)/shard_map/ppermute | solution.py:116
  760.7 40.5 %collective-permute-start.37 = (f32[4,144,128]{2,1,0:T(8,128)S(1)}, f32[4,144,128]{2,1,0:T(8,128)S(1)}, u32[]{:S(2)}, u32[]{:S(2)}) collective-permute-start(f32[4,144,128]{2,1,0:T(8,128)S(1)} %dynamic-slice_bitcast_fusion.17), channel_id=1, source_target_pairs={{0,2},{1,3},{2,0},{3,1},{4,6},{5,7},{6,4},{7,5},{8,10},{9,11},{10,... | collective-permute-start | bytes 884744 | tf_op jit(solution)/shard_map/ppermute | solution.py:116
  785.7 19.1 %collective-permute-start.42 = (f32[4,144,128]{2,1,0:T(8,128)S(1)}, f32[4,144,128]{2,1,0:T(8,128)S(1)}, u32[]{:S(2)}, u32[]{:S(2)}) collective-permute-start(f32[4,144,128]{2,1,0:T(8,128)S(1)} %dynamic-slice_bitcast_fusion.16), channel_id=1, source_target_pairs={{0,16},{8,24},{16,0},{24,8},{1,17},{9,25},{17,1},{25,9},{2,18},{10... | collective-permute-start | bytes 884744 | tf_op jit(solution)/shard_map/ppermute | solution.py:116
  801.2 20.5 %collective-permute-start.47 = (f32[4,152,128]{2,1,0:T(8,128)}, f32[4,152,128]{2,1,0:T(8,128)}, u32[]{:S(2)}, u32[]{:S(2)}) collective-permute-start(f32[4,152,128]{2,1,0:T(8,128)} %dynamic-slice_bitcast_fusion.15), channel_id=1, source_target_pairs={{0,1},{1,0},{2,3},{3,2},{4,5},{5,4},{6,7},{7,6},{8,9},{9,8},{10,11... | collective-permute-start | bytes 933896 | tf_op jit(solution)/shard_map/ppermute | solution.py:116
  816.7 67.4 %collective-permute-start.51 = (f32[8,576,128]{2,1,0:T(8,128)}, f32[8,576,128]{2,1,0:T(8,128)}, u32[]{:S(2)}, u32[]{:S(2)}) collective-permute-start(f32[8,576,128]{2,1,0:T(8,128)} %dynamic-slice_bitcast_fusion.3), channel_id=1, source_target_pairs={{0,1},{1,0},{2,3},{3,2},{4,5},{5,4},{6,7},{7,6},{8,9},{9,8},{10,11... | collective-permute-start | bytes 7077896 | tf_op jit(solution)/shard_map/ppermute | solution.py:116
  819.7 68.3 %collective-permute-start.56 = (f32[8,576,128]{2,1,0:T(8,128)}, f32[8,576,128]{2,1,0:T(8,128)}, u32[]{:S(2)}, u32[]{:S(2)}) collective-permute-start(f32[8,576,128]{2,1,0:T(8,128)} %dynamic-slice_bitcast_fusion.2), channel_id=1, source_target_pairs={{0,2},{1,3},{2,0},{3,1},{4,6},{5,7},{6,4},{7,5},{8,10},{9,11},{10,... | collective-permute-start | bytes 7077896 | tf_op jit(solution)/shard_map/ppermute | solution.py:116
  821.7 55.6 %collective-permute-start.33 = (f32[2,146,128]{2,1,0:T(8,128)S(1)}, f32[2,146,128]{2,1,0:T(8,128)S(1)}, u32[]{:S(2)}, u32[]{:S(2)}) collective-permute-start(f32[2,146,128]{2,1,0:T(8,128)S(1)} %dynamic-slice_bitcast_fusion.19), channel_id=1, source_target_pairs={{0,2},{1,3},{2,0},{3,1},{4,6},{5,7},{6,4},{7,5},{8,10},{9,11},{10,... | collective-permute-start | bytes 448520 | tf_op jit(solution)/shard_map/ppermute | solution.py:116
  822.9 72.9 %collective-permute-start.48 = (f32[2,152,128]{2,1,0:T(8,128)S(1)}, f32[2,152,128]{2,1,0:T(8,128)}, u32[]{:S(2)}, u32[]{:S(2)}) collective-permute-start(f32[2,152,128]{2,1,0:T(8,128)S(1)} %dynamic-slice_bitcast_fusion.18), channel_id=1, source_target_pairs={{0,2},{1,3},{2,0},{3,1},{4,6},{5,7},{6,4},{7,5},{8,10},{9,11},{10,... | collective-permute-start | bytes 466952 | tf_op jit(solution)/shard_map/ppermute | solution.py:116
  825.9 53.6 %collective-permute-start.39 = (f32[1,144,128]{2,1,0:T(8,128)S(1)}, f32[1,144,128]{2,1,0:T(8,128)S(1)}, u32[]{:S(2)}, u32[]{:S(2)}) collective-permute-start(f32[1,144,128]{2,1,0:T(8,128)S(1)} %constant_dynamic-slice_fusion.4), channel_id=1, source_target_pairs={{0,4},{1,5},{2,6},{3,7},{4,0},{5,1},{6,2},{7,3},{8,12},{9,13},{10,... | collective-permute-start | bytes 221192 | tf_op jit(solution)/shard_map/ppermute | solution.py:116
  888.0 22.9 %collective-permute-start.52 = (f32[4,576,128]{2,1,0:T(8,128)}, f32[4,576,128]{2,1,0:T(8,128)}, u32[]{:S(2)}, u32[]{:S(2)}) collective-permute-start(f32[4,576,128]{2,1,0:T(8,128)} %dynamic-slice_bitcast_fusion.6), channel_id=1, source_target_pairs={{0,2},{1,3},{2,0},{3,1},{4,6},{5,7},{6,4},{7,5},{8,10},{9,11},{10,... | collective-permute-start | bytes 3538952 | tf_op jit(solution)/shard_map/ppermute | solution.py:116
  892.5 28.1 %collective-permute-start.57 = (f32[4,576,128]{2,1,0:T(8,128)}, f32[4,576,128]{2,1,0:T(8,128)}, u32[]{:S(2)}, u32[]{:S(2)}) collective-permute-start(f32[4,576,128]{2,1,0:T(8,128)} %dynamic-slice_bitcast_fusion.5), channel_id=1, source_target_pairs={{0,16},{8,24},{16,0},{24,8},{1,17},{9,25},{17,1},{25,9},{2,18},{10... | collective-permute-start | bytes 3538952 | tf_op jit(solution)/shard_map/ppermute | solution.py:116
  896.7 26.5 %collective-permute-start.49 = (f32[1,152,128]{2,1,0:T(8,128)S(1)}, f32[1,152,128]{2,1,0:T(8,128)S(1)}, u32[]{:S(2)}, u32[]{:S(2)}) collective-permute-start(f32[1,152,128]{2,1,0:T(8,128)S(1)} %constant_dynamic-slice_fusion.2), channel_id=1, source_target_pairs={{0,4},{1,5},{2,6},{3,7},{4,0},{5,1},{6,2},{7,3},{8,12},{9,13},{10,... | collective-permute-start | bytes 233480 | tf_op jit(solution)/shard_map/ppermute | solution.py:116
  (121 other events, 1258.7 us)
